TPU v7x, 512 devices: a whole 4x8x8 slice. The times are simulated.
512 devices in a mesh: row: 16 (over z, y_lo), col: 32 (over y_hi, x, core).
Axes of the slice: x: 4, y: 8 (y_hi: 4, y_lo: 2; y = y_hi * 2 + y_lo), z: 8, core: 2. Of those that a mesh axis runs over, the one named last changes fastest.
Arguments:
- pressure: float32 [512, 1024, 512], P('row', 'col'), may hold values from -6 to 6
- cut_exponent: int32 [16, 32, 2], P('row', 'col'), may hold values from 0 to 3
- group_map: int32 [16, 32, 2], P('row', 'col'), may hold values from 0 to 15
Outputs:
- coeffs: float32 [512, 1024, 512], P('row', 'col')
- group_mass: float32 [16, 4], replicated
Inputs may be any that keep to these rules, and one draw needn't show every extreme that they name: `cut_exponent`: one exponent per block of 32 x 32 x 512 // 2 cells.
All inputs are finite; a program needn't handle non-finite values.
Results may differ from a plain program's by a relative error of at most 0.0001.
Values sent between devices are 32-bit elements; how exact they have to be, the bound alone decides.
No kernel may reach another device: no remote copies, remote signals or barrier semaphores. Data moves between devices by JAX's collectives and lax.ppermute only.
A program may use at most 64 MiB of HBM per device.

v0:
```python
import jax
import jax.numpy as jnp
from jax import lax
from jax.sharding import Mesh
from jax.sharding import PartitionSpec as P

GROUPS = 16
ROW = ("row_0", "row_1")
COL = ("col_0", "col_1", "col_2")
ROW_COL = ("row_0", "row_1", "col_0", "col_1", "col_2")


cut_levels = (0.25, 0.5, 1.0, 2.0)


def extended_2(value, sides, width):
    for axis, dim in sides:
        devices, length = (lax.axis_size(axis), value.shape[dim])
        up = [(i, (i + 1) % devices) for i in range(devices)]
        down = [(j, i) for i, j in up]
        last = lax.slice_in_dim(value, length - width, length, axis=dim)
        initial = lax.slice_in_dim(value, 0, width, axis=dim)
        before = lax.ppermute(last, axis, up)
        after = lax.ppermute(initial, axis, down)
        value = jnp.concatenate([before, value, after], axis=dim)
    return value


def by_axis(value, axes):
    for axis in axes:
        value = lax.psum(value, axis)
    return value


def slice_dim(values, axis_pos, offset, length):
    return lax.slice_in_dim(values, offset, offset + length, axis=axis_pos)


def parity_part(signal, axis_pos, which):
    length = signal.shape[axis_pos]
    return lax.slice_in_dim(signal, which, length, stride=2, axis=axis_pos)


def alternate(smooth, detail, axis_pos):
    merged = jnp.stack([smooth, detail], axis_pos + 1)
    shape = list(smooth.shape)
    shape[axis_pos] = 2 * shape[axis_pos]
    return merged.reshape(tuple(shape))


def predict_odd(padded, axis_pos, offset, length):
    near = slice_dim(padded, axis_pos, offset + 1, length) + slice_dim(
        padded, axis_pos, offset + 2, length
    )
    far_sum = slice_dim(padded, axis_pos, offset, length) + slice_dim(
        padded, axis_pos, offset + 3, length
    )
    return 0.5625 * near - 0.0625 * far_sum


def update_even(padded, axis_pos, offset, length):
    near = slice_dim(padded, axis_pos, offset + 1, length) + slice_dim(
        padded, axis_pos, offset + 2, length
    )
    far_sum = slice_dim(padded, axis_pos, offset, length) + slice_dim(
        padded, axis_pos, offset + 3, length
    )
    return 0.28125 * near - 0.03125 * far_sum


def lift_parts(extended, axis_pos):
    half = (extended.shape[axis_pos] - 12) // 2
    evens_ext = parity_part(extended, axis_pos, 0)
    odds_ext = parity_part(extended, axis_pos, 1)
    detail_ext = slice_dim(odds_ext, axis_pos, 1, half + 3) - predict_odd(
        evens_ext, axis_pos, 0, half + 3
    )
    smooth = slice_dim(evens_ext, axis_pos, 3, half) + update_even(detail_ext, axis_pos, 0, half)
    detail = slice_dim(detail_ext, axis_pos, 2, half)
    return alternate(smooth, detail, axis_pos)


def cyclic_pad(values, axis_pos):
    length = values.shape[axis_pos]
    return jnp.concatenate(
        [slice_dim(values, axis_pos, length - 2, 2), values, slice_dim(values, axis_pos, 0, 2)],
        axis=axis_pos,
    )


def depth_table(size_z):
    ident = (
        jnp.arange(size_z, dtype=jnp.int32)[:, None] == jnp.arange(size_z, dtype=jnp.int32)[None, :]
    ).astype(jnp.float32)
    half = size_z // 2
    evens_half = lax.slice_in_dim(ident, 0, size_z, stride=2, axis=1)
    odds_half = lax.slice_in_dim(ident, 1, size_z, stride=2, axis=1)
    detail = odds_half - predict_odd(cyclic_pad(evens_half, 1), 1, 1, half)
    smooth = evens_half + update_even(cyclic_pad(detail, 1), 1, 0, half)
    return jnp.stack([smooth, detail], 2).reshape(size_z, size_z)


def shards(pressure, cut_exponent, group_map):
    signal = pressure
    extended = extended_2(signal, ((ROW, 0),), 6)
    signal = lift_parts(extended, 0)
    extended_cols = extended_2(signal, ((COL, 1),), 6)
    signal = lift_parts(extended_cols, 1)
    size_x, size_y, size_z = signal.shape
    table = depth_table(size_z)
    coeffs = jnp.dot(
        signal.reshape(size_x * size_y, size_z),
        table,
        precision=lax.Precision.HIGHEST,
        preferred_element_type=jnp.float32,
    ).reshape(size_x, size_y, size_z)
    blocks_z = cut_exponent.shape[2]
    parity_x = (jnp.arange(size_x, dtype=jnp.int32) % 2)[:, None, None]
    parity_y = (jnp.arange(size_y, dtype=jnp.int32) % 2)[None, :, None]
    parity_z = (jnp.arange(size_z, dtype=jnp.int32) % 2)[None, None, :]
    detail_mask = parity_x + parity_y + parity_z > 0
    magnitude = jnp.where(detail_mask, jnp.abs(coeffs), jnp.float32(0.0))
    shaped = magnitude.reshape(size_x, size_y, blocks_z, size_z // blocks_z)
    scales = jnp.exp2(-cut_exponent[0, 0].astype(jnp.float32))
    cells = size_x * size_y * (size_z // blocks_z)
    block_list = []
    for level_value in cut_levels:
        limit = (level_value * scales)[None, None, :, None]
        block_list.append(jnp.sum(jnp.maximum(shaped - limit, 0.0), axis=(0, 1, 3)) / cells)
    block_mass = jnp.stack(block_list, -1)
    onehot = (group_map[0, 0][:, None] == jnp.arange(GROUPS, dtype=jnp.int32)[None, :]).astype(
        jnp.float32
    )
    partial_mass = jnp.einsum("zg,zk->gk", onehot, block_mass, precision=lax.Precision.HIGHEST)
    group_mass = by_axis(partial_mass, ROW_COL)
    return (coeffs, group_mass)


def solution(mesh):
    split = Mesh(mesh.devices.reshape(8, 2, 4, 4, 2), ("row_0", "row_1", "col_0", "col_1", "col_2"))
    in_specs = (P(ROW, COL, None), P(ROW, COL, None), P(ROW, COL, None))
    out_specs = (P(ROW, COL, None), P())
    return jax.shard_map(
        shards, mesh=split, in_specs=in_specs, out_specs=out_specs, check_vma=False
    )
```

profile of v0, /device:TPU:1, one launch (start us, length us, event | category | flops | bytes accessed | tf_op | source)
XLA Modules:
  0.0 157.2 jit_solution(16425999100789924649)
XLA Ops:
  0.6 1.9 %fusion.53 = (f32[6,32,512]{2,1,0:T(8,128)S(1)}, f32[6,32,512]{2,1,0:T(8,128)}) fusion(f32[32,32,512]{2,1,0:T(8,128)} %param.3), kind=kLoop, calls=%fused_computation.101 | loop fusion | bytes 1572864 | tf_op jit(solution)/shard_map/slice | solution.py:22
  2.6 4.0 %collective-permute-start = (f32[6,32,512]{2,1,0:T(8,128)}, f32[6,32,512]{2,1,0:T(8,128)S(1)}, u32[]{:S(2)}, u32[]{:S(2)}) collective-permute-start(f32[6,32,512]{2,1,0:T(8,128)} %get-tuple-element.13), channel_id=1, source_target_pairs={{0,32},{32,64},{64,96},{96,128},{128,160},{160,192},{192,224},{224... | collective-permute-start | bytes 1179656 | tf_op jit(solution)/shard_map/ppermute | solution.py:23
  6.6 10.4 %collective-permute-start.1 = (f32[6,32,512]{2,1,0:T(8,128)S(1)}, f32[6,32,512]{2,1,0:T(8,128)S(1)}, u32[]{:S(2)}, u32[]{:S(2)}) collective-permute-start(f32[6,32,512]{2,1,0:T(8,128)S(1)} %get-tuple-element.12), channel_id=1, source_target_pairs={{32,0},{64,32},{96,64},{128,96},{160,128},{192,160},{224,192},{256... | collective-permute-start | bytes 1179656 | tf_op jit(solution)/shard_map/ppermute | solution.py:24
  17.0 0.1 fusion.20
  17.1 19.5 %slice.166 = f32[512,256]{1,0:T(8,128)S(1)} slice(f32[512,512]{1,0:T(8,128)S(1)} %fusion.20), slice={[0:512:1], [0:512:2]} | slice | bytes 1048576 | tf_op jit(solution)/shard_map/slice | solution.py:96
  36.6 19.5 %slice.167 = f32[512,256]{1,0:T(8,128)S(1)} slice(f32[512,512]{1,0:T(8,128)S(1)} %fusion.20), slice={[0:512:1], [1:512:2]} | slice | bytes 1048576 | tf_op jit(solution)/shard_map/slice | solution.py:97
  56.0 0.0 copy-start.1
  56.0 0.1 fusion.55
  56.2 0.7 fusion.31
  56.9 0.1 fusion.54
  57.0 0.0 copy-done.1
  57.0 0.1 broadcast_bitcast_fusion
  57.1 0.1 broadcast_bitcast_fusion.2
  57.2 0.6 fusion.26
  57.8 0.1 pad_maximum_fusion.3
  57.9 0.6 copy.13
  58.5 1.7 %reshape.144 = f32[512,512]{0,1:T(8,128)} reshape(f32[512,256,2]{0,2,1:T(2,128)S(1)} %copy.13) | data formatting | bytes 2097152 | tf_op jit(solution)/shard_map/reshape | solution.py:100
  60.2 0.0 collective-permute-done
  60.2 1.8 %constant_dynamic-update-slice_fusion.1 = f32[44,32,512]{2,1,0:T(8,128)S(1)} fusion(f32[44,32,512]{2,1,0:T(8,128)S(1)} %constant_dynamic-update-slice_fusion.2, f32[32,32,512]{2,1,0:T(8,128)} %param.3), kind=kLoop, calls=%fused_computation.66 | loop fusion | bytes 4194304
  62.0 0.0 collective-permute-done.1
  62.0 0.3 fusion.51
  62.3 0.3 fusion.6
  62.7 0.3 fusion.16
  63.0 0.2 pad_maximum_fusion.1
  63.2 0.1 fusion.52
  63.4 4.0 %collective-permute-start.2 = (f32[32,6,512]{2,1,0:T(8,128)S(1)}, f32[32,6,512]{2,1,0:T(8,128)S(1)}, u32[]{:S(2)}, u32[]{:S(2)}) collective-permute-start(f32[32,6,512]{2,1,0:T(8,128)S(1)} %get-tuple-element.10), channel_id=1, source_target_pairs={{0,1},{1,2},{2,3},{3,4},{4,5},{5,6},{6,7},{7,8},{8,9},{9,10},{10,1... | collective-permute-start | bytes 1179656 | tf_op jit(solution)/shard_map/ppermute | solution.py:23
  67.3 2.1 %collective-permute-start.3 = (f32[32,6,512]{2,1,0:T(8,128)S(1)}, f32[32,6,512]{2,1,0:T(8,128)S(1)}, u32[]{:S(2)}, u32[]{:S(2)}) collective-permute-start(f32[32,6,512]{2,1,0:T(8,128)S(1)} %get-tuple-element.11), channel_id=1, source_target_pairs={{1,0},{2,1},{3,2},{4,3},{5,4},{6,5},{7,6},{8,7},{9,8},{10,9},{11,1... | collective-permute-start | bytes 1179656 | tf_op jit(solution)/shard_map/ppermute | solution.py:24
  69.4 0.1 broadcast_add_fusion
  69.5 3.9 %collective-permute-done.2 = f32[32,6,512]{2,1,0:T(8,128)S(1)} collective-permute-done((f32[32,6,512]{2,1,0:T(8,128)S(1)}, f32[32,6,512]{2,1,0:T(8,128)S(1)}, u32[]{:S(2)}, u32[]{:S(2)}) %collective-permute-start.2) | collective-permute-done | bytes 393248 | tf_op jit(solution)/shard_map/ppermute | solution.py:23
  73.4 4.7 %collective-permute-done.3 = f32[32,6,512]{2,1,0:T(8,128)S(1)} collective-permute-done((f32[32,6,512]{2,1,0:T(8,128)S(1)}, f32[32,6,512]{2,1,0:T(8,128)S(1)}, u32[]{:S(2)}, u32[]{:S(2)}) %collective-permute-start.3) | collective-permute-done | bytes 393248 | tf_op jit(solution)/shard_map/ppermute | solution.py:24
  78.1 2.1 %pad_maximum_fusion = f32[32,44,512]{2,1,0:T(8,128)} fusion(f32[32,6,512]{2,1,0:T(8,128)S(1)} %collective-permute-done.3, f32[32,32,512]{2,1,0:T(8,128)S(1)} %bitcast.47, f32[32,6,512]{2,1,0:T(8,128)S(1)} %collective-permute-done.2), kind=kLoop, calls=%fused_computation | loop fusion | flops 1441792 | bytes 5767168 | tf_op jit(solution)/shard_map/concatenate | solution.py:25
  80.3 6.2 %slice.154 = f32[32,22,512]{2,1,0:T(8,128)S(1)} slice(f32[32,44,512]{2,1,0:T(8,128)} %pad_maximum_fusion), slice={[0:32:1], [0:44:2], [0:512:1]} | slice | bytes 2883584 | tf_op jit(solution)/shard_map/slice | solution.py:41
  86.4 6.2 %slice.156 = f32[32,22,512]{2,1,0:T(8,128)S(1)} slice(f32[32,44,512]{2,1,0:T(8,128)} %pad_maximum_fusion), slice={[0:32:1], [1:44:2], [0:512:1]} | slice | bytes 2883584 | tf_op jit(solution)/shard_map/slice | solution.py:41
  92.6 0.8 fusion.2
  93.5 0.6 fusion.11
  94.1 0.3 pad_maximum_fusion.2
  94.4 1.7 %copy.12 = f32[32,16,2,512]{3,2,1,0:T(2,128)S(1)} copy(f32[32,16,2,512]{3,1,0,2:T(8,128)S(1)} %pad_maximum_fusion.2) | data formatting | bytes 4194304 | tf_op jit(solution)/shard_map/stack | solution.py:45
  96.0 0.0 copy-start
  96.1 2.5 %dot_general.8 = f32[32,32,512]{2,1,0:T(8,128)} reshape(f32[32,16,2,512]{3,2,1,0:T(2,128)S(1)} %copy.12) | data formatting | bytes 4194304 | tf_op jit(solution)/shard_map/dot_general | solution.py:111
  98.6 0.0 copy-done
  98.6 0.0 copy-start.2
  98.6 7.3 %maximum_reduce_fusion.3 = (f32[512]{0:T(512)S(1)}, f32[512]{0:T(512)S(1)}, f32[512]{0:T(512)S(1)}, f32[512]{0:T(512)S(1)}, f32[32,32,512]{2,1,0:T(8,128)}) fusion(f32[512]{0:T(512)S(1)} %bitcast.49, s32[512]{0:T(512)S(1)} %add_select_fusion, s32[32,32]{1,0:T(8,128)S(1)} %broadcast_add_fusion, f32[512]{0:T(512)S(1)} %bitcast.50, f32[512]{0:T(512)S(1)} %bitcast.51, ...), kind=kOutput, calls=%fused_computation.6 | convolution fusion | flops 3229612032 | bytes 5265408 | tf_op jit(solution)/shard_map/dot_general | solution.py:111
  105.9 0.1 reduce_sum.75
  106.1 0.1 reduce_sum.72
  106.2 0.1 reduce_sum.54
  106.4 0.1 reduce_sum.51
  106.5 0.0 copy-done.2
  106.5 0.2 fusion.36
  106.7 12.3 %psum.35 = f32[16,4]{0,1:T(4,128)S(1)} all-reduce(f32[16,4]{0,1:T(4,128)S(1)} %fusion.36), channel_id=1, replica_groups=mesh['row_0'=8,'row_1'=2,'col_0'=4,'col_1'=4,'col_2'=2] {'row_0'}, use_global_device_ids=true, to_apply=%region_8.9 | all-reduce | flops 64 | bytes 512 | tf_op jit(solution)/shard_map/psum | solution.py:31
  119.0 4.0 %psum.36 = f32[16,4]{0,1:T(4,128)S(1)} all-reduce(f32[16,4]{0,1:T(4,128)S(1)} %psum.35), channel_id=1, replica_groups=mesh['row_0'=8,'row_1'=2,'col_0'=4,'col_1'=4,'col_2'=2] {'row_1'}, use_global_device_ids=true, to_apply=%region_9.10 | all-reduce | flops 64 | bytes 512 | tf_op jit(solution)/shard_map/psum | solution.py:31
  123.0 10.6 %psum.37 = f32[16,4]{0,1:T(4,128)S(1)} all-reduce(f32[16,4]{0,1:T(4,128)S(1)} %psum.36), channel_id=1, replica_groups=mesh['row_0'=8,'row_1'=2,'col_0'=4,'col_1'=4,'col_2'=2] {'col_0'}, use_global_device_ids=true, to_apply=%region_10.11 | all-reduce | flops 64 | bytes 512 | tf_op jit(solution)/shard_map/psum | solution.py:31
  133.6 18.0 %psum.38 = f32[16,4]{0,1:T(4,128)S(1)} all-reduce(f32[16,4]{0,1:T(4,128)S(1)} %psum.37), channel_id=1, replica_groups=mesh['row_0'=8,'row_1'=2,'col_0'=4,'col_1'=4,'col_2'=2] {'col_1'}, use_global_device_ids=true, to_apply=%region_11.12 | all-reduce | flops 64 | bytes 512 | tf_op jit(solution)/shard_map/psum | solution.py:31
  151.5 5.7 %psum.39 = f32[16,4]{0,1:T(4,128)} all-reduce(f32[16,4]{0,1:T(4,128)S(1)} %psum.38), channel_id=1, replica_groups=mesh['row_0'=8,'row_1'=2,'col_0'=4,'col_1'=4,'col_2'=2] {'col_2'}, use_global_device_ids=true, to_apply=%region_12.13 | all-reduce | flops 64 | bytes 512 | tf_op jit(solution)/shard_map/psum | solution.py:31
  (18 shorter events, 0.2 us)
Async XLA Ops:
  2.6 57.6 %collective-permute-start = (f32[6,32,512]{2,1,0:T(8,128)}, f32[6,32,512]{2,1,0:T(8,128)S(1)}, u32[]{:S(2)}, u32[]{:S(2)}) collective-permute-start(f32[6,32,512]{2,1,0:T(8,128)} %get-tuple-element.13), channel_id=1, source_target_pairs={{0,32},{32,64},{64,96},{96,128},{128,160},{160,192},{192,224},{224... | collective-permute-start | bytes 1179656 | tf_op jit(solution)/shard_map/ppermute | solution.py:23
  6.6 55.4 %collective-permute-start.1 = (f32[6,32,512]{2,1,0:T(8,128)S(1)}, f32[6,32,512]{2,1,0:T(8,128)S(1)}, u32[]{:S(2)}, u32[]{:S(2)}) collective-permute-start(f32[6,32,512]{2,1,0:T(8,128)S(1)} %get-tuple-element.12), channel_id=1, source_target_pairs={{32,0},{64,32},{96,64},{128,96},{160,128},{192,160},{224,192},{256... | collective-permute-start | bytes 1179656 | tf_op jit(solution)/shard_map/ppermute | solution.py:24
  56.0 1.0 copy-start.1
  63.4 10.1 %collective-permute-start.2 = (f32[32,6,512]{2,1,0:T(8,128)S(1)}, f32[32,6,512]{2,1,0:T(8,128)S(1)}, u32[]{:S(2)}, u32[]{:S(2)}) collective-permute-start(f32[32,6,512]{2,1,0:T(8,128)S(1)} %get-tuple-element.10), channel_id=1, source_target_pairs={{0,1},{1,2},{2,3},{3,4},{4,5},{5,6},{6,7},{7,8},{8,9},{9,10},{10,1... | collective-permute-start | bytes 1179656 | tf_op jit(solution)/shard_map/ppermute | solution.py:23
  67.3 10.8 %collective-permute-start.3 = (f32[32,6,512]{2,1,0:T(8,128)S(1)}, f32[32,6,512]{2,1,0:T(8,128)S(1)}, u32[]{:S(2)}, u32[]{:S(2)}) collective-permute-start(f32[32,6,512]{2,1,0:T(8,128)S(1)} %get-tuple-element.11), channel_id=1, source_target_pairs={{1,0},{2,1},{3,2},{4,3},{5,4},{6,5},{7,6},{8,7},{9,8},{10,9},{11,1... | collective-permute-start | bytes 1179656 | tf_op jit(solution)/shard_map/ppermute | solution.py:24
  96.0 2.5 %copy-start = (f32[512,512]{0,1:T(8,128)S(1)}, f32[512,512]{0,1:T(8,128)}, u32[]{:S(2)}) copy-start(f32[512,512]{0,1:T(8,128)} %reshape.144) | copy-start | bytes 3145732
  98.6 7.9 %copy-start.2 = (s32[1,1,2]{2,1,0:T(1,128)S(1)}, s32[1,1,2]{2,1,0:T(1,128)}, u32[]{:S(2)}) copy-start(s32[1,1,2]{2,1,0:T(1,128)} %param.5) | copy-start | bytes 28
where the time goes:
time: 158 us; the launch traced here: 157 us
  local copies, waits for them, and re-layouts  62.3 us (39%)
  blocking collectives  50.5 us (32%)
  starting transfers between devices  20.5 us (13%)
  waiting for transfers between devices  8.6 us (5%)
  matrix products  7.53 us (5%)
  other arithmetic  6.84 us (4%)
    psum x5, blocking collectives, by_axis(): value = lax.psum(value, axis)  50.5 us
    slice x1, local copies, waits for them, and re-layouts, depth_table(): odds_half = lax.slice_in_dim(ident, 1, size_z, stride=2, axis=1)  19.5 us
    slice x1, local copies, waits for them, and re-layouts, depth_table(): evens_half = lax.slice_in_dim(ident, 0, size_z, stride=2, axis=1)  19.5 us
    slice x3, local copies, waits for them, and re-layouts, parity_part(): return lax.slice_in_dim(signal, which, length, stride=2, axis=axis_pos)  12.6 us
    ppermute x2, starting transfers between devices, extended_2(): after = lax.ppermute(initial, axis, down)  12.5 us
    ppermute x2, starting transfers between devices, extended_2(): before = lax.ppermute(last, axis, up)  7.97 us
    dot_general x1, matrix products, shards(): jnp.dot(signal.reshape(size_x * size_y, size_z), table, precision=lax.Pre...  7.35 us
    ppermute x2, waiting for transfers between devices, extended_2(): after = lax.ppermute(initial, axis, down)  4.69 us
  transfers between devices with their start and end apart: 4, of which 2 were waited for; matrix products, arithmetic and copies ran while one was open for 29% of the time, Pallas kernels for 0%

commit v1 on v0

v1 whole, which is shorter than its diff:
```python
import functools

import jax
import jax.numpy as jnp
from jax import lax
from jax.experimental import pallas as pl
from jax.experimental.pallas import tpu as pltpu
from jax.sharding import PartitionSpec as P

GROUPS = 16
LEVELS = (0.25, 0.5, 1.0, 2.0)
A, B, C, G = 0.5625, 0.0625, 0.28125, 0.03125
F32 = jnp.float32
VMEM = pl.BlockSpec(memory_space=pltpu.VMEM)
PARAMS = pltpu.CompilerParams(vmem_limit_bytes=16 << 20)
ANY = pl.BlockSpec(memory_space=pl.ANY)


def in_vmem(shape):
    return pltpu.VMEM(shape, F32)


def lane_lift(v):
    size = v.shape[-1]
    odd = lax.broadcasted_iota(jnp.int32, v.shape, 1) % 2 == 1
    near = pltpu.roll(v, 1, axis=1) + pltpu.roll(v, size - 1, axis=1)
    far = pltpu.roll(v, 3, axis=1) + pltpu.roll(v, size - 3, axis=1)
    w = jnp.where(odd, v - (A * near - B * far), v)
    near = pltpu.roll(w, 1, axis=1) + pltpu.roll(w, size - 1, axis=1)
    far = pltpu.roll(w, 3, axis=1) + pltpu.roll(w, size - 3, axis=1)
    return jnp.where(odd, w, w + (C * near - G * far))


def to_right(at):
    e0, o0, e1, o1, e2 = at(2), at(1), at(4), at(3), at(6)
    return e0, o0 - A * e0 + B * e1, o1 - A * (e1 + e0) + B * e2


def to_left(at):
    e0, o0, e1, e2 = at(0), at(1), at(2), at(4)
    return e0, e1, o0 - A * (e0 + e1) + B * e2


FROM_LEFT = {0: (C * B, C, -G), 1: (B, 0.0, 0.0), 2: (C * B, -G, 0.0), 4: (-G * B, 0.0, 0.0)}
FROM_RIGHT = {
    6: (-G * B, 0.0, 0.0),
    4: (C * B + G * A, -G * B, 0.0),
    3: (B, 0.0, 0.0),
    2: (C * (B - A), C * B, -G),
    1: (-A, B, 0.0),
}


def combine(coefs, lines):
    total = None
    for coef, line in zip(coefs, lines):
        if coef != 0.0:
            term = coef * line
            total = term if total is None else total + term
    return total


def edge_kernel(nx, ny, p_ref, right_ref, left_ref, first, last, sems):
    lo = pltpu.make_async_copy(p_ref.at[pl.ds(0, 5 * ny)], first, sems.at[0])
    hi = pltpu.make_async_copy(p_ref.at[pl.ds((nx - 6) * ny, 6 * ny)], last, sems.at[1])
    lo.start()
    hi.start()
    lo.wait()

    def left(t, _):
        rows = lambda x: pl.ds(pl.multiple_of(x * ny + t * 8, 8), 8)
        for k, v in enumerate(to_left(lambda i: first[rows(i), :])):
            left_ref[rows(k), :] = lane_lift(v)
        return 0

    lax.fori_loop(0, ny // 8, left, 0)
    hi.wait()

    def right(t, _):
        rows = lambda x: pl.ds(pl.multiple_of(x * ny + t * 8, 8), 8)
        for k, v in enumerate(to_right(lambda i: last[rows(6 - i), :])):
            right_ref[rows(k), :] = lane_lift(v)
        return 0

    lax.fori_loop(0, ny // 8, right, 0)


def row_partials(nx, ny, w_ref, x, slot, right_ref, left_ref):
    head = w_ref[pl.ds(pl.multiple_of(x * ny, 8), 8), :]
    tail = w_ref[pl.ds(pl.multiple_of(x * ny + ny - 8, 8), 8), :]
    for k, v in enumerate(to_right(lambda i: tail[8 - i : 9 - i, :])):
        right_ref[pl.ds(k * nx + slot, 1), :] = v
    for k, v in enumerate(to_left(lambda i: head[i : i + 1, :])):
        left_ref[pl.ds(k * nx + slot, 1), :] = v


def bulk_kernel(nx, ny, p_ref, after_ref, w_ref, right_ref, left_ref, raw, sems):
    del after_ref
    chunks = 4
    size = nx * ny // chunks
    copies = []
    for i in range(chunks):
        part = pl.ds(i * size, size)
        copies.append(pltpu.make_async_copy(p_ref.at[part], raw.at[part], sems.at[i]))
        copies[-1].start()
    for i in range(chunks):
        copies[i].wait()

        def depth(t, _):
            rows = pl.ds(pl.multiple_of(i * size + t * 8, 8), 8)
            w_ref[rows, :] = lane_lift(raw[rows, :])
            return 0

        lax.fori_loop(0, size // 8, depth, 0, unroll=2)
    half = nx // 2

    def column(t, _):
        for c in range(w_ref.shape[1] // 128):
            lanes = slice(c * 128, (c + 1) * 128)
            rows = lambda x: pl.ds(pl.multiple_of(x * ny + t * 8, 8), 8)
            e = [w_ref[rows(2 * j), lanes] for j in range(half)]
            d = {-2: B * e[0], -1: B * e[1] - A * e[0], half: B * e[half - 1]}
            for j in range(half):
                near = e[j] + e[j + 1] if j + 1 < half else e[j]
                v = w_ref[rows(2 * j + 1), lanes] - A * near
                far = [e[i] for i in (j - 1, j + 2) if 0 <= i < half]
                if far:
                    v = v + B * functools.reduce(lambda a, b: a + b, far)
                d[j] = v
                w_ref[rows(2 * j + 1), lanes] = v
            for j in range(half):
                w_ref[rows(2 * j), lanes] = e[j] + (C * (d[j - 1] + d[j]) - G * (d[j - 2] + d[j + 1]))
        return 0

    lax.fori_loop(0, ny // 8, column, 0)

    def partial(x, _):
        row_partials(nx, ny, w_ref, x, x, right_ref, left_ref)
        return 0

    lax.fori_loop(0, nx, partial, 0)


def plane_kernel(nx, ny, got_l_ref, got_r_ref, w_ref, right_in, left_in, fixed_ref, right_ref, left_ref):
    def fix(t, _):
        rows = lambda x: pl.ds(pl.multiple_of(x * ny + t * 8, 8), 8)
        lines = [got_l_ref[rows(k), :] for k in range(3)]
        for x in range(6):
            v = w_ref[rows(x), :]
            fixed_ref[rows(x), :] = v + combine(FROM_LEFT[x], lines) if x in FROM_LEFT else v
        lines = [got_r_ref[rows(k), :] for k in range(3)]
        for back in range(6, 0, -1):
            v = w_ref[rows(nx - back), :]
            fixed_ref[rows(12 - back), :] = v + combine(FROM_RIGHT[back], lines) if back in FROM_RIGHT else v
        return 0

    lax.fori_loop(0, ny // 8, fix, 0)
    right_ref[...] = right_in[...]
    left_ref[...] = left_in[...]
    for x in FROM_LEFT:
        row_partials(nx, ny, fixed_ref, x, x, right_ref, left_ref)
    for back in FROM_RIGHT:
        row_partials(nx, ny, fixed_ref, 12 - back, nx - back, right_ref, left_ref)


def excess(acc, v, even_plane, limits):
    m = jnp.abs(v)
    if even_plane:
        row = lax.broadcasted_iota(jnp.int32, v.shape, 0)
        lane = lax.broadcasted_iota(jnp.int32, v.shape, 1)
        m = jnp.where((row | lane) % 2 == 1, m, 0.0)
    return [a + jnp.maximum(m - lim, 0.0) for a, lim in zip(acc, limits)]


def rows_kernel(nx, ny, w_ref, fixed_ref, lim_ref, out_ref, edge_ref, acc_ref, mid, sems):
    size = w_ref.shape[1]
    acc_ref[...] = jnp.zeros_like(acc_ref)

    def lift(src, at_plane):
        v = src[pl.ds(pl.multiple_of(at_plane * ny, 8), ny), :]
        row = lax.broadcasted_iota(jnp.int32, v.shape, 0)
        odd = row % 2 == 1

        def at(u, by):
            r = pltpu.roll(u, -by % ny, axis=0)
            return jnp.where((row + by >= 0) & (row + by < ny), r, 0.0)

        near = at(v, -1) + at(v, 1)
        far = at(v, -3) + at(v, 3)
        w = jnp.where(odd, v - (A * near - B * far), v)
        near = at(w, -1) + at(w, 1)
        far = at(w, -3) + at(w, 3)
        s = w + (C * near - G * far)
        e0, e1, last = v[0:1, :], v[2:3, :], v[ny - 2 : ny - 1, :]
        before1, before2, after = B * e1 - A * e0, B * e0, B * last
        s = s + jnp.where(row == 0, C * before1 - G * before2, 0.0)
        s = s + jnp.where(row == 2, -G * before1, 0.0)
        s = s + jnp.where(row == ny - 2, -G * after, 0.0)
        return jnp.where(odd, w, s)

    def plane(src, at_plane, x, even_plane):
        v = lift(src, at_plane)
        edge_ref[pl.ds(pl.multiple_of(x * 16, 8), 8), :] = v[0:8, :]
        edge_ref[pl.ds(pl.multiple_of(x * 16 + 8, 8), 8), :] = v[ny - 8 : ny, :]
        mid[x] = v[8 : ny - 8, :]
        limits = [jnp.broadcast_to(lim_ref[l : l + 1, :], (8, size)) for l in range(4)]
        acc = [acc_ref[l] for l in range(4)]
        for t in range(1, ny // 8 - 1):
            acc = excess(acc, v[8 * t : 8 * t + 8, :], even_plane, limits)
        for l in range(4):
            acc_ref[l] = acc[l]

    copies = []
    middle = (nx - 12) // 2
    for i, (src, start, x0, each) in enumerate(
        ((fixed_ref, 0, 0, 6), (w_ref, 6, 6, middle), (w_ref, 6 + middle, 6 + middle, middle), (fixed_ref, 6, nx - 6, 6))
    ):

        def pair(j, _):
            plane(src, start + 2 * j, x0 + 2 * j, True)
            plane(src, start + 2 * j + 1, x0 + 2 * j + 1, False)
            return 0

        lax.fori_loop(0, each // 2, pair, 0)
        part = pl.ds(x0, each)
        copies.append(pltpu.make_async_copy(mid.at[part], out_ref.at[part, pl.ds(8, ny - 16), :], sems.at[i]))
        copies[-1].start()
    for copy in copies:
        copy.wait()


def final_kernel(nx, ny, scale, got_l_ref, got_r_ref, edge_ref, acc_in, lim_ref, hot_ref, out_in, out_ref, mass_ref, head, tail, acc_ref, sems):
    del out_in
    size = edge_ref.shape[1]
    row = lax.broadcasted_iota(jnp.int32, (8, size), 0)

    def weights(table, place, k):
        total = jnp.zeros((8, size), F32)
        for line, coefs in table.items():
            if coefs[k] != 0.0:
                total = jnp.where(row == place(line), coefs[k], total)
        return total

    from_l = [weights(FROM_LEFT, lambda i: i, k) for k in range(3)]
    from_r = [weights(FROM_RIGHT, lambda i: 8 - i, k) for k in range(3)]
    acc_ref[...] = acc_in[...]

    def tiles(x, even_plane):
        limits = [jnp.broadcast_to(lim_ref[l : l + 1, :], (8, size)) for l in range(4)]
        acc = [acc_ref[l] for l in range(4)]
        for got, table, dest, at in ((got_l_ref, from_l, head, 0), (got_r_ref, from_r, tail, 8)):
            v = edge_ref[pl.ds(pl.multiple_of(x * 16 + at, 8), 8), :]
            for k in range(3):
                v = v + table[k] * got[pl.ds(k * nx + x, 1), :]
            dest[x] = v
            acc = excess(acc, v, even_plane, limits)
        for l in range(4):
            acc_ref[l] = acc[l]

    parts = 4
    each = nx // parts
    copies = []
    for i in range(parts):

        def pair(j, _):
            tiles(i * each + 2 * j, True)
            tiles(i * each + 2 * j + 1, False)
            return 0

        lax.fori_loop(0, each // 2, pair, 0)
        part = pl.ds(i * each, each)
        for n, (src, at) in enumerate(((head, 0), (tail, ny - 8))):
            copies.append(pltpu.make_async_copy(src.at[part], out_ref.at[part, pl.ds(at, 8), :], sems.at[2 * i + n]))
            copies[-1].start()
    blocks = 2
    width = size // blocks
    lines = []
    for c in range(blocks):
        for l in range(4):
            lines.append(jnp.sum(acc_ref[l, :, c * width : (c + 1) * width], axis=0, keepdims=True))
    sums = jnp.sum(jnp.concatenate(lines, axis=0), axis=1, keepdims=True)
    line = jnp.sum(sums * hot_ref[...], axis=0, keepdims=True) * scale
    for i in range(mass_ref.shape[0]):
        mass_ref[i] = line
    for copy in copies:
        copy.wait()


def neighbours(value_up, value_down, axis):
    n = lax.axis_size(axis)
    up = [(i, (i + 1) % n) for i in range(n)]
    return lax.ppermute(value_up, axis, up), lax.ppermute(value_down, axis, [(j, i) for i, j in up])


def near(*values):
    return [pltpu.with_memory_space_constraint(v, pltpu.VMEM) for v in values]


def far(value):
    return pltpu.with_memory_space_constraint(value, pltpu.HBM)


def cost(flops):
    return pl.CostEstimate(flops=flops, bytes_accessed=4 << 20, transcendentals=0)


def shards(pressure, cut_exponent, group_map):
    nx, ny, size = pressure.shape
    flat = pressure.reshape(nx * ny, size)
    blocks_z = cut_exponent.shape[2]
    scales = jnp.exp2(-cut_exponent[0, 0].astype(F32))
    limits = jnp.repeat(jnp.array(LEVELS, F32)[:, None] * scales[None, :], size // blocks_z, axis=1)
    lane = jnp.arange(128, dtype=jnp.int32)[None, None, :]
    want = 4 * group_map[0, 0][:, None, None] + jnp.arange(4, dtype=jnp.int32)[None, :, None]
    hot = (lane == want).astype(F32).reshape(4 * blocks_z, 128)
    edge = pl.pallas_call(
        functools.partial(edge_kernel, nx, ny),
        out_shape=(in_vmem((3 * ny, size)), in_vmem((3 * ny, size))),
        in_specs=[ANY],
        out_specs=(VMEM, VMEM),
        scratch_shapes=[pltpu.VMEM((5 * ny, size), F32), pltpu.VMEM((6 * ny, size), F32), pltpu.SemaphoreType.DMA((2,))],
        compiler_params=PARAMS,
        name="edge",
    )
    right, left = edge(far(flat))
    from_left, from_right = neighbours(right, left, "row")
    bulk = pl.pallas_call(
        functools.partial(bulk_kernel, nx, ny),
        out_shape=(in_vmem((nx * ny, size)), in_vmem((3 * nx, size)), in_vmem((3 * nx, size))),
        in_specs=[ANY, VMEM],
        out_specs=(VMEM, VMEM, VMEM),
        scratch_shapes=[pltpu.VMEM((nx * ny, size), F32), pltpu.SemaphoreType.DMA((4,))],
        cost_estimate=cost(40_000_000),
        compiler_params=PARAMS,
        name="bulk",
    )
    work, right, left = bulk(far(flat), *near(right))
    plane = pl.pallas_call(
        functools.partial(plane_kernel, nx, ny),
        out_shape=(in_vmem((12 * ny, size)), in_vmem((3 * nx, size)), in_vmem((3 * nx, size))),
        in_specs=[VMEM] * 5,
        out_specs=(VMEM, VMEM, VMEM),
        compiler_params=PARAMS,
        name="plane",
    )
    fixed, right, left = plane(*near(from_left, from_right, work, right, left))
    from_left, from_right = neighbours(right, left, "col")
    rows = pl.pallas_call(
        functools.partial(rows_kernel, nx, ny),
        out_shape=(jax.ShapeDtypeStruct((nx, ny, size), F32), in_vmem((nx * 16, size)), in_vmem((4, 8, size))),
        in_specs=[VMEM, VMEM, VMEM],
        out_specs=(ANY, VMEM, VMEM),
        scratch_shapes=[pltpu.VMEM((nx, ny - 16, size), F32), pltpu.SemaphoreType.DMA((4,))],
        cost_estimate=cost(40_000_000),
        compiler_params=PARAMS,
        name="rows",
    )
    coeffs, edges, acc = rows(*near(work, fixed, limits))
    n_row, n_col = lax.axis_size("row"), lax.axis_size("col")
    scale = 1.0 / (nx * ny * (size // blocks_z))
    final = pl.pallas_call(
        functools.partial(final_kernel, nx, ny, scale),
        out_shape=(jax.ShapeDtypeStruct((nx, ny, size), F32), in_vmem((n_row, 1, 128))),
        in_specs=[VMEM] * 6 + [ANY],
        out_specs=(ANY, VMEM),
        input_output_aliases={6: 0},
        scratch_shapes=[
            pltpu.VMEM((nx, 8, size), F32),
            pltpu.VMEM((nx, 8, size), F32),
            pltpu.VMEM((4, 8, size), F32),
            pltpu.SemaphoreType.DMA((8,)),
        ],
        compiler_params=PARAMS,
        name="final",
    )
    coeffs, mass = final(*near(from_left, from_right, edges, acc, limits, hot), coeffs)
    mass = lax.all_to_all(mass, "row", 0, 0).sum(0, keepdims=True)
    mass = lax.all_to_all(jnp.broadcast_to(mass, (n_col, 1, 128)), "col", 0, 0).sum(0)
    return coeffs, mass[0, : 4 * GROUPS].reshape(GROUPS, 4)


def solution(mesh):
    split = P("row", "col", None)
    return jax.shard_map(shards, mesh=mesh, in_specs=(split, split, split), out_specs=(split, P()), check_vma=False)
```

time: 158 us -> 82.2 us (0.52)
  local copies, waits for them, and re-layouts: 62.3 us -> 0.96 us
  Pallas kernels: 0 us -> 25 us
  blocking collectives: 50.5 us -> 33.9 us
  waiting for transfers between devices: 8.6 us -> 0.69 us
  matrix products: 7.53 us -> 0 us
  other arithmetic: 6.84 us -> 0.28 us
    slice x9 -> x1, local copies, waits for them, and re-layouts: 53.8 us -> 0.02 us  [shards(): return (coeffs, mass[0, :4 * GROUPS].reshape(GROUPS, 4))]
    psum x5 -> x0, blocking collectives: 50.5 us -> none  [by_axis(): value = lax.psum(value, axis)]
    all_to_all x0 -> x2, blocking collectives: none -> 33.9 us  [the longest x1 22.5 us: shards(): lax.all_to_all(jnp.broadcast_to(mass, (n_col, 1, 128)), 'col', 0, 0).sum(0)]
    pallas_call x0 -> x5, Pallas kernels: none -> 25 us  [the longest x1 15.8 us: shards(): work, right, left = bulk(far(flat), *near(right))]
    ppermute x4, waiting for transfers between devices: 8.6 us -> 0.69 us  [the longest x2 0.69 us: neighbours(): lax.ppermute(value_down, axis, [(j, i) for i, j in up])]
    dot_general x2 -> x0, matrix products: 7.53 us -> none  [the longest x1 7.35 us: shards(): jnp.dot(signal.reshape(size_x * size_y, size_z), table, precision=lax.Pre...]
    dot_general x1 -> x0, local copies, waits for them, and re-layouts: 2.51 us -> none  [shards(): jnp.dot(signal.reshape(size_x * size_y, size_z), table, precision=lax.Pre...]
    another operation x2 -> x1, local copies, waits for them, and re-layouts: 2.27 us -> 0.08 us  [shards(): return (coeffs, mass[0, :4 * GROUPS].reshape(GROUPS, 4))]
  transfers between devices with their start and end apart: 4 -> 4, of which waited for: 2 -> 1; matrix products, arithmetic and copies ran while one was open for 29% -> 0% of each run, Pallas kernels for 0% -> 25%
where the time goes in v1:
time: 82.2 us; the launch traced here: 81.9 us
  blocking collectives  33.9 us (41%)
  Pallas kernels  25 us (30%)
  starting transfers between devices  20.3 us (25%)
  local copies, waits for them, and re-layouts  0.96 us (1%)
    all_to_all x1, blocking collectives, shards(): lax.all_to_all(jnp.broadcast_to(mass, (n_col, 1, 128)), 'col', 0, 0).sum(0)  22.5 us
    pallas_call x1, Pallas kernels, shards(): work, right, left = bulk(far(flat), *near(right))  15.8 us
    ppermute x2, starting transfers between devices, neighbours(): lax.ppermute(value_down, axis, [(j, i) for i, j in up])  12.3 us
    all_to_all x1, blocking collectives, shards(): mass = lax.all_to_all(mass, 'row', 0, 0).sum(0, keepdims=True)  11.3 us
    ppermute x2, starting transfers between devices, neighbours(): lax.ppermute(value_up, axis, up)  7.98 us
    pallas_call x1, Pallas kernels, shards(): coeffs, edges, acc = rows(*near(work, fixed, limits))  4.58 us
    pallas_call x1, Pallas kernels, shards(): right, left = edge(far(flat))  2.69 us
  transfers between devices with their start and end apart: 4, of which 1 were waited for; matrix products, arithmetic and copies ran while one was open for 0% of the time, Pallas kernels for 25%

profile of v1, /device:TPU:1, one launch (start us, length us, event | category | flops | bytes accessed | tf_op | source)
XLA Modules:
  0.0 81.9 jit_solution(14571271197469429122)
XLA Ops:
  0.6 0.0 copy-start
  0.6 0.0 copy-start.1
  0.7 0.0 copy-start.2
  0.7 2.7 %edge.1 = (f32[96,512]{1,0:T(8,128)S(1)}, f32[96,512]{1,0:T(8,128)S(1)}) custom-call(f32[1024,512]{1,0:T(8,128)} %bitcast.12), custom_call_target="tpu_custom_call" | custom-call | tf_op jit(solution)/shard_map/edge/pallas_call | solution.py:325
  3.4 4.0 %collective-permute-start = (f32[96,512]{1,0:T(8,128)S(1)}, f32[96,512]{1,0:T(8,128)S(1)}, u32[]{:S(2)}, u32[]{:S(2)}) collective-permute-start(f32[96,512]{1,0:T(8,128)S(1)} %get-tuple-element.15.after_ref), channel_id=1, source_target_pairs={{0,32},{32,64},{64,96},{96,128},{128,160},{160,192},{192,224},{224... | collective-permute-start | bytes 589832 | tf_op jit(solution)/shard_map/ppermute | solution.py:292
  7.4 10.4 %collective-permute-start.1 = (f32[96,512]{1,0:T(8,128)S(1)}, f32[96,512]{1,0:T(8,128)S(1)}, u32[]{:S(2)}, u32[]{:S(2)}) collective-permute-start(f32[96,512]{1,0:T(8,128)S(1)} %get-tuple-element.16), channel_id=1, source_target_pairs={{32,0},{64,32},{96,64},{128,96},{160,128},{192,160},{224,192},{256... | collective-permute-start | bytes 589832 | tf_op jit(solution)/shard_map/ppermute | solution.py:292
  17.8 0.0 copy-done.1
  17.8 0.0 copy-done
  17.8 0.1 broadcast_multiply_fusion
  17.9 0.1 broadcast_bitcast_fusion
  18.0 0.0 copy-done.2
  18.0 0.1 iota_add_fusion
  18.1 0.1 add.24
  18.1 15.8 %bulk.1 = (f32[1024,512]{1,0:T(8,128)S(1)}, f32[96,512]{1,0:T(8,128)S(1)}, f32[96,512]{1,0:T(8,128)S(1)}) custom-call(f32[1024,512]{1,0:T(8,128)} %bitcast.13, f32[96,512]{1,0:T(8,128)S(1)} %get-tuple-element.15.after_ref), custom_call_target="tpu_custom_call" | custom-call | flops 40000000 | bytes 4194304 | tf_op jit(solution)/shard_map/bulk/pallas_call | solution.py:337
  34.0 0.0 collective-permute-done.got_l_ref
  34.0 0.0 collective-permute-done.1.got_r_ref
  34.0 0.3 plane.1
  34.3 4.0 %collective-permute-start.2 = (f32[96,512]{1,0:T(8,128)S(1)}, f32[96,512]{1,0:T(8,128)S(1)}, u32[]{:S(2)}, u32[]{:S(2)}) collective-permute-start(f32[96,512]{1,0:T(8,128)S(1)} %get-tuple-element.20), channel_id=1, source_target_pairs={{0,1},{1,2},{2,3},{3,4},{4,5},{5,6},{6,7},{7,8},{8,9},{9,10},{10,1... | collective-permute-start | bytes 589832 | tf_op jit(solution)/shard_map/ppermute | solution.py:292
  38.3 1.9 %collective-permute-start.3 = (f32[96,512]{1,0:T(8,128)S(1)}, f32[96,512]{1,0:T(8,128)S(1)}, u32[]{:S(2)}, u32[]{:S(2)}) collective-permute-start(f32[96,512]{1,0:T(8,128)S(1)} %get-tuple-element.21), channel_id=1, source_target_pairs={{1,0},{2,1},{3,2},{4,3},{5,4},{6,5},{7,6},{8,7},{9,8},{10,9},{11,1... | collective-permute-start | bytes 589832 | tf_op jit(solution)/shard_map/ppermute | solution.py:292
  40.2 0.1 fusion.hot_ref
  40.3 4.6 %rows.1 = (f32[32,32,512]{2,1,0:T(8,128)}, f32[512,512]{1,0:T(8,128)S(1)}, f32[4,8,512]{2,1,0:T(8,128)S(1)}) custom-call(f32[1024,512]{1,0:T(8,128)S(1)} %get-tuple-element.17.w_ref, f32[384,512]{1,0:T(8,128)S(1)} %get-tuple-element.22.fixed_ref, f32[4,512]{1,0:T(4,128)S(1)} %bitcast.10), custom_call_target="tpu_custom_call" | custom-call | flops 40000000 | bytes 4194304 | tf_op jit(solution)/shard_map/rows/pallas_call | solution.py:358
  44.9 0.0 collective-permute-done.2.got_l_ref
  44.9 0.7 collective-permute-done.3.got_r_ref
  45.6 1.6 %final.1 = (f32[32,32,512]{2,1,0:T(8,128)}, f32[16,1,128]{2,1,0:T(1,128)S(1)}) custom-call(f32[96,512]{1,0:T(8,128)S(1)} %collective-permute-done.2.got_l_ref, f32[96,512]{1,0:T(8,128)S(1)} %collective-permute-done.3.got_r_ref, f32[512,512]{1,0:T(8,128)S(1)} %get-tuple-element.23.edge_ref, ...), custom_call_target="tpu_custom_call", output_to_operand_aliasing={{0}: (6, {})} | custom-call | tf_op jit(solution)/shard_map/final/pallas_call | solution.py:376
  47.2 11.3 %all_to_all.10 = f32[16,1,128]{2,1,0:T(1,128)S(1)} all-to-all(f32[16,1,128]{2,1,0:T(1,128)S(1)} %get-tuple-element.27), channel_id=1, replica_groups=mesh['row'=16,'col'=32] {'row'}, dimensions={0} | all-to-all | bytes 16384 | tf_op jit(solution)/shard_map/all_to_all | solution.py:377
  58.6 22.5 %all_to_all.11 = f32[32,1,128]{2,1,0:T(1,128)S(1)} all-to-all(f32[32,1,128]{2,1,0:T(1,128)S(1)} %broadcast_in_dim.5), channel_id=1, replica_groups=mesh['row'=16,'col'=32] {'col'}, dimensions={0} | all-to-all | bytes 32768 | tf_op jit(solution)/shard_map/all_to_all | solution.py:378
  81.2 0.1 reshape_squeeze.3
  81.3 0.7 copy.11
  (7 shorter events, 0.1 us)
Async XLA Ops:
  0.6 17.2 %copy-start = (f32[4]{0:T(128)S(1)}, f32[4]{0:T(128)}, u32[]{:S(2)}) copy-start(f32[4]{0:T(128)} %constant.8.clone) | copy-start | bytes 52
  0.6 17.2 %copy-start.1 = (s32[1,1,2]{2,1,0:T(1,128)S(1)}, s32[1,1,2]{2,1,0:T(1,128)}, u32[]{:S(2)}) copy-start(s32[1,1,2]{2,1,0:T(1,128)} %param.5) | copy-start | bytes 28
  0.7 17.3 %copy-start.2 = (s32[1,1,2]{2,1,0:T(1,128)S(1)}, s32[1,1,2]{2,1,0:T(1,128)}, u32[]{:S(2)}) copy-start(s32[1,1,2]{2,1,0:T(1,128)} %param.6) | copy-start | bytes 28
  3.4 30.6 %collective-permute-start = (f32[96,512]{1,0:T(8,128)S(1)}, f32[96,512]{1,0:T(8,128)S(1)}, u32[]{:S(2)}, u32[]{:S(2)}) collective-permute-start(f32[96,512]{1,0:T(8,128)S(1)} %get-tuple-element.15.after_ref), channel_id=1, source_target_pairs={{0,32},{32,64},{64,96},{96,128},{128,160},{160,192},{192,224},{224... | collective-permute-start | bytes 589832 | tf_op jit(solution)/shard_map/ppermute | solution.py:292
  7.4 26.6 %collective-permute-start.1 = (f32[96,512]{1,0:T(8,128)S(1)}, f32[96,512]{1,0:T(8,128)S(1)}, u32[]{:S(2)}, u32[]{:S(2)}) collective-permute-start(f32[96,512]{1,0:T(8,128)S(1)} %get-tuple-element.16), channel_id=1, source_target_pairs={{32,0},{64,32},{96,64},{128,96},{160,128},{192,160},{224,192},{256... | collective-permute-start | bytes 589832 | tf_op jit(solution)/shard_map/ppermute | solution.py:292
  34.3 10.6 %collective-permute-start.2 = (f32[96,512]{1,0:T(8,128)S(1)}, f32[96,512]{1,0:T(8,128)S(1)}, u32[]{:S(2)}, u32[]{:S(2)}) collective-permute-start(f32[96,512]{1,0:T(8,128)S(1)} %get-tuple-element.20), channel_id=1, source_target_pairs={{0,1},{1,2},{2,3},{3,4},{4,5},{5,6},{6,7},{7,8},{8,9},{9,10},{10,1... | collective-permute-start | bytes 589832 | tf_op jit(solution)/shard_map/ppermute | solution.py:292
  38.3 7.3 %collective-permute-start.3 = (f32[96,512]{1,0:T(8,128)S(1)}, f32[96,512]{1,0:T(8,128)S(1)}, u32[]{:S(2)}, u32[]{:S(2)}) collective-permute-start(f32[96,512]{1,0:T(8,128)S(1)} %get-tuple-element.21), channel_id=1, source_target_pairs={{1,0},{2,1},{3,2},{4,3},{5,4},{6,5},{7,6},{8,7},{9,8},{10,9},{11,1... | collective-permute-start | bytes 589832 | tf_op jit(solution)/shard_map/ppermute | solution.py:292

commit v2 on v1

--- a/solution.py
+++ b/solution.py
@@ -2,6 +2,7 @@
 
 import jax
 import jax.numpy as jnp
+import numpy as np
 from jax import lax
 from jax.experimental import pallas as pl
 from jax.experimental.pallas import tpu as pltpu
@@ -31,6 +32,25 @@
     return jnp.where(odd, w, w + (C * near - G * far))
 
 
+def lane_table(size):
+    shift = lambda m, by: np.roll(m, by, axis=1)
+    ident = np.eye(size)
+    e, o = ident[:, 0::2], ident[:, 1::2]
+    d = o - A * (e + shift(e, -1)) + B * (shift(e, 1) + shift(e, -2))
+    s = e + C * (shift(d, 1) + d) - G * (shift(d, 2) + shift(d, -1))
+    return np.stack([s, d], axis=2).reshape(size, size).astype(jnp.bfloat16)
+
+
+def table_lift(v, table):
+    total = None
+    for _ in range(3):
+        piece = v.astype(jnp.bfloat16)
+        v = v - piece.astype(F32)
+        term = jnp.dot(piece, table, preferred_element_type=F32)
+        total = term if total is None else total + term
+    return total
+
+
 def to_right(at):
     e0, o0, e1, o1, e2 = at(2), at(1), at(4), at(3), at(6)
     return e0, o0 - A * e0 + B * e1, o1 - A * (e1 + e0) + B * e2
@@ -66,23 +86,11 @@
     lo.start()
     hi.start()
     lo.wait()
-
-    def left(t, _):
-        rows = lambda x: pl.ds(pl.multiple_of(x * ny + t * 8, 8), 8)
-        for k, v in enumerate(to_left(lambda i: first[rows(i), :])):
-            left_ref[rows(k), :] = lane_lift(v)
-        return 0
-
-    lax.fori_loop(0, ny // 8, left, 0)
+    for k, v in enumerate(to_left(lambda i: first[pl.ds(i * ny, ny), :])):
+        left_ref[pl.ds(k * ny, ny), :] = lane_lift(v)
     hi.wait()
-
-    def right(t, _):
-        rows = lambda x: pl.ds(pl.multiple_of(x * ny + t * 8, 8), 8)
-        for k, v in enumerate(to_right(lambda i: last[rows(6 - i), :])):
-            right_ref[rows(k), :] = lane_lift(v)
-        return 0
-
-    lax.fori_loop(0, ny // 8, right, 0)
+    for k, v in enumerate(to_right(lambda i: last[pl.ds((6 - i) * ny, ny), :])):
+        right_ref[pl.ds(k * ny, ny), :] = lane_lift(v)
 
 
 def row_partials(nx, ny, w_ref, x, slot, right_ref, left_ref):
@@ -94,7 +102,7 @@
         left_ref[pl.ds(k * nx + slot, 1), :] = v
 
 
-def bulk_kernel(nx, ny, p_ref, after_ref, w_ref, right_ref, left_ref, raw, sems):
+def bulk_kernel(nx, ny, p_ref, after_ref, table_ref, w_ref, right_ref, left_ref, raw, sems):
     del after_ref
     chunks = 4
     size = nx * ny // chunks
@@ -106,12 +114,8 @@
     for i in range(chunks):
         copies[i].wait()
 
-        def depth(t, _):
-            rows = pl.ds(pl.multiple_of(i * size + t * 8, 8), 8)
-            w_ref[rows, :] = lane_lift(raw[rows, :])
-            return 0
-
-        lax.fori_loop(0, size // 8, depth, 0, unroll=2)
+        part = pl.ds(i * size, size)
+        w_ref[part, :] = table_lift(raw[part, :], table_ref[...])
     half = nx // 2
 
     def column(t, _):
@@ -138,7 +142,7 @@
         row_partials(nx, ny, w_ref, x, x, right_ref, left_ref)
         return 0
 
-    lax.fori_loop(0, nx, partial, 0)
+    lax.fori_loop(0, nx, partial, 0, unroll=4)
 
 
 def plane_kernel(nx, ny, got_l_ref, got_r_ref, w_ref, right_in, left_in, fixed_ref, right_ref, left_ref):
@@ -178,25 +182,12 @@
 
     def lift(src, at_plane):
         v = src[pl.ds(pl.multiple_of(at_plane * ny, 8), ny), :]
-        row = lax.broadcasted_iota(jnp.int32, v.shape, 0)
-        odd = row % 2 == 1
-
-        def at(u, by):
-            r = pltpu.roll(u, -by % ny, axis=0)
-            return jnp.where((row + by >= 0) & (row + by < ny), r, 0.0)
-
-        near = at(v, -1) + at(v, 1)
-        far = at(v, -3) + at(v, 3)
-        w = jnp.where(odd, v - (A * near - B * far), v)
-        near = at(w, -1) + at(w, 1)
-        far = at(w, -3) + at(w, 3)
-        s = w + (C * near - G * far)
-        e0, e1, last = v[0:1, :], v[2:3, :], v[ny - 2 : ny - 1, :]
-        before1, before2, after = B * e1 - A * e0, B * e0, B * last
-        s = s + jnp.where(row == 0, C * before1 - G * before2, 0.0)
-        s = s + jnp.where(row == 2, -G * before1, 0.0)
-        s = s + jnp.where(row == ny - 2, -G * after, 0.0)
-        return jnp.where(odd, w, s)
+        v = jnp.concatenate([v, jnp.zeros((8, size), F32)], axis=0)
+        odd = lax.broadcasted_iota(jnp.int32, v.shape, 0) % 2 == 1
+        at = lambda u, by: pltpu.roll(u, by % (ny + 8), axis=0)
+        w = jnp.where(odd, v - (A * (at(v, 1) + at(v, -1)) - B * (at(v, 3) + at(v, -3))), v)
+        s = w + (C * (at(w, 1) + at(w, -1)) - G * (at(w, 3) + at(w, -3)))
+        return jnp.where(odd, w, s)[0:ny, :]
 
     def plane(src, at_plane, x, even_plane):
         v = lift(src, at_plane)
@@ -279,9 +270,10 @@
         for l in range(4):
             lines.append(jnp.sum(acc_ref[l, :, c * width : (c + 1) * width], axis=0, keepdims=True))
     sums = jnp.sum(jnp.concatenate(lines, axis=0), axis=1, keepdims=True)
-    line = jnp.sum(sums * hot_ref[...], axis=0, keepdims=True) * scale
+    sums = (sums * scale) * hot_ref[...]
+    both = sums[0:4, :] + sums[4:8, :]
     for i in range(mass_ref.shape[0]):
-        mass_ref[i] = line
+        mass_ref[i] = both
     for copy in copies:
         copy.wait()
 
@@ -310,9 +302,7 @@
     blocks_z = cut_exponent.shape[2]
     scales = jnp.exp2(-cut_exponent[0, 0].astype(F32))
     limits = jnp.repeat(jnp.array(LEVELS, F32)[:, None] * scales[None, :], size // blocks_z, axis=1)
-    lane = jnp.arange(128, dtype=jnp.int32)[None, None, :]
-    want = 4 * group_map[0, 0][:, None, None] + jnp.arange(4, dtype=jnp.int32)[None, :, None]
-    hot = (lane == want).astype(F32).reshape(4 * blocks_z, 128)
+    hot = (jnp.arange(128, dtype=jnp.int32)[None, :] == jnp.repeat(group_map[0, 0], 4)[:, None]).astype(F32)
     edge = pl.pallas_call(
         functools.partial(edge_kernel, nx, ny),
         out_shape=(in_vmem((3 * ny, size)), in_vmem((3 * ny, size))),
@@ -327,14 +317,14 @@
     bulk = pl.pallas_call(
         functools.partial(bulk_kernel, nx, ny),
         out_shape=(in_vmem((nx * ny, size)), in_vmem((3 * nx, size)), in_vmem((3 * nx, size))),
-        in_specs=[ANY, VMEM],
+        in_specs=[ANY, VMEM, VMEM],
         out_specs=(VMEM, VMEM, VMEM),
         scratch_shapes=[pltpu.VMEM((nx * ny, size), F32), pltpu.SemaphoreType.DMA((4,))],
         cost_estimate=cost(40_000_000),
         compiler_params=PARAMS,
         name="bulk",
     )
-    work, right, left = bulk(far(flat), *near(right))
+    work, right, left = bulk(far(flat), *near(right, jnp.asarray(lane_table(size))))
     plane = pl.pallas_call(
         functools.partial(plane_kernel, nx, ny),
         out_shape=(in_vmem((12 * ny, size)), in_vmem((3 * nx, size)), in_vmem((3 * nx, size))),
@@ -360,7 +350,7 @@
     scale = 1.0 / (nx * ny * (size // blocks_z))
     final = pl.pallas_call(
         functools.partial(final_kernel, nx, ny, scale),
-        out_shape=(jax.ShapeDtypeStruct((nx, ny, size), F32), in_vmem((n_row, 1, 128))),
+        out_shape=(jax.ShapeDtypeStruct((nx, ny, size), F32), in_vmem((n_row, 4, 128))),
         in_specs=[VMEM] * 6 + [ANY],
         out_specs=(ANY, VMEM),
         input_output_aliases={6: 0},
@@ -374,9 +364,9 @@
         name="final",
     )
     coeffs, mass = final(*near(from_left, from_right, edges, acc, limits, hot), coeffs)
-    mass = lax.all_to_all(mass, "row", 0, 0).sum(0, keepdims=True)
-    mass = lax.all_to_all(jnp.broadcast_to(mass, (n_col, 1, 128)), "col", 0, 0).sum(0)
-    return coeffs, mass[0, : 4 * GROUPS].reshape(GROUPS, 4)
+    mass = lax.all_to_all(mass, "row", 0, 0).sum(0)
+    mass = lax.all_to_all(jnp.broadcast_to(mass, (n_col, 4, 128)), "col", 0, 0).sum(0)
+    return coeffs, mass[:, :GROUPS].T
 
 
 def solution(mesh):

time: 82.2 us -> 73.3 us (0.89)
  Pallas kernels: 25 us -> 13.5 us
  blocking collectives: 33.9 us -> 35.6 us
  waiting for transfers between devices: 0.69 us -> 1.69 us
    pallas_call x1, Pallas kernels: 15.8 us -> 5.58 us  [shards(): bulk(far(flat), *near(right, jnp.asarray(lane_table(size))))]
    all_to_all x2, blocking collectives: 33.9 us -> 35.6 us  [the longest x1 23.4 us: shards(): lax.all_to_all(jnp.broadcast_to(mass, (n_col, 4, 128)), 'col', 0, 0).sum(0)]
    ppermute x2, waiting for transfers between devices: 0.69 us -> 1.68 us  [neighbours(): lax.ppermute(value_down, axis, [(j, i) for i, j in up])]
    pallas_call x1, Pallas kernels: 4.58 us -> 3.59 us  [shards(): coeffs, edges, acc = rows(*near(work, fixed, limits))]
  transfers between devices with their start and end apart: 4 -> 4, of which waited for: 1 -> 1; matrix products, arithmetic and copies ran while one was open for 0% -> 1% of each run, Pallas kernels for 25% -> 13%
where the time goes in v2:
time: 73.3 us; the launch traced here: 73 us
  blocking collectives  35.6 us (49%)
  starting transfers between devices  20.3 us (28%)
  Pallas kernels  13.5 us (18%)
  waiting for transfers between devices  1.69 us (2%)
  local copies, waits for them, and re-layouts  0.85 us (1%)
  between operations  0.78 us (1%)
    all_to_all x1, blocking collectives, shards(): lax.all_to_all(jnp.broadcast_to(mass, (n_col, 4, 128)), 'col', 0, 0).sum(0)  23.4 us
    ppermute x2, starting transfers between devices, neighbours(): lax.ppermute(value_down, axis, [(j, i) for i, j in up])  12.3 us
    all_to_all x1, blocking collectives, shards(): mass = lax.all_to_all(mass, 'row', 0, 0).sum(0)  12.2 us
    ppermute x2, starting transfers between devices, neighbours(): lax.ppermute(value_up, axis, up)  7.98 us
    pallas_call x1, Pallas kernels, shards(): bulk(far(flat), *near(right, jnp.asarray(lane_table(size))))  5.58 us
    pallas_call x1, Pallas kernels, shards(): coeffs, edges, acc = rows(*near(work, fixed, limits))  3.59 us
    pallas_call x1, Pallas kernels, shards(): right, left = edge(far(flat))  2.38 us
    ppermute x2, waiting for transfers between devices, neighbours(): lax.ppermute(value_down, axis, [(j, i) for i, j in up])  1.68 us
  transfers between devices with their start and end apart: 4, of which 1 were waited for; matrix products, arithmetic and copies ran while one was open for 1% of the time, Pallas kernels for 13%

profile of v2, /device:TPU:1, one launch (start us, length us, event | category | flops | bytes accessed | tf_op | source)
XLA Modules:
  0.0 73.0 jit_solution(7937787610645859129)
XLA Ops:
  0.6 0.0 copy-start.1
  0.6 0.0 copy-start
  0.7 0.0 copy-start.2
  0.7 0.0 copy-start.3
  0.7 2.4 %edge.1 = (f32[96,512]{1,0:T(8,128)S(1)}, f32[96,512]{1,0:T(8,128)S(1)}) custom-call(f32[1024,512]{1,0:T(8,128)} %bitcast.11), custom_call_target="tpu_custom_call" | custom-call | tf_op jit(solution)/shard_map/edge/pallas_call | solution.py:315
  3.1 4.0 %collective-permute-start = (f32[96,512]{1,0:T(8,128)S(1)}, f32[96,512]{1,0:T(8,128)S(1)}, u32[]{:S(2)}, u32[]{:S(2)}) collective-permute-start(f32[96,512]{1,0:T(8,128)S(1)} %get-tuple-element.15.after_ref), channel_id=1, source_target_pairs={{0,32},{32,64},{64,96},{96,128},{128,160},{160,192},{192,224},{224... | collective-permute-start | bytes 589832 | tf_op jit(solution)/shard_map/ppermute | solution.py:284
  7.1 10.4 %collective-permute-start.1 = (f32[96,512]{1,0:T(8,128)S(1)}, f32[96,512]{1,0:T(8,128)S(1)}, u32[]{:S(2)}, u32[]{:S(2)}) collective-permute-start(f32[96,512]{1,0:T(8,128)S(1)} %get-tuple-element.16), channel_id=1, source_target_pairs={{32,0},{64,32},{96,64},{128,96},{160,128},{192,160},{224,192},{256... | collective-permute-start | bytes 589832 | tf_op jit(solution)/shard_map/ppermute | solution.py:284
  17.5 0.0 copy-done.2
  17.5 0.0 copy-done.1
  17.5 0.1 broadcast_multiply_fusion
  17.6 0.1 broadcast_bitcast_fusion
  17.7 0.0 copy-done.3
  17.7 0.1 broadcast_in_dim.13
  17.8 0.1 eq.16
  17.8 0.0 copy-done
  17.8 5.6 %bulk.1 = (f32[1024,512]{1,0:T(8,128)S(1)}, f32[96,512]{1,0:T(8,128)S(1)}, f32[96,512]{1,0:T(8,128)S(1)}) custom-call(f32[1024,512]{1,0:T(8,128)} %bitcast.12, f32[96,512]{1,0:T(8,128)S(1)} %get-tuple-element.15.after_ref, bf16[512,512]{1,0:T(8,128)(2,1)S(1)} %copy-done), custom_call_target="tpu_custom_call" | custom-call | flops 40000000 | bytes 4194304 | tf_op jit(solution)/shard_map/bulk/pallas_call | solution.py:327
  23.4 0.0 collective-permute-done.got_l_ref
  23.4 0.0 collective-permute-done.1.got_r_ref
  23.5 0.3 plane.1
  23.7 4.0 %collective-permute-start.2 = (f32[96,512]{1,0:T(8,128)S(1)}, f32[96,512]{1,0:T(8,128)S(1)}, u32[]{:S(2)}, u32[]{:S(2)}) collective-permute-start(f32[96,512]{1,0:T(8,128)S(1)} %get-tuple-element.20), channel_id=1, source_target_pairs={{0,1},{1,2},{2,3},{3,4},{4,5},{5,6},{6,7},{7,8},{8,9},{9,10},{10,1... | collective-permute-start | bytes 589832 | tf_op jit(solution)/shard_map/ppermute | solution.py:284
  27.7 1.9 %collective-permute-start.3 = (f32[96,512]{1,0:T(8,128)S(1)}, f32[96,512]{1,0:T(8,128)S(1)}, u32[]{:S(2)}, u32[]{:S(2)}) collective-permute-start(f32[96,512]{1,0:T(8,128)S(1)} %get-tuple-element.21), channel_id=1, source_target_pairs={{1,0},{2,1},{3,2},{4,3},{5,4},{6,5},{7,6},{8,7},{9,8},{10,9},{11,1... | collective-permute-start | bytes 589832 | tf_op jit(solution)/shard_map/ppermute | solution.py:284
  29.6 0.1 fusion.hot_ref
  29.7 3.6 %rows.1 = (f32[32,32,512]{2,1,0:T(8,128)}, f32[512,512]{1,0:T(8,128)S(1)}, f32[4,8,512]{2,1,0:T(8,128)S(1)}) custom-call(f32[1024,512]{1,0:T(8,128)S(1)} %get-tuple-element.17.w_ref, f32[384,512]{1,0:T(8,128)S(1)} %get-tuple-element.22.fixed_ref, f32[4,512]{1,0:T(4,128)S(1)} %bitcast.9), custom_call_target="tpu_custom_call" | custom-call | flops 40000000 | bytes 4194304 | tf_op jit(solution)/shard_map/rows/pallas_call | solution.py:348
  33.3 0.0 collective-permute-done.2.got_l_ref
  33.3 1.7 %collective-permute-done.3.got_r_ref = f32[96,512]{1,0:T(8,128)S(1)} collective-permute-done((f32[96,512]{1,0:T(8,128)S(1)}, f32[96,512]{1,0:T(8,128)S(1)}, u32[]{:S(2)}, u32[]{:S(2)}) %collective-permute-start.3) | collective-permute-done | bytes 196640 | tf_op jit(solution)/shard_map/ppermute | solution.py:284
  35.0 1.6 %final.1 = (f32[32,32,512]{2,1,0:T(8,128)}, f32[16,4,128]{2,1,0:T(4,128)S(1)}) custom-call(f32[96,512]{1,0:T(8,128)S(1)} %collective-permute-done.2.got_l_ref, f32[96,512]{1,0:T(8,128)S(1)} %collective-permute-done.3.got_r_ref, f32[512,512]{1,0:T(8,128)S(1)} %get-tuple-element.23.edge_ref, ...), custom_call_target="tpu_custom_call", output_to_operand_aliasing={{0}: (6, {})} | custom-call | tf_op jit(solution)/shard_map/final/pallas_call | solution.py:366
  36.6 12.2 %all_to_all.10 = f32[16,4,128]{2,1,0:T(4,128)S(1)} all-to-all(f32[16,4,128]{2,1,0:T(4,128)S(1)} %get-tuple-element.27), channel_id=1, replica_groups=mesh['row'=16,'col'=32] {'row'}, dimensions={0} | all-to-all | bytes 65536 | tf_op jit(solution)/shard_map/all_to_all | solution.py:367
  48.9 23.4 %all_to_all.11 = f32[32,4,128]{2,1,0:T(4,128)S(1)} all-to-all(f32[32,4,128]{2,1,0:T(4,128)S(1)} %broadcast_in_dim.14), channel_id=1, replica_groups=mesh['row'=16,'col'=32] {'col'}, dimensions={0} | all-to-all | bytes 131072 | tf_op jit(solution)/shard_map/all_to_all | solution.py:368
  72.4 0.6 slice_bitcast_fusion
  (5 shorter events, 0.1 us)
Async XLA Ops:
  0.6 16.9 %copy-start.1 = (f32[4]{0:T(128)S(1)}, f32[4]{0:T(128)}, u32[]{:S(2)}) copy-start(f32[4]{0:T(128)} %constant.8.clone) | copy-start | bytes 52
  0.6 17.2 %copy-start = (bf16[512,512]{1,0:T(8,128)(2,1)S(1)}, bf16[512,512]{1,0:T(8,128)(2,1)}, u32[]{:S(2)}) copy-start(bf16[512,512]{1,0:T(8,128)(2,1)} %constant.9.clone.table_ref) | copy-start | bytes 1572868
  0.7 16.8 %copy-start.2 = (s32[1,1,2]{2,1,0:T(1,128)S(1)}, s32[1,1,2]{2,1,0:T(1,128)}, u32[]{:S(2)}) copy-start(s32[1,1,2]{2,1,0:T(1,128)} %param.6) | copy-start | bytes 28
  0.7 17.0 %copy-start.3 = (s32[1,1,2]{2,1,0:T(1,128)S(1)}, s32[1,1,2]{2,1,0:T(1,128)}, u32[]{:S(2)}) copy-start(s32[1,1,2]{2,1,0:T(1,128)} %param.7) | copy-start | bytes 28
  3.1 20.4 %collective-permute-start = (f32[96,512]{1,0:T(8,128)S(1)}, f32[96,512]{1,0:T(8,128)S(1)}, u32[]{:S(2)}, u32[]{:S(2)}) collective-permute-start(f32[96,512]{1,0:T(8,128)S(1)} %get-tuple-element.15.after_ref), channel_id=1, source_target_pairs={{0,32},{32,64},{64,96},{96,128},{128,160},{160,192},{192,224},{224... | collective-permute-start | bytes 589832 | tf_op jit(solution)/shard_map/ppermute | solution.py:284
  7.1 16.3 %collective-permute-start.1 = (f32[96,512]{1,0:T(8,128)S(1)}, f32[96,512]{1,0:T(8,128)S(1)}, u32[]{:S(2)}, u32[]{:S(2)}) collective-permute-start(f32[96,512]{1,0:T(8,128)S(1)} %get-tuple-element.16), channel_id=1, source_target_pairs={{32,0},{64,32},{96,64},{128,96},{160,128},{192,160},{224,192},{256... | collective-permute-start | bytes 589832 | tf_op jit(solution)/shard_map/ppermute | solution.py:284
  23.7 9.6 %collective-permute-start.2 = (f32[96,512]{1,0:T(8,128)S(1)}, f32[96,512]{1,0:T(8,128)S(1)}, u32[]{:S(2)}, u32[]{:S(2)}) collective-permute-start(f32[96,512]{1,0:T(8,128)S(1)} %get-tuple-element.20), channel_id=1, source_target_pairs={{0,1},{1,2},{2,3},{3,4},{4,5},{5,6},{6,7},{7,8},{8,9},{9,10},{10,1... | collective-permute-start | bytes 589832 | tf_op jit(solution)/shard_map/ppermute | solution.py:284
  27.7 7.3 %collective-permute-start.3 = (f32[96,512]{1,0:T(8,128)S(1)}, f32[96,512]{1,0:T(8,128)S(1)}, u32[]{:S(2)}, u32[]{:S(2)}) collective-permute-start(f32[96,512]{1,0:T(8,128)S(1)} %get-tuple-element.21), channel_id=1, source_target_pairs={{1,0},{2,1},{3,2},{4,3},{5,4},{6,5},{7,6},{8,7},{9,8},{10,9},{11,1... | collective-permute-start | bytes 589832 | tf_op jit(solution)/shard_map/ppermute | solution.py:284

commit v3 on v2

--- a/solution.py
+++ b/solution.py
@@ -6,9 +6,14 @@
 from jax import lax
 from jax.experimental import pallas as pl
 from jax.experimental.pallas import tpu as pltpu
+from jax.sharding import Mesh
 from jax.sharding import PartitionSpec as P
 
 GROUPS = 16
+ROW = ("z", "y_lo")
+COL = ("y_hi", "x", "core")
+FIRST = ("y_hi", "y_lo", "core")
+SECOND = ("z", "x")
 LEVELS = (0.25, 0.5, 1.0, 2.0)
 A, B, C, G = 0.5625, 0.0625, 0.28125, 0.03125
 F32 = jnp.float32
@@ -93,16 +98,18 @@
         right_ref[pl.ds(k * ny, ny), :] = lane_lift(v)
 
 
-def row_partials(nx, ny, w_ref, x, slot, right_ref, left_ref):
+def row_partials(nx, ny, w_ref, x, slot, inner_ref, outer_ref):
+    even = lax.axis_index("core") == 0
     head = w_ref[pl.ds(pl.multiple_of(x * ny, 8), 8), :]
     tail = w_ref[pl.ds(pl.multiple_of(x * ny + ny - 8, 8), 8), :]
-    for k, v in enumerate(to_right(lambda i: tail[8 - i : 9 - i, :])):
-        right_ref[pl.ds(k * nx + slot, 1), :] = v
-    for k, v in enumerate(to_left(lambda i: head[i : i + 1, :])):
-        left_ref[pl.ds(k * nx + slot, 1), :] = v
-
-
-def bulk_kernel(nx, ny, p_ref, after_ref, table_ref, w_ref, right_ref, left_ref, raw, sems):
+    right = to_right(lambda i: tail[8 - i : 9 - i, :])
+    left = to_left(lambda i: head[i : i + 1, :])
+    for k, (r, l) in enumerate(zip(right, left)):
+        inner_ref[pl.ds(k * nx + slot, 1), :] = jnp.where(even, r, l)
+        outer_ref[pl.ds(k * nx + slot, 1), :] = jnp.where(even, l, r)
+
+
+def bulk_kernel(nx, ny, p_ref, after_ref, table_ref, w_ref, inner_ref, outer_ref, raw, sems):
     del after_ref
     chunks = 4
     size = nx * ny // chunks
@@ -139,13 +146,13 @@
     lax.fori_loop(0, ny // 8, column, 0)
 
     def partial(x, _):
-        row_partials(nx, ny, w_ref, x, x, right_ref, left_ref)
+        row_partials(nx, ny, w_ref, x, x, inner_ref, outer_ref)
         return 0
 
     lax.fori_loop(0, nx, partial, 0, unroll=4)
 
 
-def plane_kernel(nx, ny, got_l_ref, got_r_ref, w_ref, right_in, left_in, fixed_ref, right_ref, left_ref):
+def plane_kernel(nx, ny, got_l_ref, got_r_ref, w_ref, inner_in, outer_in, fixed_ref, inner_ref, outer_ref):
     def fix(t, _):
         rows = lambda x: pl.ds(pl.multiple_of(x * ny + t * 8, 8), 8)
         lines = [got_l_ref[rows(k), :] for k in range(3)]
@@ -159,12 +166,12 @@
         return 0
 
     lax.fori_loop(0, ny // 8, fix, 0)
-    right_ref[...] = right_in[...]
-    left_ref[...] = left_in[...]
+    inner_ref[...] = inner_in[...]
+    outer_ref[...] = outer_in[...]
     for x in FROM_LEFT:
-        row_partials(nx, ny, fixed_ref, x, x, right_ref, left_ref)
+        row_partials(nx, ny, fixed_ref, x, x, inner_ref, outer_ref)
     for back in FROM_RIGHT:
-        row_partials(nx, ny, fixed_ref, 12 - back, nx - back, right_ref, left_ref)
+        row_partials(nx, ny, fixed_ref, 12 - back, nx - back, inner_ref, outer_ref)
 
 
 def excess(acc, v, even_plane, limits):
@@ -220,7 +227,7 @@
         copy.wait()
 
 
-def final_kernel(nx, ny, scale, got_l_ref, got_r_ref, edge_ref, acc_in, lim_ref, hot_ref, out_in, out_ref, mass_ref, head, tail, acc_ref, sems):
+def final_kernel(nx, ny, scale, outer_ref, inner_ref, edge_ref, acc_in, lim_ref, hot_ref, out_in, out_ref, mass_ref, head, tail, acc_ref, sems):
     del out_in
     size = edge_ref.shape[1]
     row = lax.broadcasted_iota(jnp.int32, (8, size), 0)
@@ -235,14 +242,19 @@
     from_l = [weights(FROM_LEFT, lambda i: i, k) for k in range(3)]
     from_r = [weights(FROM_RIGHT, lambda i: 8 - i, k) for k in range(3)]
     acc_ref[...] = acc_in[...]
+    even = lax.axis_index("core") == 0
 
     def tiles(x, even_plane):
         limits = [jnp.broadcast_to(lim_ref[l : l + 1, :], (8, size)) for l in range(4)]
         acc = [acc_ref[l] for l in range(4)]
-        for got, table, dest, at in ((got_l_ref, from_l, head, 0), (got_r_ref, from_r, tail, 8)):
+        inner = [inner_ref[pl.ds(k * nx + x, 1), :] for k in range(3)]
+        outer = [outer_ref[pl.ds(k * nx + x, 1), :] for k in range(3)]
+        left = [jnp.where(even, o, i) for i, o in zip(inner, outer)]
+        right = [jnp.where(even, i, o) for i, o in zip(inner, outer)]
+        for got, table, dest, at in ((left, from_l, head, 0), (right, from_r, tail, 8)):
             v = edge_ref[pl.ds(pl.multiple_of(x * 16 + at, 8), 8), :]
             for k in range(3):
-                v = v + table[k] * got[pl.ds(k * nx + x, 1), :]
+                v = v + table[k] * got[k]
             dest[x] = v
             acc = excess(acc, v, even_plane, limits)
         for l in range(4):
@@ -270,10 +282,9 @@
         for l in range(4):
             lines.append(jnp.sum(acc_ref[l, :, c * width : (c + 1) * width], axis=0, keepdims=True))
     sums = jnp.sum(jnp.concatenate(lines, axis=0), axis=1, keepdims=True)
-    sums = (sums * scale) * hot_ref[...]
-    both = sums[0:4, :] + sums[4:8, :]
+    line = jnp.sum((sums * scale) * hot_ref[...], axis=0, keepdims=True)
     for i in range(mass_ref.shape[0]):
-        mass_ref[i] = both
+        mass_ref[i] = line
     for copy in copies:
         copy.wait()
 
@@ -282,6 +293,11 @@
     n = lax.axis_size(axis)
     up = [(i, (i + 1) % n) for i in range(n)]
     return lax.ppermute(value_up, axis, up), lax.ppermute(value_down, axis, [(j, i) for i, j in up])
+
+
+def pair_swaps(n):
+    inner = [(i, i ^ 1) for i in range(n)]
+    return inner, [((i + 1) % n, (j + 1) % n) for i, j in inner]
 
 
 def near(*values):
@@ -302,7 +318,9 @@
     blocks_z = cut_exponent.shape[2]
     scales = jnp.exp2(-cut_exponent[0, 0].astype(F32))
     limits = jnp.repeat(jnp.array(LEVELS, F32)[:, None] * scales[None, :], size // blocks_z, axis=1)
-    hot = (jnp.arange(128, dtype=jnp.int32)[None, :] == jnp.repeat(group_map[0, 0], 4)[:, None]).astype(F32)
+    level = jnp.tile(jnp.arange(4, dtype=jnp.int32), blocks_z)
+    place = GROUPS * level + jnp.repeat(group_map[0, 0], 4)
+    hot = (jnp.arange(128, dtype=jnp.int32)[None, :] == place[:, None]).astype(F32)
     edge = pl.pallas_call(
         functools.partial(edge_kernel, nx, ny),
         out_shape=(in_vmem((3 * ny, size)), in_vmem((3 * ny, size))),
@@ -313,7 +331,7 @@
         name="edge",
     )
     right, left = edge(far(flat))
-    from_left, from_right = neighbours(right, left, "row")
+    from_left, from_right = neighbours(right, left, ROW)
     bulk = pl.pallas_call(
         functools.partial(bulk_kernel, nx, ny),
         out_shape=(in_vmem((nx * ny, size)), in_vmem((3 * nx, size)), in_vmem((3 * nx, size))),
@@ -324,7 +342,7 @@
         compiler_params=PARAMS,
         name="bulk",
     )
-    work, right, left = bulk(far(flat), *near(right, jnp.asarray(lane_table(size))))
+    work, inner, outer = bulk(far(flat), *near(right, jnp.asarray(lane_table(size))))
     plane = pl.pallas_call(
         functools.partial(plane_kernel, nx, ny),
         out_shape=(in_vmem((12 * ny, size)), in_vmem((3 * nx, size)), in_vmem((3 * nx, size))),
@@ -333,8 +351,10 @@
         compiler_params=PARAMS,
         name="plane",
     )
-    fixed, right, left = plane(*near(from_left, from_right, work, right, left))
-    from_left, from_right = neighbours(right, left, "col")
+    fixed, inner, outer = plane(*near(from_left, from_right, work, inner, outer))
+    swap_inner, swap_outer = pair_swaps(lax.axis_size(COL))
+    inner = lax.ppermute(inner, COL, swap_inner)
+    outer = lax.ppermute(outer, COL, swap_outer)
     rows = pl.pallas_call(
         functools.partial(rows_kernel, nx, ny),
         out_shape=(jax.ShapeDtypeStruct((nx, ny, size), F32), in_vmem((nx * 16, size)), in_vmem((4, 8, size))),
@@ -346,11 +366,11 @@
         name="rows",
     )
     coeffs, edges, acc = rows(*near(work, fixed, limits))
-    n_row, n_col = lax.axis_size("row"), lax.axis_size("col")
+    n_first, n_second = lax.axis_size(FIRST), lax.axis_size(SECOND)
     scale = 1.0 / (nx * ny * (size // blocks_z))
     final = pl.pallas_call(
         functools.partial(final_kernel, nx, ny, scale),
-        out_shape=(jax.ShapeDtypeStruct((nx, ny, size), F32), in_vmem((n_row, 4, 128))),
+        out_shape=(jax.ShapeDtypeStruct((nx, ny, size), F32), in_vmem((n_first, 1, 128))),
         in_specs=[VMEM] * 6 + [ANY],
         out_specs=(ANY, VMEM),
         input_output_aliases={6: 0},
@@ -363,12 +383,21 @@
         compiler_params=PARAMS,
         name="final",
     )
-    coeffs, mass = final(*near(from_left, from_right, edges, acc, limits, hot), coeffs)
-    mass = lax.all_to_all(mass, "row", 0, 0).sum(0)
-    mass = lax.all_to_all(jnp.broadcast_to(mass, (n_col, 4, 128)), "col", 0, 0).sum(0)
-    return coeffs, mass[:, :GROUPS].T
+    coeffs, mass = final(*near(outer, inner, edges, acc, limits, hot), coeffs)
+    mass = lax.all_to_all(mass, FIRST, 0, 0).sum(0)
+    mass = lax.all_to_all(jnp.broadcast_to(mass, (n_second, 1, 128)), SECOND, 0, 0).sum(0)
+    return coeffs, mass[0, : 4 * GROUPS].reshape(4, GROUPS).T
 
 
 def solution(mesh):
-    split = P("row", "col", None)
-    return jax.shard_map(shards, mesh=mesh, in_specs=(split, split, split), out_specs=(split, P()), check_vma=False)
+    rows, cols = mesh.devices.shape
+    z, y_hi = rows // 2, max(cols // 8, 1)
+    devices = mesh.devices.reshape(z, 2, y_hi, cols // 2 // y_hi, 2)
+    split = P(ROW, COL, None)
+    return jax.shard_map(
+        shards,
+        mesh=Mesh(devices, ROW + COL),
+        in_specs=(split, split, split),
+        out_specs=(split, P()),
+        check_vma=False,
+    )

time: 73.3 us -> 67.4 us (0.920)
  blocking collectives: 35.6 us -> 27.4 us
  starting transfers between devices: 20.3 us -> 23.9 us
  waiting for transfers between devices: 1.69 us -> 0.01 us
    ppermute x0 -> x2, starting transfers between devices: none -> 9.48 us  [the longest x1 5.52 us: shards(): inner = lax.ppermute(inner, COL, swap_inner)]
    all_to_all x2, blocking collectives: 35.6 us -> 27.4 us  [the longest x1 15.3 us: shards(): lax.all_to_all(jnp.broadcast_to(mass, (n_second, 1, 128)), SECOND, 0, 0)]
    ppermute x2 -> x1, starting transfers between devices: 7.98 us -> 4.02 us  [neighbours(): lax.ppermute(value_up, axis, up)]
    ppermute x2 -> x1, starting transfers between devices: 12.3 us -> 10.4 us  [neighbours(): lax.ppermute(value_down, axis, [(j, i) for i, j in up])]
    ppermute x2 -> x1, waiting for transfers between devices: 1.68 us -> 0.01 us  [neighbours(): lax.ppermute(value_down, axis, [(j, i) for i, j in up])]
  transfers between devices with their start and end apart: 4 -> 4, of which waited for: 1 -> 0; matrix products, arithmetic and copies ran while one was open for 1% -> 1% of each run, Pallas kernels for 13% -> 14%
where the time goes in v3:
time: 67.4 us; the launch traced here: 67 us
  blocking collectives  27.4 us (41%)
  starting transfers between devices  23.9 us (35%)
  Pallas kernels  13.8 us (20%)
  local copies, waits for them, and re-layouts  0.89 us (1%)
  between operations  0.79 us (1%)
    all_to_all x1, blocking collectives, shards(): lax.all_to_all(jnp.broadcast_to(mass, (n_second, 1, 128)), SECOND, 0, 0)  15.3 us
    all_to_all x1, blocking collectives, shards(): mass = lax.all_to_all(mass, FIRST, 0, 0).sum(0)  12 us
    ppermute x1, starting transfers between devices, neighbours(): lax.ppermute(value_down, axis, [(j, i) for i, j in up])  10.4 us
    pallas_call x1, Pallas kernels, shards(): bulk(far(flat), *near(right, jnp.asarray(lane_table(size))))  5.79 us
    ppermute x1, starting transfers between devices, shards(): inner = lax.ppermute(inner, COL, swap_inner)  5.52 us
    ppermute x1, starting transfers between devices, neighbours(): lax.ppermute(value_up, axis, up)  4.02 us
    ppermute x1, starting transfers between devices, shards(): outer = lax.ppermute(outer, COL, swap_outer)  3.96 us
    pallas_call x1, Pallas kernels, shards(): coeffs, edges, acc = rows(*near(work, fixed, limits))  3.59 us
  transfers between devices with their start and end apart: 4, of which 0 were waited for; matrix products, arithmetic and copies ran while one was open for 1% of the time, Pallas kernels for 14%

profile of v3, /device:TPU:1, one launch (start us, length us, event | category | flops | bytes accessed | tf_op | source)
XLA Modules:
  0.0 67.0 jit_solution(13469051372087019608)
XLA Ops:
  0.6 0.0 copy-start.1
  0.6 0.0 copy-start
  0.7 0.0 copy-start.2
  0.7 0.0 copy-start.3
  0.7 2.4 %edge.1 = (f32[96,512]{1,0:T(8,128)S(1)}, f32[96,512]{1,0:T(8,128)S(1)}) custom-call(f32[1024,512]{1,0:T(8,128)} %bitcast.12), custom_call_target="tpu_custom_call" | custom-call | tf_op jit(solution)/shard_map/edge/pallas_call | solution.py:333
  3.1 4.0 %collective-permute-start = (f32[96,512]{1,0:T(8,128)S(1)}, f32[96,512]{1,0:T(8,128)S(1)}, u32[]{:S(2)}, u32[]{:S(2)}) collective-permute-start(f32[96,512]{1,0:T(8,128)S(1)} %get-tuple-element.15.after_ref), channel_id=1, source_target_pairs={{0,32},{32,64},{64,96},{96,128},{128,160},{160,192},{192,224},{224... | collective-permute-start | bytes 589832 | tf_op jit(solution)/shard_map/ppermute | solution.py:295
  7.1 10.4 %collective-permute-start.1 = (f32[96,512]{1,0:T(8,128)S(1)}, f32[96,512]{1,0:T(8,128)S(1)}, u32[]{:S(2)}, u32[]{:S(2)}) collective-permute-start(f32[96,512]{1,0:T(8,128)S(1)} %get-tuple-element.16), channel_id=1, source_target_pairs={{32,0},{64,32},{96,64},{128,96},{160,128},{192,160},{224,192},{256... | collective-permute-start | bytes 589832 | tf_op jit(solution)/shard_map/ppermute | solution.py:295
  17.5 0.0 copy-done.2
  17.5 0.0 copy-done.1
  17.5 0.1 broadcast_multiply_fusion
  17.6 0.1 broadcast_bitcast_fusion
  17.7 0.0 copy-done.3
  17.7 0.1 multiply_add_fusion
  17.8 0.1 add.11
  17.8 0.0 copy-done
  17.8 5.8 %bulk.1 = (f32[1024,512]{1,0:T(8,128)S(1)}, f32[96,512]{1,0:T(8,128)S(1)}, f32[96,512]{1,0:T(8,128)S(1)}) custom-call(f32[1024,512]{1,0:T(8,128)} %bitcast.13, f32[96,512]{1,0:T(8,128)S(1)} %get-tuple-element.15.after_ref, bf16[512,512]{1,0:T(8,128)(2,1)S(1)} %copy-done), custom_call_target="tpu_custom_call" | custom-call | flops 40000000 | bytes 4194304 | tf_op jit(solution)/shard_map/bulk/pallas_call | solution.py:345
  23.6 0.0 collective-permute-done.got_l_ref
  23.7 0.0 collective-permute-done.1.got_r_ref
  23.7 0.3 plane.1
  24.0 4.0 %collective-permute-start.2 = (f32[96,512]{1,0:T(8,128)S(1)}, f32[96,512]{1,0:T(8,128)S(1)}, u32[]{:S(2)}, u32[]{:S(2)}) collective-permute-start(f32[96,512]{1,0:T(8,128)S(1)} %get-tuple-element.20), channel_id=1, source_target_pairs={{1,2},{2,1},{3,4},{4,3},{5,6},{6,5},{7,8},{8,7},{9,10},{10,9},{11,... | collective-permute-start | bytes 589832 | tf_op jit(solution)/shard_map/ppermute | solution.py:357
  28.0 5.5 %collective-permute-start.3 = (f32[96,512]{1,0:T(8,128)S(1)}, f32[96,512]{1,0:T(8,128)S(1)}, u32[]{:S(2)}, u32[]{:S(2)}) collective-permute-start(f32[96,512]{1,0:T(8,128)S(1)} %get-tuple-element.21), channel_id=1, source_target_pairs={{0,1},{1,0},{2,3},{3,2},{4,5},{5,4},{6,7},{7,6},{8,9},{9,8},{10,11... | collective-permute-start | bytes 589832 | tf_op jit(solution)/shard_map/ppermute | solution.py:356
  33.5 0.1 fusion.hot_ref
  33.6 3.6 %rows.1 = (f32[32,32,512]{2,1,0:T(8,128)}, f32[512,512]{1,0:T(8,128)S(1)}, f32[4,8,512]{2,1,0:T(8,128)S(1)}) custom-call(f32[1024,512]{1,0:T(8,128)S(1)} %get-tuple-element.17.w_ref, f32[384,512]{1,0:T(8,128)S(1)} %get-tuple-element.22.fixed_ref, f32[4,512]{1,0:T(4,128)S(1)} %bitcast.10), custom_call_target="tpu_custom_call" | custom-call | flops 40000000 | bytes 4194304 | tf_op jit(solution)/shard_map/rows/pallas_call | solution.py:368
  37.2 0.0 collective-permute-done.2.outer_ref
  37.2 0.0 collective-permute-done.3.inner_ref
  37.2 1.7 %final.1 = (f32[32,32,512]{2,1,0:T(8,128)}, f32[16,1,128]{2,1,0:T(1,128)S(1)}) custom-call(f32[96,512]{1,0:T(8,128)S(1)} %collective-permute-done.2.outer_ref, f32[96,512]{1,0:T(8,128)S(1)} %collective-permute-done.3.inner_ref, f32[512,512]{1,0:T(8,128)S(1)} %get-tuple-element.23.edge_ref, ...), custom_call_target="tpu_custom_call", output_to_operand_aliasing={{0}: (6, {})} | custom-call | tf_op jit(solution)/shard_map/final/pallas_call | solution.py:386
  38.9 12.0 %all_to_all.10 = f32[16,1,128]{2,1,0:T(1,128)S(1)} all-to-all(f32[16,1,128]{2,1,0:T(1,128)S(1)} %get-tuple-element.27), channel_id=1, replica_groups=mesh['z'=8,'y_lo'=2,'y_hi'=4,'x'=4,'core'=2] {'y_hi','y_lo','core'}, dimensions={0} | all-to-all | bytes 16384 | tf_op jit(solution)/shard_map/all_to_all | solution.py:387
  51.0 15.3 %all_to_all.11 = f32[32,1,128]{2,1,0:T(1,128)S(1)} all-to-all(f32[32,1,128]{2,1,0:T(1,128)S(1)} %broadcast_in_dim.15), channel_id=1, replica_groups=mesh['z'=8,'y_lo'=2,'y_hi'=4,'x'=4,'core'=2] {'z','x'}, dimensions={0} | all-to-all | bytes 32768 | tf_op jit(solution)/shard_map/all_to_all | solution.py:388
  66.4 0.7 reshape_squeeze.3
  (6 shorter events, 0.1 us)
Async XLA Ops:
  0.6 16.9 %copy-start.1 = (f32[4]{0:T(128)S(1)}, f32[4]{0:T(128)}, u32[]{:S(2)}) copy-start(f32[4]{0:T(128)} %constant.10.clone) | copy-start | bytes 52
  0.6 17.2 %copy-start = (bf16[512,512]{1,0:T(8,128)(2,1)S(1)}, bf16[512,512]{1,0:T(8,128)(2,1)}, u32[]{:S(2)}) copy-start(bf16[512,512]{1,0:T(8,128)(2,1)} %constant.11.clone.table_ref) | copy-start | bytes 1572868
  0.7 16.8 %copy-start.2 = (s32[1,1,2]{2,1,0:T(1,128)S(1)}, s32[1,1,2]{2,1,0:T(1,128)}, u32[]{:S(2)}) copy-start(s32[1,1,2]{2,1,0:T(1,128)} %param.6) | copy-start | bytes 28
  0.7 17.0 %copy-start.3 = (s32[1,1,2]{2,1,0:T(1,128)S(1)}, s32[1,1,2]{2,1,0:T(1,128)}, u32[]{:S(2)}) copy-start(s32[1,1,2]{2,1,0:T(1,128)} %param.7) | copy-start | bytes 28
  3.1 20.6 %collective-permute-start = (f32[96,512]{1,0:T(8,128)S(1)}, f32[96,512]{1,0:T(8,128)S(1)}, u32[]{:S(2)}, u32[]{:S(2)}) collective-permute-start(f32[96,512]{1,0:T(8,128)S(1)} %get-tuple-element.15.after_ref), channel_id=1, source_target_pairs={{0,32},{32,64},{64,96},{96,128},{128,160},{160,192},{192,224},{224... | collective-permute-start | bytes 589832 | tf_op jit(solution)/shard_map/ppermute | solution.py:295
  7.1 16.6 %collective-permute-start.1 = (f32[96,512]{1,0:T(8,128)S(1)}, f32[96,512]{1,0:T(8,128)S(1)}, u32[]{:S(2)}, u32[]{:S(2)}) collective-permute-start(f32[96,512]{1,0:T(8,128)S(1)} %get-tuple-element.16), channel_id=1, source_target_pairs={{32,0},{64,32},{96,64},{128,96},{160,128},{192,160},{224,192},{256... | collective-permute-start | bytes 589832 | tf_op jit(solution)/shard_map/ppermute | solution.py:295
  24.0 13.2 %collective-permute-start.2 = (f32[96,512]{1,0:T(8,128)S(1)}, f32[96,512]{1,0:T(8,128)S(1)}, u32[]{:S(2)}, u32[]{:S(2)}) collective-permute-start(f32[96,512]{1,0:T(8,128)S(1)} %get-tuple-element.20), channel_id=1, source_target_pairs={{1,2},{2,1},{3,4},{4,3},{5,6},{6,5},{7,8},{8,7},{9,10},{10,9},{11,... | collective-permute-start | bytes 589832 | tf_op jit(solution)/shard_map/ppermute | solution.py:357
  28.0 9.2 %collective-permute-start.3 = (f32[96,512]{1,0:T(8,128)S(1)}, f32[96,512]{1,0:T(8,128)S(1)}, u32[]{:S(2)}, u32[]{:S(2)}) collective-permute-start(f32[96,512]{1,0:T(8,128)S(1)} %get-tuple-element.21), channel_id=1, source_target_pairs={{0,1},{1,0},{2,3},{3,2},{4,5},{5,4},{6,7},{7,6},{8,9},{9,8},{10,11... | collective-permute-start | bytes 589832 | tf_op jit(solution)/shard_map/ppermute | solution.py:356

commit v4 on v3

--- a/solution.py
+++ b/solution.py
@@ -92,21 +92,28 @@
     hi.start()
     lo.wait()
     for k, v in enumerate(to_left(lambda i: first[pl.ds(i * ny, ny), :])):
-        left_ref[pl.ds(k * ny, ny), :] = lane_lift(v)
+        left_ref[pl.ds(k * ny, ny), :] = v
     hi.wait()
     for k, v in enumerate(to_right(lambda i: last[pl.ds((6 - i) * ny, ny), :])):
-        right_ref[pl.ds(k * ny, ny), :] = lane_lift(v)
-
-
-def row_partials(nx, ny, w_ref, x, slot, inner_ref, outer_ref):
-    even = lax.axis_index("core") == 0
-    head = w_ref[pl.ds(pl.multiple_of(x * ny, 8), 8), :]
-    tail = w_ref[pl.ds(pl.multiple_of(x * ny + ny - 8, 8), 8), :]
-    right = to_right(lambda i: tail[8 - i : 9 - i, :])
-    left = to_left(lambda i: head[i : i + 1, :])
-    for k, (r, l) in enumerate(zip(right, left)):
-        inner_ref[pl.ds(k * nx + slot, 1), :] = jnp.where(even, r, l)
-        outer_ref[pl.ds(k * nx + slot, 1), :] = jnp.where(even, l, r)
+        right_ref[pl.ds(k * ny, ny), :] = v
+
+
+def boundary_lines(head, tail):
+    return (*to_right(lambda i: tail[8 - i : 9 - i, :]), *to_left(lambda i: head[i : i + 1, :]))
+
+
+def edge_weights(size):
+    row = lax.broadcasted_iota(jnp.int32, (8, size), 0)
+
+    def weights(table, place, k):
+        total = jnp.zeros((8, size), F32)
+        for line, coefs in table.items():
+            if coefs[k] != 0.0:
+                total = jnp.where(row == place(line), coefs[k], total)
+        return total
+
+    head = [weights(FROM_LEFT, lambda i: i, k) for k in range(3)]
+    return head, [weights(FROM_RIGHT, lambda i: 8 - i, k) for k in range(3)]
 
 
 def bulk_kernel(nx, ny, p_ref, after_ref, table_ref, w_ref, inner_ref, outer_ref, raw, sems):
@@ -145,33 +152,40 @@
 
     lax.fori_loop(0, ny // 8, column, 0)
 
+    even = lax.axis_index("core") == 0
+
     def partial(x, _):
-        row_partials(nx, ny, w_ref, x, x, inner_ref, outer_ref)
+        head = w_ref[pl.ds(pl.multiple_of(x * ny, 8), 8), :]
+        tail = w_ref[pl.ds(pl.multiple_of(x * ny + ny - 8, 8), 8), :]
+        lines = boundary_lines(head, tail)
+        for k, (right, left) in enumerate(zip(lines[:3], lines[3:])):
+            inner_ref[pl.ds(k * nx + x, 1), :] = jnp.where(even, right, left)
+            outer_ref[pl.ds(k * nx + x, 1), :] = jnp.where(even, left, right)
         return 0
 
     lax.fori_loop(0, nx, partial, 0, unroll=4)
 
 
-def plane_kernel(nx, ny, got_l_ref, got_r_ref, w_ref, inner_in, outer_in, fixed_ref, inner_ref, outer_ref):
-    def fix(t, _):
-        rows = lambda x: pl.ds(pl.multiple_of(x * ny + t * 8, 8), 8)
-        lines = [got_l_ref[rows(k), :] for k in range(3)]
-        for x in range(6):
-            v = w_ref[rows(x), :]
-            fixed_ref[rows(x), :] = v + combine(FROM_LEFT[x], lines) if x in FROM_LEFT else v
-        lines = [got_r_ref[rows(k), :] for k in range(3)]
-        for back in range(6, 0, -1):
-            v = w_ref[rows(nx - back), :]
-            fixed_ref[rows(12 - back), :] = v + combine(FROM_RIGHT[back], lines) if back in FROM_RIGHT else v
-        return 0
-
-    lax.fori_loop(0, ny // 8, fix, 0)
+def plane_kernel(nx, ny, got_l_ref, got_r_ref, table_ref, inner_in, outer_in, inner_ref, outer_ref, lines):
+    size = table_ref.shape[0]
+    even = lax.axis_index("core") == 0
+    lines[...] = jnp.zeros_like(lines)
+    for h in range(6):
+        got = (got_l_ref, got_r_ref)[h // 3]
+        at = h % 3 * ny
+        for m, line in enumerate(boundary_lines(got[at : at + 8, :], got[at + ny - 8 : at + ny, :])):
+            lines[6 * h + m : 6 * h + m + 1, :] = line
+    lines[...] = table_lift(lines[...], table_ref[...])
     inner_ref[...] = inner_in[...]
     outer_ref[...] = outer_in[...]
-    for x in FROM_LEFT:
-        row_partials(nx, ny, fixed_ref, x, x, inner_ref, outer_ref)
-    for back in FROM_RIGHT:
-        row_partials(nx, ny, fixed_ref, 12 - back, nx - back, inner_ref, outer_ref)
+    for first, at, weights in zip((0, 3), (0, nx - 8), edge_weights(size)):
+        for k in range(3):
+            row = lambda h, m: lines[6 * h + m : 6 * h + m + 1, :]
+            right = sum(weights[i] * row(first + i, k) for i in range(3))
+            left = sum(weights[i] * row(first + i, 3 + k) for i in range(3))
+            part = slice(k * nx + at, k * nx + at + 8)
+            inner_ref[part, :] = inner_ref[part, :] + jnp.where(even, right, left)
+            outer_ref[part, :] = outer_ref[part, :] + jnp.where(even, left, right)
 
 
 def excess(acc, v, even_plane, limits):
@@ -183,9 +197,39 @@
     return [a + jnp.maximum(m - lim, 0.0) for a, lim in zip(acc, limits)]
 
 
-def rows_kernel(nx, ny, w_ref, fixed_ref, lim_ref, out_ref, edge_ref, acc_ref, mid, sems):
+def rows_kernel(nx, ny, w_ref, got_l_ref, got_r_ref, table_ref, cut_ref, group_ref, out_ref, acc_ref, lim_ref, hot_ref, halo, fixed_ref):
     size = w_ref.shape[1]
+    blocks = cut_ref.shape[1]
+    lane = lax.broadcasted_iota(jnp.int32, (1, size), 1)
+    cut = jnp.zeros((1, size), jnp.int32)
+    place = lax.broadcasted_iota(jnp.int32, (8, 128), 0)
+    group = jnp.zeros((8, 128), jnp.int32)
+    for c in range(blocks):
+        cut = jnp.where(lane // (size // blocks) == c, cut_ref[:, c : c + 1], cut)
+        group = jnp.where(place // 4 == c, group_ref[:, c : c + 1], group)
+    scales = jnp.exp2(-cut.astype(F32))
+    for l, level in enumerate(LEVELS):
+        lim_ref[l : l + 1, :] = level * scales
+    hot = lax.broadcasted_iota(jnp.int32, (8, 128), 1) == GROUPS * (place % 4) + group
+    hot_ref[...] = jnp.where(hot, 1.0, 0.0)
     acc_ref[...] = jnp.zeros_like(acc_ref)
+
+    halo[pl.ds(0, 3 * ny), :] = table_lift(got_l_ref[...], table_ref[...])
+    halo[pl.ds(3 * ny, 3 * ny), :] = table_lift(got_r_ref[...], table_ref[...])
+
+    def fix(t, _):
+        rows = lambda x: pl.ds(pl.multiple_of(x * ny + t * 8, 8), 8)
+        lines = [halo[rows(k), :] for k in range(3)]
+        for x in range(6):
+            v = w_ref[rows(x), :]
+            fixed_ref[rows(x), :] = v + combine(FROM_LEFT[x], lines) if x in FROM_LEFT else v
+        lines = [halo[rows(3 + k), :] for k in range(3)]
+        for back in range(6, 0, -1):
+            v = w_ref[rows(nx - back), :]
+            fixed_ref[rows(12 - back), :] = v + combine(FROM_RIGHT[back], lines) if back in FROM_RIGHT else v
+        return 0
+
+    lax.fori_loop(0, ny // 8, fix, 0)
 
     def lift(src, at_plane):
         v = src[pl.ds(pl.multiple_of(at_plane * ny, 8), ny), :]
@@ -198,9 +242,7 @@
 
     def plane(src, at_plane, x, even_plane):
         v = lift(src, at_plane)
-        edge_ref[pl.ds(pl.multiple_of(x * 16, 8), 8), :] = v[0:8, :]
-        edge_ref[pl.ds(pl.multiple_of(x * 16 + 8, 8), 8), :] = v[ny - 8 : ny, :]
-        mid[x] = v[8 : ny - 8, :]
+        out_ref[pl.ds(pl.multiple_of(x * ny, 8), ny), :] = v
         limits = [jnp.broadcast_to(lim_ref[l : l + 1, :], (8, size)) for l in range(4)]
         acc = [acc_ref[l] for l in range(4)]
         for t in range(1, ny // 8 - 1):
@@ -208,11 +250,7 @@
         for l in range(4):
             acc_ref[l] = acc[l]
 
-    copies = []
-    middle = (nx - 12) // 2
-    for i, (src, start, x0, each) in enumerate(
-        ((fixed_ref, 0, 0, 6), (w_ref, 6, 6, middle), (w_ref, 6 + middle, 6 + middle, middle), (fixed_ref, 6, nx - 6, 6))
-    ):
+    for src, start, x0, each in ((fixed_ref, 0, 0, 6), (w_ref, 6, 6, nx - 12), (fixed_ref, 6, nx - 6, 6)):
 
         def pair(j, _):
             plane(src, start + 2 * j, x0 + 2 * j, True)
@@ -220,27 +258,11 @@
             return 0
 
         lax.fori_loop(0, each // 2, pair, 0)
-        part = pl.ds(x0, each)
-        copies.append(pltpu.make_async_copy(mid.at[part], out_ref.at[part, pl.ds(8, ny - 16), :], sems.at[i]))
-        copies[-1].start()
-    for copy in copies:
-        copy.wait()
-
-
-def final_kernel(nx, ny, scale, outer_ref, inner_ref, edge_ref, acc_in, lim_ref, hot_ref, out_in, out_ref, mass_ref, head, tail, acc_ref, sems):
-    del out_in
-    size = edge_ref.shape[1]
-    row = lax.broadcasted_iota(jnp.int32, (8, size), 0)
-
-    def weights(table, place, k):
-        total = jnp.zeros((8, size), F32)
-        for line, coefs in table.items():
-            if coefs[k] != 0.0:
-                total = jnp.where(row == place(line), coefs[k], total)
-        return total
-
-    from_l = [weights(FROM_LEFT, lambda i: i, k) for k in range(3)]
-    from_r = [weights(FROM_RIGHT, lambda i: 8 - i, k) for k in range(3)]
+
+
+def final_kernel(nx, ny, scale, outer_ref, inner_ref, acc_in, lim_ref, hot_ref, base_ref, out_ref, mass_ref, acc_ref):
+    size = base_ref.shape[1]
+    from_l, from_r = edge_weights(size)
     acc_ref[...] = acc_in[...]
     even = lax.axis_index("core") == 0
 
@@ -251,30 +273,22 @@
         outer = [outer_ref[pl.ds(k * nx + x, 1), :] for k in range(3)]
         left = [jnp.where(even, o, i) for i, o in zip(inner, outer)]
         right = [jnp.where(even, i, o) for i, o in zip(inner, outer)]
-        for got, table, dest, at in ((left, from_l, head, 0), (right, from_r, tail, 8)):
-            v = edge_ref[pl.ds(pl.multiple_of(x * 16 + at, 8), 8), :]
+        for got, table, at in ((left, from_l, 0), (right, from_r, ny - 8)):
+            part = pl.ds(pl.multiple_of(x * ny + at, 8), 8)
+            v = base_ref[part, :]
             for k in range(3):
                 v = v + table[k] * got[k]
-            dest[x] = v
+            out_ref[part, :] = v
             acc = excess(acc, v, even_plane, limits)
         for l in range(4):
             acc_ref[l] = acc[l]
 
-    parts = 4
-    each = nx // parts
-    copies = []
-    for i in range(parts):
-
-        def pair(j, _):
-            tiles(i * each + 2 * j, True)
-            tiles(i * each + 2 * j + 1, False)
-            return 0
-
-        lax.fori_loop(0, each // 2, pair, 0)
-        part = pl.ds(i * each, each)
-        for n, (src, at) in enumerate(((head, 0), (tail, ny - 8))):
-            copies.append(pltpu.make_async_copy(src.at[part], out_ref.at[part, pl.ds(at, 8), :], sems.at[2 * i + n]))
-            copies[-1].start()
+    def pair(j, _):
+        tiles(2 * j, True)
+        tiles(2 * j + 1, False)
+        return 0
+
+    lax.fori_loop(0, nx // 2, pair, 0, unroll=2)
     blocks = 2
     width = size // blocks
     lines = []
@@ -285,8 +299,6 @@
     line = jnp.sum((sums * scale) * hot_ref[...], axis=0, keepdims=True)
     for i in range(mass_ref.shape[0]):
         mass_ref[i] = line
-    for copy in copies:
-        copy.wait()
 
 
 def neighbours(value_up, value_down, axis):
@@ -316,11 +328,7 @@
     nx, ny, size = pressure.shape
     flat = pressure.reshape(nx * ny, size)
     blocks_z = cut_exponent.shape[2]
-    scales = jnp.exp2(-cut_exponent[0, 0].astype(F32))
-    limits = jnp.repeat(jnp.array(LEVELS, F32)[:, None] * scales[None, :], size // blocks_z, axis=1)
-    level = jnp.tile(jnp.arange(4, dtype=jnp.int32), blocks_z)
-    place = GROUPS * level + jnp.repeat(group_map[0, 0], 4)
-    hot = (jnp.arange(128, dtype=jnp.int32)[None, :] == place[:, None]).astype(F32)
+    table = jnp.asarray(lane_table(size))
     edge = pl.pallas_call(
         functools.partial(edge_kernel, nx, ny),
         out_shape=(in_vmem((3 * ny, size)), in_vmem((3 * ny, size))),
@@ -342,51 +350,49 @@
         compiler_params=PARAMS,
         name="bulk",
     )
-    work, inner, outer = bulk(far(flat), *near(right, jnp.asarray(lane_table(size))))
+    work, inner, outer = bulk(far(flat), *near(right, table))
     plane = pl.pallas_call(
         functools.partial(plane_kernel, nx, ny),
-        out_shape=(in_vmem((12 * ny, size)), in_vmem((3 * nx, size)), in_vmem((3 * nx, size))),
+        out_shape=(in_vmem((3 * nx, size)), in_vmem((3 * nx, size))),
         in_specs=[VMEM] * 5,
-        out_specs=(VMEM, VMEM, VMEM),
+        out_specs=(VMEM, VMEM),
+        scratch_shapes=[pltpu.VMEM((40, size), F32)],
         compiler_params=PARAMS,
         name="plane",
     )
-    fixed, inner, outer = plane(*near(from_left, from_right, work, inner, outer))
+    inner, outer = plane(*near(from_left, from_right, table, inner, outer))
     swap_inner, swap_outer = pair_swaps(lax.axis_size(COL))
     inner = lax.ppermute(inner, COL, swap_inner)
     outer = lax.ppermute(outer, COL, swap_outer)
     rows = pl.pallas_call(
         functools.partial(rows_kernel, nx, ny),
-        out_shape=(jax.ShapeDtypeStruct((nx, ny, size), F32), in_vmem((nx * 16, size)), in_vmem((4, 8, size))),
-        in_specs=[VMEM, VMEM, VMEM],
-        out_specs=(ANY, VMEM, VMEM),
-        scratch_shapes=[pltpu.VMEM((nx, ny - 16, size), F32), pltpu.SemaphoreType.DMA((4,))],
+        out_shape=(in_vmem((nx * ny, size)), in_vmem((4, 8, size)), in_vmem((4, size)), in_vmem((8, 128))),
+        in_specs=[VMEM] * 6,
+        out_specs=(VMEM,) * 4,
+        scratch_shapes=[pltpu.VMEM((6 * ny, size), F32), pltpu.VMEM((12 * ny, size), F32)],
         cost_estimate=cost(40_000_000),
         compiler_params=PARAMS,
         name="rows",
     )
-    coeffs, edges, acc = rows(*near(work, fixed, limits))
+    base, acc, limits, hot = rows(
+        *near(work, from_left, from_right, table, cut_exponent.reshape(1, blocks_z), group_map.reshape(1, blocks_z))
+    )
     n_first, n_second = lax.axis_size(FIRST), lax.axis_size(SECOND)
     scale = 1.0 / (nx * ny * (size // blocks_z))
     final = pl.pallas_call(
         functools.partial(final_kernel, nx, ny, scale),
-        out_shape=(jax.ShapeDtypeStruct((nx, ny, size), F32), in_vmem((n_first, 1, 128))),
-        in_specs=[VMEM] * 6 + [ANY],
-        out_specs=(ANY, VMEM),
-        input_output_aliases={6: 0},
-        scratch_shapes=[
-            pltpu.VMEM((nx, 8, size), F32),
-            pltpu.VMEM((nx, 8, size), F32),
-            pltpu.VMEM((4, 8, size), F32),
-            pltpu.SemaphoreType.DMA((8,)),
-        ],
+        out_shape=(in_vmem((nx * ny, size)), in_vmem((n_first, 1, 128))),
+        in_specs=[VMEM] * 6,
+        out_specs=(VMEM, VMEM),
+        input_output_aliases={5: 0},
+        scratch_shapes=[pltpu.VMEM((4, 8, size), F32)],
         compiler_params=PARAMS,
         name="final",
     )
-    coeffs, mass = final(*near(outer, inner, edges, acc, limits, hot), coeffs)
+    coeffs, mass = final(*near(outer, inner, acc, limits, hot, base))
     mass = lax.all_to_all(mass, FIRST, 0, 0).sum(0)
     mass = lax.all_to_all(jnp.broadcast_to(mass, (n_second, 1, 128)), SECOND, 0, 0).sum(0)
-    return coeffs, mass[0, : 4 * GROUPS].reshape(4, GROUPS).T
+    return coeffs.reshape(nx, ny, size), mass[0, : 4 * GROUPS].reshape(4, GROUPS).T
 
 
 def solution(mesh):

time: 67.4 us -> 66.3 us (0.984)
  blocking collectives: 27.4 us -> 12 us
  starting transfers between devices: 23.9 us -> 31.2 us
  waiting for transfers between devices: 0.01 us -> 7.15 us
  local copies, waits for them, and re-layouts: 0.89 us -> 2.64 us
  Pallas kernels: 13.8 us -> 12.1 us
    all_to_all x1 -> x0, blocking collectives: 15.3 us -> none  [shards(): lax.all_to_all(jnp.broadcast_to(mass, (n_second, 1, 128)), SECOND, 0, 0)]
    all_to_all x0 -> x1, starting transfers between devices: none -> 7.31 us  [shards(): lax.all_to_all(jnp.broadcast_to(mass, (n_second, 1, 128)), SECOND, 0, 0)]
    all_to_all x0 -> x1, waiting for transfers between devices: none -> 7.14 us  [shards(): lax.all_to_all(jnp.broadcast_to(mass, (n_second, 1, 128)), SECOND, 0, 0)]
    unnamed x10 -> x7, local copies, waits for them, and re-layouts: 0.1 us -> 1.34 us
    pallas_call x1, Pallas kernels: 2.38 us -> 1.2 us  [shards(): right, left = edge(far(flat))]
  transfers between devices with their start and end apart: 4 -> 5, of which waited for: 0 -> 1; matrix products, arithmetic and copies ran while one was open for 1% -> 2% of each run, Pallas kernels for 14% -> 14%
where the time goes in v4:
time: 66.3 us; the launch traced here: 66 us
  starting transfers between devices  31.2 us (47%)
  Pallas kernels  12.1 us (18%)
  blocking collectives  12 us (18%)
  waiting for transfers between devices  7.15 us (11%)
  local copies, waits for them, and re-layouts  2.64 us (4%)
  between operations  0.78 us (1%)
    all_to_all x1, blocking collectives, shards(): mass = lax.all_to_all(mass, FIRST, 0, 0).sum(0)  12 us
    ppermute x1, starting transfers between devices, neighbours(): lax.ppermute(value_down, axis, [(j, i) for i, j in up])  10.4 us
    all_to_all x1, starting transfers between devices, shards(): lax.all_to_all(jnp.broadcast_to(mass, (n_second, 1, 128)), SECOND, 0, 0)  7.31 us
    all_to_all x1, waiting for transfers between devices, shards(): lax.all_to_all(jnp.broadcast_to(mass, (n_second, 1, 128)), SECOND, 0, 0)  7.14 us
    pallas_call x1, Pallas kernels, shards(): work, inner, outer = bulk(far(flat), *near(right, table))  5.79 us
    ppermute x1, starting transfers between devices, shards(): inner = lax.ppermute(inner, COL, swap_inner)  5.52 us
    ppermute x1, starting transfers between devices, neighbours(): lax.ppermute(value_up, axis, up)  4.02 us
    ppermute x1, starting transfers between devices, shards(): outer = lax.ppermute(outer, COL, swap_outer)  3.95 us
  transfers between devices with their start and end apart: 5, of which 1 were waited for; matrix products, arithmetic and copies ran while one was open for 2% of the time, Pallas kernels for 14%

profile of v4, /device:TPU:1, one launch (start us, length us, event | category | flops | bytes accessed | tf_op | source)
XLA Modules:
  0.0 66.0 jit_solution(2879757064978725366)
XLA Ops:
  0.6 0.0 copy-start
  0.6 1.2 %edge.1 = (f32[96,512]{1,0:T(8,128)S(1)}, f32[96,512]{1,0:T(8,128)S(1)}) custom-call(f32[1024,512]{1,0:T(8,128)} %bitcast.10), custom_call_target="tpu_custom_call" | custom-call | tf_op jit(solution)/shard_map/edge/pallas_call | solution.py:341
  1.8 0.0 copy-start.1
  1.9 0.0 copy-start.2
  1.9 4.0 %collective-permute-start = (f32[96,512]{1,0:T(8,128)S(1)}, f32[96,512]{1,0:T(8,128)S(1)}, u32[]{:S(2)}, u32[]{:S(2)}) collective-permute-start(f32[96,512]{1,0:T(8,128)S(1)} %get-tuple-element.15.after_ref), channel_id=1, source_target_pairs={{0,32},{32,64},{64,96},{96,128},{128,160},{160,192},{192,224},{224... | collective-permute-start | bytes 589832 | tf_op jit(solution)/shard_map/ppermute | solution.py:307
  5.9 10.4 %collective-permute-start.1 = (f32[96,512]{1,0:T(8,128)S(1)}, f32[96,512]{1,0:T(8,128)S(1)}, u32[]{:S(2)}, u32[]{:S(2)}) collective-permute-start(f32[96,512]{1,0:T(8,128)S(1)} %get-tuple-element.16), channel_id=1, source_target_pairs={{32,0},{64,32},{96,64},{128,96},{160,128},{192,160},{224,192},{256... | collective-permute-start | bytes 589832 | tf_op jit(solution)/shard_map/ppermute | solution.py:307
  16.3 0.0 copy-done
  16.3 5.8 %bulk.1 = (f32[1024,512]{1,0:T(8,128)S(1)}, f32[96,512]{1,0:T(8,128)S(1)}, f32[96,512]{1,0:T(8,128)S(1)}) custom-call(f32[1024,512]{1,0:T(8,128)} %bitcast.11, f32[96,512]{1,0:T(8,128)S(1)} %get-tuple-element.15.after_ref, bf16[512,512]{1,0:T(8,128)(2,1)S(1)} %copy-done), custom_call_target="tpu_custom_call" | custom-call | flops 40000000 | bytes 4194304 | tf_op jit(solution)/shard_map/bulk/pallas_call | solution.py:353
  22.1 0.0 collective-permute-done.got_l_ref
  22.1 0.0 collective-permute-done.1.got_r_ref
  22.1 0.5 plane.1
  22.6 4.0 %collective-permute-start.2 = (f32[96,512]{1,0:T(8,128)S(1)}, f32[96,512]{1,0:T(8,128)S(1)}, u32[]{:S(2)}, u32[]{:S(2)}) collective-permute-start(f32[96,512]{1,0:T(8,128)S(1)} %get-tuple-element.19), channel_id=1, source_target_pairs={{1,2},{2,1},{3,4},{4,3},{5,6},{6,5},{7,8},{8,7},{9,10},{10,9},{11,... | collective-permute-start | bytes 589832 | tf_op jit(solution)/shard_map/ppermute | solution.py:366
  26.6 5.5 %collective-permute-start.3 = (f32[96,512]{1,0:T(8,128)S(1)}, f32[96,512]{1,0:T(8,128)S(1)}, u32[]{:S(2)}, u32[]{:S(2)}) collective-permute-start(f32[96,512]{1,0:T(8,128)S(1)} %get-tuple-element.20), channel_id=1, source_target_pairs={{0,1},{1,0},{2,3},{3,2},{4,5},{5,4},{6,7},{7,6},{8,9},{9,8},{10,11... | collective-permute-start | bytes 589832 | tf_op jit(solution)/shard_map/ppermute | solution.py:365
  32.1 0.0 copy-done.1
  32.1 0.0 copy-done.2
  32.1 3.6 %rows.1 = (f32[1024,512]{1,0:T(8,128)S(1)}, f32[4,8,512]{2,1,0:T(8,128)S(1)}, f32[4,512]{1,0:T(4,128)S(1)}, f32[8,128]{1,0:T(8,128)S(1)}) custom-call(f32[1024,512]{1,0:T(8,128)S(1)} %get-tuple-element.21.w_ref, f32[96,512]{1,0:T(8,128)S(1)} %collective-permute-done.got_l_ref, f32[96,512]{1,0:T(8,128)S(1)} %collective-permute-done.1.got_r_ref, ...), custom_call_target="tpu_custom_call" | custom-call | flops 40000000 | bytes 4194304 | tf_op jit(solution)/shard_map/rows/pallas_call | solution.py:377
  35.8 0.0 collective-permute-done.2.outer_ref
  35.8 0.0 collective-permute-done.3.inner_ref
  35.8 1.0 %final.1 = (f32[1024,512]{1,0:T(8,128)S(1)}, f32[16,1,128]{2,1,0:T(1,128)S(1)}) custom-call(f32[96,512]{1,0:T(8,128)S(1)} %collective-permute-done.2.outer_ref, f32[96,512]{1,0:T(8,128)S(1)} %collective-permute-done.3.inner_ref, f32[4,8,512]{2,1,0:T(8,128)S(1)} %get-tuple-element.22.acc_in, ...), custom_call_target="tpu_custom_call", output_to_operand_aliasing={{0}: (5, {})} | custom-call | tf_op jit(solution)/shard_map/final/pallas_call | solution.py:392
  36.8 12.0 %all_to_all.10 = f32[16,1,128]{2,1,0:T(1,128)S(1)} all-to-all(f32[16,1,128]{2,1,0:T(1,128)S(1)} %get-tuple-element.27), channel_id=1, replica_groups=mesh['z'=8,'y_lo'=2,'y_hi'=4,'x'=4,'core'=2] {'y_hi','y_lo','core'}, dimensions={0} | all-to-all | bytes 16384 | tf_op jit(solution)/shard_map/all_to_all | solution.py:393
  48.9 0.6 broadcast_in_dim.3
  49.5 7.3 %all-to-all-start.1 = ((f32[32,1,128]{2,1,0:T(1,128)}), f32[32,1,128]{2,1,0:T(1,128)S(1)}, u32[]{:S(2)}, u32[]{:S(2)}) async-start(f32[32,1,128]{2,1,0:T(1,128)} %broadcast_in_dim.3), calls=%async_computation.1 | async-start | bytes 32768 | tf_op jit(solution)/shard_map/all_to_all | solution.py:394
  56.8 1.3 %copy.9 = f32[32,32,512]{2,1,0:T(8,128)} copy(f32[32,32,512]{2,1,0:T(8,128)S(1)} %bitcast.7) | data formatting | bytes 4194304
  58.1 7.1 %all-to-all-done.1 = f32[32,1,128]{2,1,0:T(1,128)S(1)} async-done(((f32[32,1,128]{2,1,0:T(1,128)}), f32[32,1,128]{2,1,0:T(1,128)S(1)}, u32[]{:S(2)}, u32[]{:S(2)}) %all-to-all-start.1) | async-done | bytes 16416 | tf_op jit(solution)/shard_map/all_to_all | solution.py:394
  65.3 0.7 %reshape_squeeze.3 = f32[4,16]{1,0:T(4,128)} reshape(f32[64]{0:T(128)S(1)} %slice_reduce_fusion) | data formatting | bytes 512 | tf_op jit(solution)/shard_map/reshape;squeeze | solution.py:395
  (3 shorter events, 0.1 us)
Async XLA Ops:
  0.6 15.7 %copy-start = (bf16[512,512]{1,0:T(8,128)(2,1)S(1)}, bf16[512,512]{1,0:T(8,128)(2,1)}, u32[]{:S(2)}) copy-start(bf16[512,512]{1,0:T(8,128)(2,1)} %constant.4.clone.table_ref) | copy-start | bytes 1572868
  1.8 30.3 %copy-start.1 = (s32[1,1,2]{2,1,0:T(1,128)S(1)}, s32[1,1,2]{2,1,0:T(1,128)}, u32[]{:S(2)}) copy-start(s32[1,1,2]{2,1,0:T(1,128)} %param.5) | copy-start | bytes 28
  1.9 30.3 %copy-start.2 = (s32[1,1,2]{2,1,0:T(1,128)S(1)}, s32[1,1,2]{2,1,0:T(1,128)}, u32[]{:S(2)}) copy-start(s32[1,1,2]{2,1,0:T(1,128)} %param.6) | copy-start | bytes 28
  1.9 20.2 %collective-permute-start = (f32[96,512]{1,0:T(8,128)S(1)}, f32[96,512]{1,0:T(8,128)S(1)}, u32[]{:S(2)}, u32[]{:S(2)}) collective-permute-start(f32[96,512]{1,0:T(8,128)S(1)} %get-tuple-element.15.after_ref), channel_id=1, source_target_pairs={{0,32},{32,64},{64,96},{96,128},{128,160},{160,192},{192,224},{224... | collective-permute-start | bytes 589832 | tf_op jit(solution)/shard_map/ppermute | solution.py:307
  5.9 16.2 %collective-permute-start.1 = (f32[96,512]{1,0:T(8,128)S(1)}, f32[96,512]{1,0:T(8,128)S(1)}, u32[]{:S(2)}, u32[]{:S(2)}) collective-permute-start(f32[96,512]{1,0:T(8,128)S(1)} %get-tuple-element.16), channel_id=1, source_target_pairs={{32,0},{64,32},{96,64},{128,96},{160,128},{192,160},{224,192},{256... | collective-permute-start | bytes 589832 | tf_op jit(solution)/shard_map/ppermute | solution.py:307
  22.6 13.1 %collective-permute-start.2 = (f32[96,512]{1,0:T(8,128)S(1)}, f32[96,512]{1,0:T(8,128)S(1)}, u32[]{:S(2)}, u32[]{:S(2)}) collective-permute-start(f32[96,512]{1,0:T(8,128)S(1)} %get-tuple-element.19), channel_id=1, source_target_pairs={{1,2},{2,1},{3,4},{4,3},{5,6},{6,5},{7,8},{8,7},{9,10},{10,9},{11,... | collective-permute-start | bytes 589832 | tf_op jit(solution)/shard_map/ppermute | solution.py:366
  26.6 9.2 %collective-permute-start.3 = (f32[96,512]{1,0:T(8,128)S(1)}, f32[96,512]{1,0:T(8,128)S(1)}, u32[]{:S(2)}, u32[]{:S(2)}) collective-permute-start(f32[96,512]{1,0:T(8,128)S(1)} %get-tuple-element.20), channel_id=1, source_target_pairs={{0,1},{1,0},{2,3},{3,2},{4,5},{5,4},{6,7},{7,6},{8,9},{9,8},{10,11... | collective-permute-start | bytes 589832 | tf_op jit(solution)/shard_map/ppermute | solution.py:365
  49.5 15.8 %all-to-all-start.1 = ((f32[32,1,128]{2,1,0:T(1,128)}), f32[32,1,128]{2,1,0:T(1,128)S(1)}, u32[]{:S(2)}, u32[]{:S(2)}) async-start(f32[32,1,128]{2,1,0:T(1,128)} %broadcast_in_dim.3), calls=%async_computation.1 | async-start | bytes 32768 | tf_op jit(solution)/shard_map/all_to_all | solution.py:394

commit v5 on v4

--- a/solution.py
+++ b/solution.py
@@ -22,8 +22,8 @@
 ANY = pl.BlockSpec(memory_space=pl.ANY)
 
 
-def in_vmem(shape):
-    return pltpu.VMEM(shape, F32)
+def in_vmem(shape, dtype=F32):
+    return pltpu.VMEM(shape, dtype)
 
 
 def lane_lift(v):
@@ -46,9 +46,9 @@
     return np.stack([s, d], axis=2).reshape(size, size).astype(jnp.bfloat16)
 
 
-def table_lift(v, table):
+def table_lift(v, table, pieces=2):
     total = None
-    for _ in range(3):
+    for _ in range(pieces):
         piece = v.astype(jnp.bfloat16)
         v = v - piece.astype(F32)
         term = jnp.dot(piece, table, preferred_element_type=F32)
@@ -85,17 +85,19 @@
     return total
 
 
-def edge_kernel(nx, ny, p_ref, right_ref, left_ref, first, last, sems):
+def edge_kernel(nx, ny, p_ref, outer_ref, inner_ref, first, last, sems):
     lo = pltpu.make_async_copy(p_ref.at[pl.ds(0, 5 * ny)], first, sems.at[0])
     hi = pltpu.make_async_copy(p_ref.at[pl.ds((nx - 6) * ny, 6 * ny)], last, sems.at[1])
     lo.start()
     hi.start()
+    even = lax.axis_index("y_lo") == 0
     lo.wait()
-    for k, v in enumerate(to_left(lambda i: first[pl.ds(i * ny, ny), :])):
-        left_ref[pl.ds(k * ny, ny), :] = v
     hi.wait()
-    for k, v in enumerate(to_right(lambda i: last[pl.ds((6 - i) * ny, ny), :])):
-        right_ref[pl.ds(k * ny, ny), :] = v
+    left = to_left(lambda i: first[pl.ds(i * ny, ny), :])
+    right = to_right(lambda i: last[pl.ds((6 - i) * ny, ny), :])
+    for k, (r, l) in enumerate(zip(right, left)):
+        outer_ref[pl.ds(k * ny, ny), :] = jnp.where(even, l, r)
+        inner_ref[pl.ds(k * ny, ny), :] = jnp.where(even, r, l)
 
 
 def boundary_lines(head, tail):
@@ -116,42 +118,35 @@
     return head, [weights(FROM_RIGHT, lambda i: 8 - i, k) for k in range(3)]
 
 
-def bulk_kernel(nx, ny, p_ref, after_ref, table_ref, w_ref, inner_ref, outer_ref, raw, sems):
-    del after_ref
-    chunks = 4
-    size = nx * ny // chunks
-    copies = []
-    for i in range(chunks):
+def bulk_kernel(nx, ny, p_ref, table_hbm, w_ref, inner_ref, outer_ref, table_ref, sem):
+    copy = pltpu.make_async_copy(table_hbm, table_ref, sem)
+    copy.start()
+    half = nx // 2
+    tiles = w_ref.shape[1] // 128
+
+    def column(i, _):
+        lanes = pl.ds(pl.multiple_of(i % tiles * 128, 128), 128)
+        rows = lambda x: pl.ds(pl.multiple_of(x * ny + i // tiles * 8, 8), 8)
+        e = [p_ref[rows(2 * j), lanes] for j in range(half)]
+        d = {-2: B * e[0], -1: B * e[1] - A * e[0], half: B * e[half - 1]}
+        for j in range(half):
+            near = e[j] + e[j + 1] if j + 1 < half else e[j]
+            v = p_ref[rows(2 * j + 1), lanes] - A * near
+            far = [e[i] for i in (j - 1, j + 2) if 0 <= i < half]
+            if far:
+                v = v + B * functools.reduce(lambda a, b: a + b, far)
+            d[j] = v
+            w_ref[rows(2 * j + 1), lanes] = v
+        for j in range(half):
+            w_ref[rows(2 * j), lanes] = e[j] + (C * (d[j - 1] + d[j]) - G * (d[j - 2] + d[j + 1]))
+        return 0
+
+    lax.fori_loop(0, ny // 8 * tiles, column, 0, unroll=2)
+    copy.wait()
+    size = nx * ny // 4
+    for i in range(4):
         part = pl.ds(i * size, size)
-        copies.append(pltpu.make_async_copy(p_ref.at[part], raw.at[part], sems.at[i]))
-        copies[-1].start()
-    for i in range(chunks):
-        copies[i].wait()
-
-        part = pl.ds(i * size, size)
-        w_ref[part, :] = table_lift(raw[part, :], table_ref[...])
-    half = nx // 2
-
-    def column(t, _):
-        for c in range(w_ref.shape[1] // 128):
-            lanes = slice(c * 128, (c + 1) * 128)
-            rows = lambda x: pl.ds(pl.multiple_of(x * ny + t * 8, 8), 8)
-            e = [w_ref[rows(2 * j), lanes] for j in range(half)]
-            d = {-2: B * e[0], -1: B * e[1] - A * e[0], half: B * e[half - 1]}
-            for j in range(half):
-                near = e[j] + e[j + 1] if j + 1 < half else e[j]
-                v = w_ref[rows(2 * j + 1), lanes] - A * near
-                far = [e[i] for i in (j - 1, j + 2) if 0 <= i < half]
-                if far:
-                    v = v + B * functools.reduce(lambda a, b: a + b, far)
-                d[j] = v
-                w_ref[rows(2 * j + 1), lanes] = v
-            for j in range(half):
-                w_ref[rows(2 * j), lanes] = e[j] + (C * (d[j - 1] + d[j]) - G * (d[j - 2] + d[j + 1]))
-        return 0
-
-    lax.fori_loop(0, ny // 8, column, 0)
-
+        w_ref[part, :] = table_lift(w_ref[part, :], table_ref[...], 3)
     even = lax.axis_index("core") == 0
 
     def partial(x, _):
@@ -163,17 +158,19 @@
             outer_ref[pl.ds(k * nx + x, 1), :] = jnp.where(even, left, right)
         return 0
 
-    lax.fori_loop(0, nx, partial, 0, unroll=4)
-
-
-def plane_kernel(nx, ny, got_l_ref, got_r_ref, table_ref, inner_in, outer_in, inner_ref, outer_ref, lines):
+    lax.fori_loop(0, nx, partial, 0, unroll=8)
+
+
+def plane_kernel(nx, ny, got_o_ref, got_i_ref, table_ref, inner_in, outer_in, inner_ref, outer_ref, lines):
     size = table_ref.shape[0]
     even = lax.axis_index("core") == 0
     lines[...] = jnp.zeros_like(lines)
+    y_even = lax.axis_index("y_lo") == 0
     for h in range(6):
-        got = (got_l_ref, got_r_ref)[h // 3]
         at = h % 3 * ny
-        for m, line in enumerate(boundary_lines(got[at : at + 8, :], got[at + ny - 8 : at + ny, :])):
+        of_even, of_odd = (got_o_ref, got_i_ref) if h < 3 else (got_i_ref, got_o_ref)
+        got = lambda part: jnp.where(y_even, of_even[part, :], of_odd[part, :])
+        for m, line in enumerate(boundary_lines(got(slice(at, at + 8)), got(slice(at + ny - 8, at + ny)))):
             lines[6 * h + m : 6 * h + m + 1, :] = line
     lines[...] = table_lift(lines[...], table_ref[...])
     inner_ref[...] = inner_in[...]
@@ -197,7 +194,7 @@
     return [a + jnp.maximum(m - lim, 0.0) for a, lim in zip(acc, limits)]
 
 
-def rows_kernel(nx, ny, w_ref, got_l_ref, got_r_ref, table_ref, cut_ref, group_ref, out_ref, acc_ref, lim_ref, hot_ref, halo, fixed_ref):
+def rows_kernel(nx, ny, w_ref, got_o_ref, got_i_ref, table_ref, cut_ref, group_ref, out_ref, acc_ref, lim_ref, hot_ref, halo, fixed_ref):
     size = w_ref.shape[1]
     blocks = cut_ref.shape[1]
     lane = lax.broadcasted_iota(jnp.int32, (1, size), 1)
@@ -214,8 +211,9 @@
     hot_ref[...] = jnp.where(hot, 1.0, 0.0)
     acc_ref[...] = jnp.zeros_like(acc_ref)
 
-    halo[pl.ds(0, 3 * ny), :] = table_lift(got_l_ref[...], table_ref[...])
-    halo[pl.ds(3 * ny, 3 * ny), :] = table_lift(got_r_ref[...], table_ref[...])
+    y_even = lax.axis_index("y_lo") == 0
+    halo[pl.ds(0, 3 * ny), :] = table_lift(jnp.where(y_even, got_o_ref[...], got_i_ref[...]), table_ref[...])
+    halo[pl.ds(3 * ny, 3 * ny), :] = table_lift(jnp.where(y_even, got_i_ref[...], got_o_ref[...]), table_ref[...])
 
     def fix(t, _):
         rows = lambda x: pl.ds(pl.multiple_of(x * ny + t * 8, 8), 8)
@@ -301,15 +299,23 @@
         mass_ref[i] = line
 
 
-def neighbours(value_up, value_down, axis):
-    n = lax.axis_size(axis)
-    up = [(i, (i + 1) % n) for i in range(n)]
-    return lax.ppermute(value_up, axis, up), lax.ppermute(value_down, axis, [(j, i) for i, j in up])
+def spread_kernel(parts_ref, out_ref):
+    total = parts_ref[0]
+    for i in range(1, parts_ref.shape[0]):
+        total = total + parts_ref[i]
+    for i in range(out_ref.shape[0]):
+        out_ref[i] = total
 
 
 def pair_swaps(n):
     inner = [(i, i ^ 1) for i in range(n)]
     return inner, [((i + 1) % n, (j + 1) % n) for i, j in inner]
+
+
+def exchange(outer, inner, axes):
+    swap_inner, swap_outer = pair_swaps(lax.axis_size(axes))
+    inner = lax.ppermute(inner, axes, swap_inner)
+    return lax.ppermute(outer, axes, swap_outer), inner
 
 
 def near(*values):
@@ -338,19 +344,25 @@
         compiler_params=PARAMS,
         name="edge",
     )
-    right, left = edge(far(flat))
-    from_left, from_right = neighbours(right, left, ROW)
+    outer, inner = edge(far(flat))
+    later, outer, inner = lax.optimization_barrier((flat, outer, inner))
+    got_outer, got_inner = exchange(outer, inner, ROW)
     bulk = pl.pallas_call(
         functools.partial(bulk_kernel, nx, ny),
-        out_shape=(in_vmem((nx * ny, size)), in_vmem((3 * nx, size)), in_vmem((3 * nx, size))),
-        in_specs=[ANY, VMEM, VMEM],
-        out_specs=(VMEM, VMEM, VMEM),
-        scratch_shapes=[pltpu.VMEM((nx * ny, size), F32), pltpu.SemaphoreType.DMA((4,))],
+        out_shape=(
+            in_vmem((nx * ny, size)),
+            in_vmem((3 * nx, size)),
+            in_vmem((3 * nx, size)),
+            in_vmem((size, size), jnp.bfloat16),
+        ),
+        in_specs=[VMEM, ANY],
+        out_specs=(VMEM,) * 4,
+        scratch_shapes=[pltpu.SemaphoreType.DMA],
         cost_estimate=cost(40_000_000),
         compiler_params=PARAMS,
         name="bulk",
     )
-    work, inner, outer = bulk(far(flat), *near(right, table))
+    work, inner, outer, table = bulk(*near(later), far(table))
     plane = pl.pallas_call(
         functools.partial(plane_kernel, nx, ny),
         out_shape=(in_vmem((3 * nx, size)), in_vmem((3 * nx, size))),
@@ -360,10 +372,8 @@
         compiler_params=PARAMS,
         name="plane",
     )
-    inner, outer = plane(*near(from_left, from_right, table, inner, outer))
-    swap_inner, swap_outer = pair_swaps(lax.axis_size(COL))
-    inner = lax.ppermute(inner, COL, swap_inner)
-    outer = lax.ppermute(outer, COL, swap_outer)
+    inner, outer = plane(*near(got_outer, got_inner, table, inner, outer))
+    outer, inner = exchange(outer, inner, COL)
     rows = pl.pallas_call(
         functools.partial(rows_kernel, nx, ny),
         out_shape=(in_vmem((nx * ny, size)), in_vmem((4, 8, size)), in_vmem((4, size)), in_vmem((8, 128))),
@@ -375,7 +385,7 @@
         name="rows",
     )
     base, acc, limits, hot = rows(
-        *near(work, from_left, from_right, table, cut_exponent.reshape(1, blocks_z), group_map.reshape(1, blocks_z))
+        *near(work, got_outer, got_inner, table, cut_exponent.reshape(1, blocks_z), group_map.reshape(1, blocks_z))
     )
     n_first, n_second = lax.axis_size(FIRST), lax.axis_size(SECOND)
     scale = 1.0 / (nx * ny * (size // blocks_z))
@@ -390,8 +400,16 @@
         name="final",
     )
     coeffs, mass = final(*near(outer, inner, acc, limits, hot, base))
-    mass = lax.all_to_all(mass, FIRST, 0, 0).sum(0)
-    mass = lax.all_to_all(jnp.broadcast_to(mass, (n_second, 1, 128)), SECOND, 0, 0).sum(0)
+    spread = pl.pallas_call(
+        spread_kernel,
+        out_shape=in_vmem((n_second, 1, 128)),
+        in_specs=[VMEM],
+        out_specs=VMEM,
+        compiler_params=PARAMS,
+        name="spread",
+    )
+    mass = spread(*near(lax.all_to_all(mass, FIRST, 0, 0)))
+    mass = lax.all_to_all(mass, SECOND, 0, 0).sum(0)
     return coeffs.reshape(nx, ny, size), mass[0, : 4 * GROUPS].reshape(4, GROUPS).T
 
 

time: 66.3 us -> 65.8 us (level)
  starting transfers between devices: 31.2 us -> 27.7 us
  blocking collectives: 12 us -> 14.9 us
  waiting for transfers between devices: 7.15 us -> 9.23 us
  Pallas kernels: 12.1 us -> 10.7 us
    all_to_all x1, starting transfers between devices: 7.31 us -> 3.84 us  [shards(): mass = lax.all_to_all(mass, SECOND, 0, 0).sum(0)]
    all_to_all x1, blocking collectives: 12 us -> 14.9 us  [shards(): mass = spread(*near(lax.all_to_all(mass, FIRST, 0, 0)))]
    ppermute x4, waiting for transfers between devices: 0.01 us -> 1.93 us  [the longest x2 1.93 us: exchange(): inner = lax.ppermute(inner, axes, swap_inner)]
    pallas_call x4 -> x5, Pallas kernels: 11.1 us -> 9.68 us  [the longest x1 3.9 us: shards(): work, inner, outer, table = bulk(*near(later), far(table))]
  transfers between devices with their start and end apart: 5 -> 5, of which waited for: 1 -> 2; matrix products, arithmetic and copies ran while one was open for 2% -> 2% of each run, Pallas kernels for 14% -> 11%
where the time goes in v5:
time: 65.8 us; the launch traced here: 65.4 us
  starting transfers between devices  27.7 us (42%)
  blocking collectives  14.9 us (23%)
  Pallas kernels  10.7 us (16%)
  waiting for transfers between devices  9.23 us (14%)
  local copies, waits for them, and re-layouts  2.02 us (3%)
  between operations  0.78 us (1%)
    ppermute x2, starting transfers between devices, exchange(): return (lax.ppermute(outer, axes, swap_outer), inner)  17 us
    all_to_all x1, blocking collectives, shards(): mass = spread(*near(lax.all_to_all(mass, FIRST, 0, 0)))  14.9 us
    all_to_all x1, waiting for transfers between devices, shards(): mass = lax.all_to_all(mass, SECOND, 0, 0).sum(0)  7.29 us
    ppermute x2, starting transfers between devices, exchange(): inner = lax.ppermute(inner, axes, swap_inner)  6.87 us
    pallas_call x1, Pallas kernels, shards(): work, inner, outer, table = bulk(*near(later), far(table))  3.9 us
    all_to_all x1, starting transfers between devices, shards(): mass = lax.all_to_all(mass, SECOND, 0, 0).sum(0)  3.84 us
    pallas_call x1, Pallas kernels, shards(): rows(*near(work, got_outer, got_inner, table, cut_exponent.reshape(1, blo...  3.46 us
    ppermute x2, waiting for transfers between devices, exchange(): inner = lax.ppermute(inner, axes, swap_inner)  1.93 us
  transfers between devices with their start and end apart: 5, of which 2 were waited for; matrix products, arithmetic and copies ran while one was open for 2% of the time, Pallas kernels for 11%

profile of v5, /device:TPU:1, one launch (start us, length us, event | category | flops | bytes accessed | tf_op | source)
XLA Modules:
  0.0 65.4 jit_solution(2765804080412804716)
XLA Ops:
  0.6 0.0 copy-start
  0.6 1.3 %edge.1 = (f32[96,512]{1,0:T(8,128)S(1)}, f32[96,512]{1,0:T(8,128)S(1)}) custom-call(f32[1024,512]{1,0:T(8,128)} %bitcast.7), custom_call_target="tpu_custom_call" | custom-call | tf_op jit(solution)/shard_map/edge/pallas_call | solution.py:347
  2.0 0.0 copy-start.1
  2.0 0.0 copy-start.2
  2.0 12.5 %collective-permute-start = (f32[96,512]{1,0:T(8,128)S(1)}, f32[96,512]{1,0:T(8,128)S(1)}, u32[]{:S(2)}, u32[]{:S(2)}) collective-permute-start(f32[96,512]{1,0:T(8,128)S(1)} %get-tuple-element.21), channel_id=1, source_target_pairs={{32,64},{64,32},{96,128},{128,96},{160,192},{192,160},{224,256},{2... | collective-permute-start | bytes 589832 | tf_op jit(solution)/shard_map/ppermute | solution.py:318
  14.5 1.9 %collective-permute-start.1 = (f32[96,512]{1,0:T(8,128)S(1)}, f32[96,512]{1,0:T(8,128)S(1)}, u32[]{:S(2)}, u32[]{:S(2)}) collective-permute-start(f32[96,512]{1,0:T(8,128)S(1)} %get-tuple-element.22), channel_id=1, source_target_pairs={{0,32},{32,0},{64,96},{96,64},{128,160},{160,128},{192,224},{224,1... | collective-permute-start | bytes 589832 | tf_op jit(solution)/shard_map/ppermute | solution.py:317
  16.4 0.0 copy-done
  16.4 3.9 %bulk.1 = (f32[1024,512]{1,0:T(8,128)S(1)}, f32[96,512]{1,0:T(8,128)S(1)}, f32[96,512]{1,0:T(8,128)S(1)}, bf16[512,512]{1,0:T(8,128)(2,1)S(1)}) custom-call(f32[1024,512]{1,0:T(8,128)S(1)} %bitcast.8, bf16[512,512]{1,0:T(8,128)(2,1)} %constant.4.clone.table_hbm), custom_call_target="tpu_custom_call" | custom-call | flops 40000000 | bytes 4194304 | tf_op jit(solution)/shard_map/bulk/pallas_call | solution.py:365
  20.3 0.0 collective-permute-done.got_o_ref
  20.3 1.9 %collective-permute-done.1.got_i_ref = f32[96,512]{1,0:T(8,128)S(1)} collective-permute-done((f32[96,512]{1,0:T(8,128)S(1)}, f32[96,512]{1,0:T(8,128)S(1)}, u32[]{:S(2)}, u32[]{:S(2)}) %collective-permute-start.1) | collective-permute-done | bytes 196640 | tf_op jit(solution)/shard_map/ppermute | solution.py:317
  22.3 0.4 plane.1
  22.7 4.5 %collective-permute-start.2 = (f32[96,512]{1,0:T(8,128)S(1)}, f32[96,512]{1,0:T(8,128)S(1)}, u32[]{:S(2)}, u32[]{:S(2)}) collective-permute-start(f32[96,512]{1,0:T(8,128)S(1)} %get-tuple-element.27), channel_id=1, source_target_pairs={{1,2},{2,1},{3,4},{4,3},{5,6},{6,5},{7,8},{8,7},{9,10},{10,9},{11,... | collective-permute-start | bytes 589832 | tf_op jit(solution)/shard_map/ppermute | solution.py:318
  27.2 4.9 %collective-permute-start.3 = (f32[96,512]{1,0:T(8,128)S(1)}, f32[96,512]{1,0:T(8,128)S(1)}, u32[]{:S(2)}, u32[]{:S(2)}) collective-permute-start(f32[96,512]{1,0:T(8,128)S(1)} %get-tuple-element.28), channel_id=1, source_target_pairs={{0,1},{1,0},{2,3},{3,2},{4,5},{5,4},{6,7},{7,6},{8,9},{9,8},{10,11... | collective-permute-start | bytes 589832 | tf_op jit(solution)/shard_map/ppermute | solution.py:317
  32.2 0.0 copy-done.1
  32.2 0.0 copy-done.2
  32.2 3.5 %rows.1 = (f32[1024,512]{1,0:T(8,128)S(1)}, f32[4,8,512]{2,1,0:T(8,128)S(1)}, f32[4,512]{1,0:T(4,128)S(1)}, f32[8,128]{1,0:T(8,128)S(1)}) custom-call(f32[1024,512]{1,0:T(8,128)S(1)} %get-tuple-element.29.w_ref, f32[96,512]{1,0:T(8,128)S(1)} %collective-permute-done.got_o_ref, f32[96,512]{1,0:T(8,128)S(1)} %collective-permute-done.1.got_i_ref, ...), custom_call_target="tpu_custom_call" | custom-call | flops 40000000 | bytes 4194304 | tf_op jit(solution)/shard_map/rows/pallas_call | solution.py:387
  35.7 0.0 collective-permute-done.2.outer_ref
  35.7 0.0 collective-permute-done.3.inner_ref
  35.7 1.0 %final.1 = (f32[1024,512]{1,0:T(8,128)S(1)}, f32[16,1,128]{2,1,0:T(1,128)S(1)}) custom-call(f32[96,512]{1,0:T(8,128)S(1)} %collective-permute-done.2.outer_ref, f32[96,512]{1,0:T(8,128)S(1)} %collective-permute-done.3.inner_ref, f32[4,8,512]{2,1,0:T(8,128)S(1)} %get-tuple-element.30.acc_in, ...), custom_call_target="tpu_custom_call", output_to_operand_aliasing={{0}: (5, {})} | custom-call | tf_op jit(solution)/shard_map/final/pallas_call | solution.py:402
  36.7 14.9 %all_to_all.10.parts_ref = f32[16,1,128]{2,1,0:T(1,128)S(1)} all-to-all(f32[16,1,128]{2,1,0:T(1,128)S(1)} %get-tuple-element.35), channel_id=1, replica_groups=mesh['z'=8,'y_lo'=2,'y_hi'=4,'x'=4,'core'=2] {'y_hi','y_lo','core'}, dimensions={0} | all-to-all | bytes 16384 | tf_op jit(solution)/shard_map/all_to_all | solution.py:411
  51.6 0.6 spread.1
  52.3 3.8 %all-to-all-start.1 = ((f32[32,1,128]{2,1,0:T(1,128)}), f32[32,1,128]{2,1,0:T(1,128)S(1)}, u32[]{:S(2)}, u32[]{:S(2)}) async-start(f32[32,1,128]{2,1,0:T(1,128)} %spread.1), calls=%async_computation.1 | async-start | bytes 32768 | tf_op jit(solution)/shard_map/all_to_all | solution.py:412
  56.1 1.3 %copy.8 = f32[32,32,512]{2,1,0:T(8,128)} copy(f32[32,32,512]{2,1,0:T(8,128)S(1)} %bitcast.6) | data formatting | bytes 4194304
  57.4 7.3 %all-to-all-done.1 = f32[32,1,128]{2,1,0:T(1,128)S(1)} async-done(((f32[32,1,128]{2,1,0:T(1,128)}), f32[32,1,128]{2,1,0:T(1,128)S(1)}, u32[]{:S(2)}, u32[]{:S(2)}) %all-to-all-start.1) | async-done | bytes 16416 | tf_op jit(solution)/shard_map/all_to_all | solution.py:412
  64.7 0.1 reduce_sum.11
  64.8 0.7 %reshape_squeeze.3 = f32[4,16]{1,0:T(4,128)} reshape(f32[64]{0:T(128)S(1)} %slice_reduce_fusion) | data formatting | bytes 512 | tf_op jit(solution)/shard_map/reshape;squeeze | solution.py:413
  (1 shorter events, 0.0 us)
Async XLA Ops:
  0.6 15.8 %copy-start = (f32[32,32,512]{2,1,0:T(8,128)S(1)}, f32[32,32,512]{2,1,0:T(8,128)}, u32[]{:S(2)}) copy-start(f32[32,32,512]{2,1,0:T(8,128)} %param.4) | copy-start | bytes 6291460
  2.0 30.2 %copy-start.1 = (s32[1,1,2]{2,1,0:T(1,128)S(1)}, s32[1,1,2]{2,1,0:T(1,128)}, u32[]{:S(2)}) copy-start(s32[1,1,2]{2,1,0:T(1,128)} %param.5) | copy-start | bytes 28
  2.0 30.2 %copy-start.2 = (s32[1,1,2]{2,1,0:T(1,128)S(1)}, s32[1,1,2]{2,1,0:T(1,128)}, u32[]{:S(2)}) copy-start(s32[1,1,2]{2,1,0:T(1,128)} %param.6) | copy-start | bytes 28
  2.0 18.4 %collective-permute-start = (f32[96,512]{1,0:T(8,128)S(1)}, f32[96,512]{1,0:T(8,128)S(1)}, u32[]{:S(2)}, u32[]{:S(2)}) collective-permute-start(f32[96,512]{1,0:T(8,128)S(1)} %get-tuple-element.21), channel_id=1, source_target_pairs={{32,64},{64,32},{96,128},{128,96},{160,192},{192,160},{224,256},{2... | collective-permute-start | bytes 589832 | tf_op jit(solution)/shard_map/ppermute | solution.py:318
  14.5 7.8 %collective-permute-start.1 = (f32[96,512]{1,0:T(8,128)S(1)}, f32[96,512]{1,0:T(8,128)S(1)}, u32[]{:S(2)}, u32[]{:S(2)}) collective-permute-start(f32[96,512]{1,0:T(8,128)S(1)} %get-tuple-element.22), channel_id=1, source_target_pairs={{0,32},{32,0},{64,96},{96,64},{128,160},{160,128},{192,224},{224,1... | collective-permute-start | bytes 589832 | tf_op jit(solution)/shard_map/ppermute | solution.py:317
  22.7 13.0 %collective-permute-start.2 = (f32[96,512]{1,0:T(8,128)S(1)}, f32[96,512]{1,0:T(8,128)S(1)}, u32[]{:S(2)}, u32[]{:S(2)}) collective-permute-start(f32[96,512]{1,0:T(8,128)S(1)} %get-tuple-element.27), channel_id=1, source_target_pairs={{1,2},{2,1},{3,4},{4,3},{5,6},{6,5},{7,8},{8,7},{9,10},{10,9},{11,... | collective-permute-start | bytes 589832 | tf_op jit(solution)/shard_map/ppermute | solution.py:318
  27.2 8.5 %collective-permute-start.3 = (f32[96,512]{1,0:T(8,128)S(1)}, f32[96,512]{1,0:T(8,128)S(1)}, u32[]{:S(2)}, u32[]{:S(2)}) collective-permute-start(f32[96,512]{1,0:T(8,128)S(1)} %get-tuple-element.28), channel_id=1, source_target_pairs={{0,1},{1,0},{2,3},{3,2},{4,5},{5,4},{6,7},{7,6},{8,9},{9,8},{10,11... | collective-permute-start | bytes 589832 | tf_op jit(solution)/shard_map/ppermute | solution.py:317
  52.3 12.5 %all-to-all-start.1 = ((f32[32,1,128]{2,1,0:T(1,128)}), f32[32,1,128]{2,1,0:T(1,128)S(1)}, u32[]{:S(2)}, u32[]{:S(2)}) async-start(f32[32,1,128]{2,1,0:T(1,128)} %spread.1), calls=%async_computation.1 | async-start | bytes 32768 | tf_op jit(solution)/shard_map/all_to_all | solution.py:412

commit v6 on v5

--- a/solution.py
+++ b/solution.py
@@ -85,19 +85,17 @@
     return total
 
 
-def edge_kernel(nx, ny, p_ref, outer_ref, inner_ref, first, last, sems):
+def edge_kernel(nx, ny, p_ref, right_ref, left_ref, first, last, sems):
     lo = pltpu.make_async_copy(p_ref.at[pl.ds(0, 5 * ny)], first, sems.at[0])
     hi = pltpu.make_async_copy(p_ref.at[pl.ds((nx - 6) * ny, 6 * ny)], last, sems.at[1])
     lo.start()
     hi.start()
-    even = lax.axis_index("y_lo") == 0
     lo.wait()
+    for k, v in enumerate(to_left(lambda i: first[pl.ds(i * ny, ny), :])):
+        left_ref[pl.ds(k * ny, ny), :] = v
     hi.wait()
-    left = to_left(lambda i: first[pl.ds(i * ny, ny), :])
-    right = to_right(lambda i: last[pl.ds((6 - i) * ny, ny), :])
-    for k, (r, l) in enumerate(zip(right, left)):
-        outer_ref[pl.ds(k * ny, ny), :] = jnp.where(even, l, r)
-        inner_ref[pl.ds(k * ny, ny), :] = jnp.where(even, r, l)
+    for k, v in enumerate(to_right(lambda i: last[pl.ds((6 - i) * ny, ny), :])):
+        right_ref[pl.ds(k * ny, ny), :] = v
 
 
 def boundary_lines(head, tail):
@@ -161,16 +159,14 @@
     lax.fori_loop(0, nx, partial, 0, unroll=8)
 
 
-def plane_kernel(nx, ny, got_o_ref, got_i_ref, table_ref, inner_in, outer_in, inner_ref, outer_ref, lines):
+def plane_kernel(nx, ny, got_l_ref, got_r_ref, table_ref, inner_in, outer_in, inner_ref, outer_ref, lines):
     size = table_ref.shape[0]
     even = lax.axis_index("core") == 0
     lines[...] = jnp.zeros_like(lines)
-    y_even = lax.axis_index("y_lo") == 0
     for h in range(6):
+        got = (got_l_ref, got_r_ref)[h // 3]
         at = h % 3 * ny
-        of_even, of_odd = (got_o_ref, got_i_ref) if h < 3 else (got_i_ref, got_o_ref)
-        got = lambda part: jnp.where(y_even, of_even[part, :], of_odd[part, :])
-        for m, line in enumerate(boundary_lines(got(slice(at, at + 8)), got(slice(at + ny - 8, at + ny)))):
+        for m, line in enumerate(boundary_lines(got[at : at + 8, :], got[at + ny - 8 : at + ny, :])):
             lines[6 * h + m : 6 * h + m + 1, :] = line
     lines[...] = table_lift(lines[...], table_ref[...])
     inner_ref[...] = inner_in[...]
@@ -194,7 +190,7 @@
     return [a + jnp.maximum(m - lim, 0.0) for a, lim in zip(acc, limits)]
 
 
-def rows_kernel(nx, ny, w_ref, got_o_ref, got_i_ref, table_ref, cut_ref, group_ref, out_ref, acc_ref, lim_ref, hot_ref, halo, fixed_ref):
+def rows_kernel(nx, ny, w_ref, got_l_ref, got_r_ref, table_ref, cut_ref, group_ref, out_ref, acc_ref, lim_ref, hot_ref, halo, fixed_ref):
     size = w_ref.shape[1]
     blocks = cut_ref.shape[1]
     lane = lax.broadcasted_iota(jnp.int32, (1, size), 1)
@@ -211,9 +207,8 @@
     hot_ref[...] = jnp.where(hot, 1.0, 0.0)
     acc_ref[...] = jnp.zeros_like(acc_ref)
 
-    y_even = lax.axis_index("y_lo") == 0
-    halo[pl.ds(0, 3 * ny), :] = table_lift(jnp.where(y_even, got_o_ref[...], got_i_ref[...]), table_ref[...])
-    halo[pl.ds(3 * ny, 3 * ny), :] = table_lift(jnp.where(y_even, got_i_ref[...], got_o_ref[...]), table_ref[...])
+    halo[pl.ds(0, 3 * ny), :] = table_lift(got_l_ref[...], table_ref[...])
+    halo[pl.ds(3 * ny, 3 * ny), :] = table_lift(got_r_ref[...], table_ref[...])
 
     def fix(t, _):
         rows = lambda x: pl.ds(pl.multiple_of(x * ny + t * 8, 8), 8)
@@ -312,6 +307,11 @@
     return inner, [((i + 1) % n, (j + 1) % n) for i, j in inner]
 
 
+def shift(value, by, axes):
+    n = lax.axis_size(axes)
+    return lax.ppermute(value, axes, [(i, (i + by) % n) for i in range(n)])
+
+
 def exchange(outer, inner, axes):
     swap_inner, swap_outer = pair_swaps(lax.axis_size(axes))
     inner = lax.ppermute(inner, axes, swap_inner)
@@ -344,9 +344,9 @@
         compiler_params=PARAMS,
         name="edge",
     )
-    outer, inner = edge(far(flat))
-    later, outer, inner = lax.optimization_barrier((flat, outer, inner))
-    got_outer, got_inner = exchange(outer, inner, ROW)
+    right, left = edge(far(flat))
+    later, right, left = lax.optimization_barrier((flat, right, left))
+    from_left, from_right = shift(right, 1, ROW), shift(left, -1, ROW)
     bulk = pl.pallas_call(
         functools.partial(bulk_kernel, nx, ny),
         out_shape=(
@@ -372,7 +372,7 @@
         compiler_params=PARAMS,
         name="plane",
     )
-    inner, outer = plane(*near(got_outer, got_inner, table, inner, outer))
+    inner, outer = plane(*near(from_left, from_right, table, inner, outer))
     outer, inner = exchange(outer, inner, COL)
     rows = pl.pallas_call(
         functools.partial(rows_kernel, nx, ny),
@@ -385,7 +385,7 @@
         name="rows",
     )
     base, acc, limits, hot = rows(
-        *near(work, got_outer, got_inner, table, cut_exponent.reshape(1, blocks_z), group_map.reshape(1, blocks_z))
+        *near(work, from_left, from_right, table, cut_exponent.reshape(1, blocks_z), group_map.reshape(1, blocks_z))
     )
     n_first, n_second = lax.axis_size(FIRST), lax.axis_size(SECOND)
     scale = 1.0 / (nx * ny * (size // blocks_z))

time: 65.8 us -> 66.4 us (level)
  starting transfers between devices: 27.7 us -> 32.9 us
  blocking collectives: 14.9 us -> 12.4 us
  waiting for transfers between devices: 9.23 us -> 7.31 us
    ppermute x0 -> x2, starting transfers between devices: none -> 14.4 us  [shift(): return lax.ppermute(value, axes, [(i, (i + by) % n) for i in range(n)])]
    ppermute x2 -> x1, starting transfers between devices: 17 us -> 4.16 us  [exchange(): return (lax.ppermute(outer, axes, swap_outer), inner)]
    all_to_all x1, starting transfers between devices: 3.84 us -> 8.95 us  [shards(): mass = lax.all_to_all(mass, SECOND, 0, 0).sum(0)]
    all_to_all x1, blocking collectives: 14.9 us -> 12.4 us  [shards(): mass = spread(*near(lax.all_to_all(mass, FIRST, 0, 0)))]
    ppermute x2 -> x1, waiting for transfers between devices: 1.93 us -> 0.01 us  [exchange(): inner = lax.ppermute(inner, axes, swap_inner)]
    ppermute x2 -> x1, starting transfers between devices: 6.87 us -> 5.32 us  [exchange(): inner = lax.ppermute(inner, axes, swap_inner)]
  transfers between devices with their start and end apart: 5 -> 5, of which waited for: 2 -> 1; matrix products, arithmetic and copies ran while one was open for 2% -> 2% of each run, Pallas kernels for 11% -> 11%
where the time goes in v6:
time: 66.4 us; the launch traced here: 66.1 us
  starting transfers between devices  32.9 us (50%)
  blocking collectives  12.4 us (19%)
  Pallas kernels  10.7 us (16%)
  waiting for transfers between devices  7.31 us (11%)
  local copies, waits for them, and re-layouts  2.02 us (3%)
  between operations  0.78 us (1%)
    ppermute x2, starting transfers between devices, shift(): return lax.ppermute(value, axes, [(i, (i + by) % n) for i in range(n)])  14.4 us
    all_to_all x1, blocking collectives, shards(): mass = spread(*near(lax.all_to_all(mass, FIRST, 0, 0)))  12.4 us
    all_to_all x1, starting transfers between devices, shards(): mass = lax.all_to_all(mass, SECOND, 0, 0).sum(0)  8.95 us
    all_to_all x1, waiting for transfers between devices, shards(): mass = lax.all_to_all(mass, SECOND, 0, 0).sum(0)  7.3 us
    ppermute x1, starting transfers between devices, exchange(): inner = lax.ppermute(inner, axes, swap_inner)  5.32 us
    ppermute x1, starting transfers between devices, exchange(): return (lax.ppermute(outer, axes, swap_outer), inner)  4.16 us
    pallas_call x1, Pallas kernels, shards(): work, inner, outer, table = bulk(*near(later), far(table))  3.9 us
    pallas_call x1, Pallas kernels, shards(): rows(*near(work, from_left, from_right, table, cut_exponent.reshape(1, bl...  3.47 us
  transfers between devices with their start and end apart: 5, of which 1 were waited for; matrix products, arithmetic and copies ran while one was open for 2% of the time, Pallas kernels for 11%

profile of v6, /device:TPU:1, one launch (start us, length us, event | category | flops | bytes accessed | tf_op | source)
XLA Modules:
  0.0 66.1 jit_solution(17038973054950396240)
XLA Ops:
  0.6 0.0 copy-start
  0.6 1.3 %edge.1 = (f32[96,512]{1,0:T(8,128)S(1)}, f32[96,512]{1,0:T(8,128)S(1)}) custom-call(f32[1024,512]{1,0:T(8,128)} %bitcast.7), custom_call_target="tpu_custom_call" | custom-call | tf_op jit(solution)/shard_map/edge/pallas_call | solution.py:347
  1.9 0.0 copy-start.1
  1.9 0.0 copy-start.2
  2.0 4.0 %collective-permute-start = (f32[96,512]{1,0:T(8,128)S(1)}, f32[96,512]{1,0:T(8,128)S(1)}, u32[]{:S(2)}, u32[]{:S(2)}) collective-permute-start(f32[96,512]{1,0:T(8,128)S(1)} %get-tuple-element.21), channel_id=1, source_target_pairs={{0,32},{32,64},{64,96},{96,128},{128,160},{160,192},{192,224},{224... | collective-permute-start | bytes 589832 | tf_op jit(solution)/shard_map/ppermute | solution.py:312
  6.0 10.4 %collective-permute-start.1 = (f32[96,512]{1,0:T(8,128)S(1)}, f32[96,512]{1,0:T(8,128)S(1)}, u32[]{:S(2)}, u32[]{:S(2)}) collective-permute-start(f32[96,512]{1,0:T(8,128)S(1)} %get-tuple-element.22), channel_id=1, source_target_pairs={{0,480},{32,0},{64,32},{96,64},{128,96},{160,128},{192,160},{224,1... | collective-permute-start | bytes 589832 | tf_op jit(solution)/shard_map/ppermute | solution.py:312
  16.4 0.0 copy-done
  16.4 3.9 %bulk.1 = (f32[1024,512]{1,0:T(8,128)S(1)}, f32[96,512]{1,0:T(8,128)S(1)}, f32[96,512]{1,0:T(8,128)S(1)}, bf16[512,512]{1,0:T(8,128)(2,1)S(1)}) custom-call(f32[1024,512]{1,0:T(8,128)S(1)} %bitcast.8, bf16[512,512]{1,0:T(8,128)(2,1)} %constant.4.clone.table_hbm), custom_call_target="tpu_custom_call" | custom-call | flops 40000000 | bytes 4194304 | tf_op jit(solution)/shard_map/bulk/pallas_call | solution.py:365
  20.3 0.0 collective-permute-done.got_l_ref
  20.3 0.0 collective-permute-done.1.got_r_ref
  20.3 0.4 plane.1
  20.7 4.2 %collective-permute-start.2 = (f32[96,512]{1,0:T(8,128)S(1)}, f32[96,512]{1,0:T(8,128)S(1)}, u32[]{:S(2)}, u32[]{:S(2)}) collective-permute-start(f32[96,512]{1,0:T(8,128)S(1)} %get-tuple-element.27), channel_id=1, source_target_pairs={{1,2},{2,1},{3,4},{4,3},{5,6},{6,5},{7,8},{8,7},{9,10},{10,9},{11,... | collective-permute-start | bytes 589832 | tf_op jit(solution)/shard_map/ppermute | solution.py:318
  24.9 5.3 %collective-permute-start.3 = (f32[96,512]{1,0:T(8,128)S(1)}, f32[96,512]{1,0:T(8,128)S(1)}, u32[]{:S(2)}, u32[]{:S(2)}) collective-permute-start(f32[96,512]{1,0:T(8,128)S(1)} %get-tuple-element.28), channel_id=1, source_target_pairs={{0,1},{1,0},{2,3},{3,2},{4,5},{5,4},{6,7},{7,6},{8,9},{9,8},{10,11... | collective-permute-start | bytes 589832 | tf_op jit(solution)/shard_map/ppermute | solution.py:317
  30.2 0.0 copy-done.1
  30.2 0.0 copy-done.2
  30.2 3.5 %rows.1 = (f32[1024,512]{1,0:T(8,128)S(1)}, f32[4,8,512]{2,1,0:T(8,128)S(1)}, f32[4,512]{1,0:T(4,128)S(1)}, f32[8,128]{1,0:T(8,128)S(1)}) custom-call(f32[1024,512]{1,0:T(8,128)S(1)} %get-tuple-element.29.w_ref, f32[96,512]{1,0:T(8,128)S(1)} %collective-permute-done.got_l_ref, f32[96,512]{1,0:T(8,128)S(1)} %collective-permute-done.1.got_r_ref, ...), custom_call_target="tpu_custom_call" | custom-call | flops 40000000 | bytes 4194304 | tf_op jit(solution)/shard_map/rows/pallas_call | solution.py:387
  33.7 0.0 collective-permute-done.2.outer_ref
  33.7 0.0 collective-permute-done.3.inner_ref
  33.7 1.0 %final.1 = (f32[1024,512]{1,0:T(8,128)S(1)}, f32[16,1,128]{2,1,0:T(1,128)S(1)}) custom-call(f32[96,512]{1,0:T(8,128)S(1)} %collective-permute-done.2.outer_ref, f32[96,512]{1,0:T(8,128)S(1)} %collective-permute-done.3.inner_ref, f32[4,8,512]{2,1,0:T(8,128)S(1)} %get-tuple-element.30.acc_in, ...), custom_call_target="tpu_custom_call", output_to_operand_aliasing={{0}: (5, {})} | custom-call | tf_op jit(solution)/shard_map/final/pallas_call | solution.py:402
  34.8 12.4 %all_to_all.10.parts_ref = f32[16,1,128]{2,1,0:T(1,128)S(1)} all-to-all(f32[16,1,128]{2,1,0:T(1,128)S(1)} %get-tuple-element.35), channel_id=1, replica_groups=mesh['z'=8,'y_lo'=2,'y_hi'=4,'x'=4,'core'=2] {'y_hi','y_lo','core'}, dimensions={0} | all-to-all | bytes 16384 | tf_op jit(solution)/shard_map/all_to_all | solution.py:411
  47.2 0.6 spread.1
  47.8 8.9 %all-to-all-start.1 = ((f32[32,1,128]{2,1,0:T(1,128)}), f32[32,1,128]{2,1,0:T(1,128)S(1)}, u32[]{:S(2)}, u32[]{:S(2)}) async-start(f32[32,1,128]{2,1,0:T(1,128)} %spread.1), calls=%async_computation.1 | async-start | bytes 32768 | tf_op jit(solution)/shard_map/all_to_all | solution.py:412
  56.7 1.3 %copy.8 = f32[32,32,512]{2,1,0:T(8,128)} copy(f32[32,32,512]{2,1,0:T(8,128)S(1)} %bitcast.6) | data formatting | bytes 4194304
  58.0 7.3 %all-to-all-done.1 = f32[32,1,128]{2,1,0:T(1,128)S(1)} async-done(((f32[32,1,128]{2,1,0:T(1,128)}), f32[32,1,128]{2,1,0:T(1,128)S(1)}, u32[]{:S(2)}, u32[]{:S(2)}) %all-to-all-start.1) | async-done | bytes 16416 | tf_op jit(solution)/shard_map/all_to_all | solution.py:412
  65.4 0.1 reduce_sum.11
  65.4 0.7 %reshape_squeeze.3 = f32[4,16]{1,0:T(4,128)} reshape(f32[64]{0:T(128)S(1)} %slice_reduce_fusion) | data formatting | bytes 512 | tf_op jit(solution)/shard_map/reshape;squeeze | solution.py:413
  (1 shorter events, 0.0 us)
Async XLA Ops:
  0.6 15.8 %copy-start = (f32[32,32,512]{2,1,0:T(8,128)S(1)}, f32[32,32,512]{2,1,0:T(8,128)}, u32[]{:S(2)}) copy-start(f32[32,32,512]{2,1,0:T(8,128)} %param.4) | copy-start | bytes 6291460
  1.9 28.3 %copy-start.1 = (s32[1,1,2]{2,1,0:T(1,128)S(1)}, s32[1,1,2]{2,1,0:T(1,128)}, u32[]{:S(2)}) copy-start(s32[1,1,2]{2,1,0:T(1,128)} %param.5) | copy-start | bytes 28
  1.9 28.3 %copy-start.2 = (s32[1,1,2]{2,1,0:T(1,128)S(1)}, s32[1,1,2]{2,1,0:T(1,128)}, u32[]{:S(2)}) copy-start(s32[1,1,2]{2,1,0:T(1,128)} %param.6) | copy-start | bytes 28
  2.0 18.4 %collective-permute-start = (f32[96,512]{1,0:T(8,128)S(1)}, f32[96,512]{1,0:T(8,128)S(1)}, u32[]{:S(2)}, u32[]{:S(2)}) collective-permute-start(f32[96,512]{1,0:T(8,128)S(1)} %get-tuple-element.21), channel_id=1, source_target_pairs={{0,32},{32,64},{64,96},{96,128},{128,160},{160,192},{192,224},{224... | collective-permute-start | bytes 589832 | tf_op jit(solution)/shard_map/ppermute | solution.py:312
  6.0 14.3 %collective-permute-start.1 = (f32[96,512]{1,0:T(8,128)S(1)}, f32[96,512]{1,0:T(8,128)S(1)}, u32[]{:S(2)}, u32[]{:S(2)}) collective-permute-start(f32[96,512]{1,0:T(8,128)S(1)} %get-tuple-element.22), channel_id=1, source_target_pairs={{0,480},{32,0},{64,32},{96,64},{128,96},{160,128},{192,160},{224,1... | collective-permute-start | bytes 589832 | tf_op jit(solution)/shard_map/ppermute | solution.py:312
  20.7 13.0 %collective-permute-start.2 = (f32[96,512]{1,0:T(8,128)S(1)}, f32[96,512]{1,0:T(8,128)S(1)}, u32[]{:S(2)}, u32[]{:S(2)}) collective-permute-start(f32[96,512]{1,0:T(8,128)S(1)} %get-tuple-element.27), channel_id=1, source_target_pairs={{1,2},{2,1},{3,4},{4,3},{5,6},{6,5},{7,8},{8,7},{9,10},{10,9},{11,... | collective-permute-start | bytes 589832 | tf_op jit(solution)/shard_map/ppermute | solution.py:318
  24.9 8.8 %collective-permute-start.3 = (f32[96,512]{1,0:T(8,128)S(1)}, f32[96,512]{1,0:T(8,128)S(1)}, u32[]{:S(2)}, u32[]{:S(2)}) collective-permute-start(f32[96,512]{1,0:T(8,128)S(1)} %get-tuple-element.28), channel_id=1, source_target_pairs={{0,1},{1,0},{2,3},{3,2},{4,5},{5,4},{6,7},{7,6},{8,9},{9,8},{10,11... | collective-permute-start | bytes 589832 | tf_op jit(solution)/shard_map/ppermute | solution.py:317
  47.8 17.6 %all-to-all-start.1 = ((f32[32,1,128]{2,1,0:T(1,128)}), f32[32,1,128]{2,1,0:T(1,128)S(1)}, u32[]{:S(2)}, u32[]{:S(2)}) async-start(f32[32,1,128]{2,1,0:T(1,128)} %spread.1), calls=%async_computation.1 | async-start | bytes 32768 | tf_op jit(solution)/shard_map/all_to_all | solution.py:412

commit v7 on v5

--- a/solution.py
+++ b/solution.py
@@ -12,8 +12,8 @@
 GROUPS = 16
 ROW = ("z", "y_lo")
 COL = ("y_hi", "x", "core")
-FIRST = ("y_hi", "y_lo", "core")
-SECOND = ("z", "x")
+FIRST = ("z", "core")
+SECOND = ("y_hi", "y_lo", "x")
 LEVELS = (0.25, 0.5, 1.0, 2.0)
 A, B, C, G = 0.5625, 0.0625, 0.28125, 0.03125
 F32 = jnp.float32
@@ -194,7 +194,7 @@
     return [a + jnp.maximum(m - lim, 0.0) for a, lim in zip(acc, limits)]
 
 
-def rows_kernel(nx, ny, w_ref, got_o_ref, got_i_ref, table_ref, cut_ref, group_ref, out_ref, acc_ref, lim_ref, hot_ref, halo, fixed_ref):
+def rows_kernel(nx, ny, w_ref, got_o_ref, got_i_ref, table_ref, cut_ref, group_ref, out_ref, edge_ref, acc_ref, lim_ref, hot_ref, halo, fixed_ref, mid, sems):
     size = w_ref.shape[1]
     blocks = cut_ref.shape[1]
     lane = lax.broadcasted_iota(jnp.int32, (1, size), 1)
@@ -240,7 +240,9 @@
 
     def plane(src, at_plane, x, even_plane):
         v = lift(src, at_plane)
-        out_ref[pl.ds(pl.multiple_of(x * ny, 8), ny), :] = v
+        edge_ref[pl.ds(pl.multiple_of(x * 16, 8), 8), :] = v[0:8, :]
+        edge_ref[pl.ds(pl.multiple_of(x * 16 + 8, 8), 8), :] = v[ny - 8 : ny, :]
+        mid[x] = v[8 : ny - 8, :]
         limits = [jnp.broadcast_to(lim_ref[l : l + 1, :], (8, size)) for l in range(4)]
         acc = [acc_ref[l] for l in range(4)]
         for t in range(1, ny // 8 - 1):
@@ -248,7 +250,11 @@
         for l in range(4):
             acc_ref[l] = acc[l]
 
-    for src, start, x0, each in ((fixed_ref, 0, 0, 6), (w_ref, 6, 6, nx - 12), (fixed_ref, 6, nx - 6, 6)):
+    copies = []
+    middle = (nx - 12) // 2
+    for n, (src, start, x0, each) in enumerate(
+        ((fixed_ref, 0, 0, 6), (w_ref, 6, 6, middle), (w_ref, 6 + middle, 6 + middle, middle), (fixed_ref, 6, nx - 6, 6))
+    ):
 
         def pair(j, _):
             plane(src, start + 2 * j, x0 + 2 * j, True)
@@ -256,9 +262,15 @@
             return 0
 
         lax.fori_loop(0, each // 2, pair, 0)
-
-
-def final_kernel(nx, ny, scale, outer_ref, inner_ref, acc_in, lim_ref, hot_ref, base_ref, out_ref, mass_ref, acc_ref):
+        part = pl.ds(x0, each)
+        copies.append(pltpu.make_async_copy(mid.at[part], out_ref.at[part, pl.ds(8, ny - 16), :], sems.at[n]))
+        copies[-1].start()
+    for copy in copies:
+        copy.wait()
+
+
+def final_kernel(nx, ny, scale, outer_ref, inner_ref, acc_in, lim_ref, hot_ref, base_ref, out_in, out_ref, mass_ref, acc_ref, done, sems):
+    del out_in
     size = base_ref.shape[1]
     from_l, from_r = edge_weights(size)
     acc_ref[...] = acc_in[...]
@@ -271,12 +283,11 @@
         outer = [outer_ref[pl.ds(k * nx + x, 1), :] for k in range(3)]
         left = [jnp.where(even, o, i) for i, o in zip(inner, outer)]
         right = [jnp.where(even, i, o) for i, o in zip(inner, outer)]
-        for got, table, at in ((left, from_l, 0), (right, from_r, ny - 8)):
-            part = pl.ds(pl.multiple_of(x * ny + at, 8), 8)
-            v = base_ref[part, :]
+        for n, got, table in ((0, left, from_l), (1, right, from_r)):
+            v = base_ref[pl.ds(pl.multiple_of(x * 16 + 8 * n, 8), 8), :]
             for k in range(3):
                 v = v + table[k] * got[k]
-            out_ref[part, :] = v
+            done[n, x] = v
             acc = excess(acc, v, even_plane, limits)
         for l in range(4):
             acc_ref[l] = acc[l]
@@ -286,7 +297,15 @@
         tiles(2 * j + 1, False)
         return 0
 
-    lax.fori_loop(0, nx // 2, pair, 0, unroll=2)
+    copies = []
+    start = 0
+    for i, stop in enumerate((nx // 4, nx // 2, 3 * nx // 4, nx - 4, nx)):
+        lax.fori_loop(start // 2, stop // 2, pair, 0, unroll=2)
+        part = pl.ds(start, stop - start)
+        for n, at in enumerate((0, ny - 8)):
+            copies.append(pltpu.make_async_copy(done.at[n, part], out_ref.at[part, pl.ds(at, 8), :], sems.at[2 * i + n]))
+            copies[-1].start()
+        start = stop
     blocks = 2
     width = size // blocks
     lines = []
@@ -297,6 +316,8 @@
     line = jnp.sum((sums * scale) * hot_ref[...], axis=0, keepdims=True)
     for i in range(mass_ref.shape[0]):
         mass_ref[i] = line
+    for copy in copies:
+        copy.wait()
 
 
 def spread_kernel(parts_ref, out_ref):
@@ -376,30 +397,45 @@
     outer, inner = exchange(outer, inner, COL)
     rows = pl.pallas_call(
         functools.partial(rows_kernel, nx, ny),
-        out_shape=(in_vmem((nx * ny, size)), in_vmem((4, 8, size)), in_vmem((4, size)), in_vmem((8, 128))),
+        out_shape=(
+            jax.ShapeDtypeStruct((nx, ny, size), F32),
+            in_vmem((nx * 16, size)),
+            in_vmem((4, 8, size)),
+            in_vmem((4, size)),
+            in_vmem((8, 128)),
+        ),
         in_specs=[VMEM] * 6,
-        out_specs=(VMEM,) * 4,
-        scratch_shapes=[pltpu.VMEM((6 * ny, size), F32), pltpu.VMEM((12 * ny, size), F32)],
+        out_specs=(ANY, *(VMEM,) * 4),
+        scratch_shapes=[
+            pltpu.VMEM((6 * ny, size), F32),
+            pltpu.VMEM((12 * ny, size), F32),
+            pltpu.VMEM((nx, ny - 16, size), F32),
+            pltpu.SemaphoreType.DMA((4,)),
+        ],
         cost_estimate=cost(40_000_000),
         compiler_params=PARAMS,
         name="rows",
     )
-    base, acc, limits, hot = rows(
+    coeffs, base, acc, limits, hot = rows(
         *near(work, got_outer, got_inner, table, cut_exponent.reshape(1, blocks_z), group_map.reshape(1, blocks_z))
     )
     n_first, n_second = lax.axis_size(FIRST), lax.axis_size(SECOND)
     scale = 1.0 / (nx * ny * (size // blocks_z))
     final = pl.pallas_call(
         functools.partial(final_kernel, nx, ny, scale),
-        out_shape=(in_vmem((nx * ny, size)), in_vmem((n_first, 1, 128))),
-        in_specs=[VMEM] * 6,
-        out_specs=(VMEM, VMEM),
-        input_output_aliases={5: 0},
-        scratch_shapes=[pltpu.VMEM((4, 8, size), F32)],
+        out_shape=(jax.ShapeDtypeStruct((nx, ny, size), F32), in_vmem((n_first, 1, 128))),
+        in_specs=[VMEM] * 6 + [ANY],
+        out_specs=(ANY, VMEM),
+        input_output_aliases={6: 0},
+        scratch_shapes=[
+            pltpu.VMEM((4, 8, size), F32),
+            pltpu.VMEM((2, nx, 8, size), F32),
+            pltpu.SemaphoreType.DMA((10,)),
+        ],
         compiler_params=PARAMS,
         name="final",
     )
-    coeffs, mass = final(*near(outer, inner, acc, limits, hot, base))
+    coeffs, mass = final(*near(outer, inner, acc, limits, hot, base), coeffs)
     spread = pl.pallas_call(
         spread_kernel,
         out_shape=in_vmem((n_second, 1, 128)),
@@ -410,7 +446,7 @@
     )
     mass = spread(*near(lax.all_to_all(mass, FIRST, 0, 0)))
     mass = lax.all_to_all(mass, SECOND, 0, 0).sum(0)
-    return coeffs.reshape(nx, ny, size), mass[0, : 4 * GROUPS].reshape(4, GROUPS).T
+    return coeffs, mass[0, : 4 * GROUPS].reshape(4, GROUPS).T
 
 
 def solution(mesh):

time: 65.8 us -> 65.2 us (level)
  blocking collectives: 14.9 us -> 26 us
  waiting for transfers between devices: 9.23 us -> 1.93 us
  starting transfers between devices: 27.7 us -> 23.9 us
  local copies, waits for them, and re-layouts: 2.02 us -> 0.7 us
  Pallas kernels: 10.7 us -> 11.5 us
    all_to_all x0 -> x1, blocking collectives: none -> 14.4 us  [shards(): mass = lax.all_to_all(mass, SECOND, 0, 0).sum(0)]
    all_to_all x1 -> x0, waiting for transfers between devices: 7.29 us -> none  [shards(): mass = lax.all_to_all(mass, SECOND, 0, 0).sum(0)]
    all_to_all x1 -> x0, starting transfers between devices: 3.84 us -> none  [shards(): mass = lax.all_to_all(mass, SECOND, 0, 0).sum(0)]
    all_to_all x1, blocking collectives: 14.9 us -> 11.6 us  [shards(): mass = spread(*near(lax.all_to_all(mass, FIRST, 0, 0)))]
    unnamed x7 -> x6, local copies, waits for them, and re-layouts: 1.34 us -> 0.02 us
    pallas_call x1, Pallas kernels: 3.46 us -> 4.17 us  [shards(): rows(*near(work, got_outer, got_inner, table, cut_exponent.reshape(1, blo...]
    pallas_call x1, Pallas kernels: 1.02 us -> 1.7 us  [shards(): coeffs, mass = final(*near(outer, inner, acc, limits, hot, base), coeffs)]
  transfers between devices with their start and end apart: 5 -> 4, of which waited for: 2 -> 1; matrix products, arithmetic and copies ran while one was open for 2% -> 0% of each run, Pallas kernels for 11% -> 12%
where the time goes in v7:
time: 65.2 us; the launch traced here: 64.9 us
  blocking collectives  26 us (40%)
  starting transfers between devices  23.9 us (37%)
  Pallas kernels  11.5 us (18%)
  waiting for transfers between devices  1.93 us (3%)
  between operations  0.78 us (1%)
  local copies, waits for them, and re-layouts  0.7 us (1%)
    ppermute x2, starting transfers between devices, exchange(): return (lax.ppermute(outer, axes, swap_outer), inner)  17 us
    all_to_all x1, blocking collectives, shards(): mass = lax.all_to_all(mass, SECOND, 0, 0).sum(0)  14.4 us
    all_to_all x1, blocking collectives, shards(): mass = spread(*near(lax.all_to_all(mass, FIRST, 0, 0)))  11.6 us
    ppermute x2, starting transfers between devices, exchange(): inner = lax.ppermute(inner, axes, swap_inner)  6.87 us
    pallas_call x1, Pallas kernels, shards(): rows(*near(work, got_outer, got_inner, table, cut_exponent.reshape(1, blo...  4.17 us
    pallas_call x1, Pallas kernels, shards(): work, inner, outer, table = bulk(*near(later), far(table))  3.9 us
    ppermute x2, waiting for transfers between devices, exchange(): inner = lax.ppermute(inner, axes, swap_inner)  1.93 us
    pallas_call x1, Pallas kernels, shards(): coeffs, mass = final(*near(outer, inner, acc, limits, hot, base), coeffs)  1.7 us
  transfers between devices with their start and end apart: 4, of which 1 were waited for; matrix products, arithmetic and copies ran while one was open for 0% of the time, Pallas kernels for 12%

profile of v7, /device:TPU:1, one launch (start us, length us, event | category | flops | bytes accessed | tf_op | source)
XLA Modules:
  0.0 64.9 jit_solution(12914429488657618431)
XLA Ops:
  0.6 0.0 copy-start
  0.6 1.3 %edge.1 = (f32[96,512]{1,0:T(8,128)S(1)}, f32[96,512]{1,0:T(8,128)S(1)}) custom-call(f32[1024,512]{1,0:T(8,128)} %bitcast.5), custom_call_target="tpu_custom_call" | custom-call | tf_op jit(solution)/shard_map/edge/pallas_call | solution.py:368
  2.0 0.0 copy-start.1
  2.0 0.0 copy-start.2
  2.0 12.5 %collective-permute-start = (f32[96,512]{1,0:T(8,128)S(1)}, f32[96,512]{1,0:T(8,128)S(1)}, u32[]{:S(2)}, u32[]{:S(2)}) collective-permute-start(f32[96,512]{1,0:T(8,128)S(1)} %get-tuple-element.22), channel_id=1, source_target_pairs={{32,64},{64,32},{96,128},{128,96},{160,192},{192,160},{224,256},{2... | collective-permute-start | bytes 589832 | tf_op jit(solution)/shard_map/ppermute | solution.py:339
  14.5 1.9 %collective-permute-start.1 = (f32[96,512]{1,0:T(8,128)S(1)}, f32[96,512]{1,0:T(8,128)S(1)}, u32[]{:S(2)}, u32[]{:S(2)}) collective-permute-start(f32[96,512]{1,0:T(8,128)S(1)} %get-tuple-element.23), channel_id=1, source_target_pairs={{0,32},{32,0},{64,96},{96,64},{128,160},{160,128},{192,224},{224,1... | collective-permute-start | bytes 589832 | tf_op jit(solution)/shard_map/ppermute | solution.py:338
  16.4 0.0 copy-done
  16.4 3.9 %bulk.1 = (f32[1024,512]{1,0:T(8,128)S(1)}, f32[96,512]{1,0:T(8,128)S(1)}, f32[96,512]{1,0:T(8,128)S(1)}, bf16[512,512]{1,0:T(8,128)(2,1)S(1)}) custom-call(f32[1024,512]{1,0:T(8,128)S(1)} %bitcast.6, bf16[512,512]{1,0:T(8,128)(2,1)} %constant.4.clone.table_hbm), custom_call_target="tpu_custom_call" | custom-call | flops 40000000 | bytes 4194304 | tf_op jit(solution)/shard_map/bulk/pallas_call | solution.py:386
  20.3 0.0 collective-permute-done.got_o_ref
  20.3 1.9 %collective-permute-done.1.got_i_ref = f32[96,512]{1,0:T(8,128)S(1)} collective-permute-done((f32[96,512]{1,0:T(8,128)S(1)}, f32[96,512]{1,0:T(8,128)S(1)}, u32[]{:S(2)}, u32[]{:S(2)}) %collective-permute-start.1) | collective-permute-done | bytes 196640 | tf_op jit(solution)/shard_map/ppermute | solution.py:338
  22.3 0.4 plane.1
  22.7 4.5 %collective-permute-start.2 = (f32[96,512]{1,0:T(8,128)S(1)}, f32[96,512]{1,0:T(8,128)S(1)}, u32[]{:S(2)}, u32[]{:S(2)}) collective-permute-start(f32[96,512]{1,0:T(8,128)S(1)} %get-tuple-element.28), channel_id=1, source_target_pairs={{1,2},{2,1},{3,4},{4,3},{5,6},{6,5},{7,8},{8,7},{9,10},{10,9},{11,... | collective-permute-start | bytes 589832 | tf_op jit(solution)/shard_map/ppermute | solution.py:339
  27.2 4.9 %collective-permute-start.3 = (f32[96,512]{1,0:T(8,128)S(1)}, f32[96,512]{1,0:T(8,128)S(1)}, u32[]{:S(2)}, u32[]{:S(2)}) collective-permute-start(f32[96,512]{1,0:T(8,128)S(1)} %get-tuple-element.29), channel_id=1, source_target_pairs={{0,1},{1,0},{2,3},{3,2},{4,5},{5,4},{6,7},{7,6},{8,9},{9,8},{10,11... | collective-permute-start | bytes 589832 | tf_op jit(solution)/shard_map/ppermute | solution.py:338
  32.2 0.0 copy-done.1
  32.2 0.0 copy-done.2
  32.2 4.2 %rows.1 = (f32[32,32,512]{2,1,0:T(8,128)}, f32[512,512]{1,0:T(8,128)S(1)}, f32[4,8,512]{2,1,0:T(8,128)S(1)}, f32[4,512]{1,0:T(4,128)S(1)}, f32[8,128]{1,0:T(8,128)S(1)}) custom-call(f32[1024,512]{1,0:T(8,128)S(1)} %get-tuple-element.30.w_ref, f32[96,512]{1,0:T(8,128)S(1)} %collective-permute-done.got_o_ref, f32[96,512]{1,0:T(8,128)S(1)} %collective-permute-done.1.got_i_ref, ...), custom_call_target="tpu_custom_call" | custom-call | flops 40000000 | bytes 4194304 | tf_op jit(solution)/shard_map/rows/pallas_call | solution.py:419
  36.4 0.0 collective-permute-done.2.outer_ref
  36.4 0.0 collective-permute-done.3.inner_ref
  36.4 1.7 %final.1 = (f32[32,32,512]{2,1,0:T(8,128)}, f32[16,1,128]{2,1,0:T(1,128)S(1)}) custom-call(f32[96,512]{1,0:T(8,128)S(1)} %collective-permute-done.2.outer_ref, f32[96,512]{1,0:T(8,128)S(1)} %collective-permute-done.3.inner_ref, f32[4,8,512]{2,1,0:T(8,128)S(1)} %get-tuple-element.31.acc_in, ...), custom_call_target="tpu_custom_call", output_to_operand_aliasing={{0}: (6, {})} | custom-call | tf_op jit(solution)/shard_map/final/pallas_call | solution.py:438
  38.1 11.6 %all_to_all.10.parts_ref = f32[16,1,128]{2,1,0:T(1,128)S(1)} all-to-all(f32[16,1,128]{2,1,0:T(1,128)S(1)} %get-tuple-element.37), channel_id=1, replica_groups=mesh['z'=8,'y_lo'=2,'y_hi'=4,'x'=4,'core'=2] {'z','core'}, dimensions={0} | all-to-all | bytes 16384 | tf_op jit(solution)/shard_map/all_to_all | solution.py:447
  49.7 14.4 %all_to_all.11 = f32[32,1,128]{2,1,0:T(1,128)S(1)} all-to-all(f32[32,1,128]{2,1,0:T(1,128)S(1)} %spread.1), channel_id=1, replica_groups=mesh['z'=8,'y_lo'=2,'y_hi'=4,'x'=4,'core'=2] {'y_hi','y_lo','x'}, dimensions={0} | all-to-all | bytes 32768 | tf_op jit(solution)/shard_map/all_to_all | solution.py:448
  64.2 0.1 reduce_sum.11
  64.2 0.7 %reshape_squeeze.3 = f32[4,16]{1,0:T(4,128)} reshape(f32[64]{0:T(128)S(1)} %slice_reduce_fusion) | data formatting | bytes 512 | tf_op jit(solution)/shard_map/reshape;squeeze | solution.py:449
  (2 shorter events, 0.0 us)
Async XLA Ops:
  0.6 15.8 %copy-start = (f32[32,32,512]{2,1,0:T(8,128)S(1)}, f32[32,32,512]{2,1,0:T(8,128)}, u32[]{:S(2)}) copy-start(f32[32,32,512]{2,1,0:T(8,128)} %param.4) | copy-start | bytes 6291460
  2.0 30.2 %copy-start.1 = (s32[1,1,2]{2,1,0:T(1,128)S(1)}, s32[1,1,2]{2,1,0:T(1,128)}, u32[]{:S(2)}) copy-start(s32[1,1,2]{2,1,0:T(1,128)} %param.5) | copy-start | bytes 28
  2.0 30.2 %copy-start.2 = (s32[1,1,2]{2,1,0:T(1,128)S(1)}, s32[1,1,2]{2,1,0:T(1,128)}, u32[]{:S(2)}) copy-start(s32[1,1,2]{2,1,0:T(1,128)} %param.6) | copy-start | bytes 28
  2.0 18.4 %collective-permute-start = (f32[96,512]{1,0:T(8,128)S(1)}, f32[96,512]{1,0:T(8,128)S(1)}, u32[]{:S(2)}, u32[]{:S(2)}) collective-permute-start(f32[96,512]{1,0:T(8,128)S(1)} %get-tuple-element.22), channel_id=1, source_target_pairs={{32,64},{64,32},{96,128},{128,96},{160,192},{192,160},{224,256},{2... | collective-permute-start | bytes 589832 | tf_op jit(solution)/shard_map/ppermute | solution.py:339
  14.5 7.8 %collective-permute-start.1 = (f32[96,512]{1,0:T(8,128)S(1)}, f32[96,512]{1,0:T(8,128)S(1)}, u32[]{:S(2)}, u32[]{:S(2)}) collective-permute-start(f32[96,512]{1,0:T(8,128)S(1)} %get-tuple-element.23), channel_id=1, source_target_pairs={{0,32},{32,0},{64,96},{96,64},{128,160},{160,128},{192,224},{224,1... | collective-permute-start | bytes 589832 | tf_op jit(solution)/shard_map/ppermute | solution.py:338
  22.7 13.7 %collective-permute-start.2 = (f32[96,512]{1,0:T(8,128)S(1)}, f32[96,512]{1,0:T(8,128)S(1)}, u32[]{:S(2)}, u32[]{:S(2)}) collective-permute-start(f32[96,512]{1,0:T(8,128)S(1)} %get-tuple-element.28), channel_id=1, source_target_pairs={{1,2},{2,1},{3,4},{4,3},{5,6},{6,5},{7,8},{8,7},{9,10},{10,9},{11,... | collective-permute-start | bytes 589832 | tf_op jit(solution)/shard_map/ppermute | solution.py:339
  27.2 9.2 %collective-permute-start.3 = (f32[96,512]{1,0:T(8,128)S(1)}, f32[96,512]{1,0:T(8,128)S(1)}, u32[]{:S(2)}, u32[]{:S(2)}) collective-permute-start(f32[96,512]{1,0:T(8,128)S(1)} %get-tuple-element.29), channel_id=1, source_target_pairs={{0,1},{1,0},{2,3},{3,2},{4,5},{5,4},{6,7},{7,6},{8,9},{9,8},{10,11... | collective-permute-start | bytes 589832 | tf_op jit(solution)/shard_map/ppermute | solution.py:338

commit v8 on v7

--- a/solution.py
+++ b/solution.py
@@ -24,17 +24,6 @@
 
 def in_vmem(shape, dtype=F32):
     return pltpu.VMEM(shape, dtype)
-
-
-def lane_lift(v):
-    size = v.shape[-1]
-    odd = lax.broadcasted_iota(jnp.int32, v.shape, 1) % 2 == 1
-    near = pltpu.roll(v, 1, axis=1) + pltpu.roll(v, size - 1, axis=1)
-    far = pltpu.roll(v, 3, axis=1) + pltpu.roll(v, size - 3, axis=1)
-    w = jnp.where(odd, v - (A * near - B * far), v)
-    near = pltpu.roll(w, 1, axis=1) + pltpu.roll(w, size - 1, axis=1)
-    far = pltpu.roll(w, 3, axis=1) + pltpu.roll(w, size - 3, axis=1)
-    return jnp.where(odd, w, w + (C * near - G * far))
 
 
 def lane_table(size):
@@ -269,43 +258,53 @@
         copy.wait()
 
 
-def final_kernel(nx, ny, scale, outer_ref, inner_ref, acc_in, lim_ref, hot_ref, base_ref, out_in, out_ref, mass_ref, acc_ref, done, sems):
+def side_tiles(nx, ny, at_tail, got_ref, acc_in, lim_ref, base_ref, out_ref, acc_ref, done, sems, stops):
+    size = base_ref.shape[1]
+    table = [jnp.where(at_tail, r, l) for l, r in zip(*edge_weights(size))]
+    offset = jnp.where(at_tail, 8, 0)
+    acc_ref[...] = acc_in[...]
+
+    def tile(x, even_plane, acc, limits):
+        v = base_ref[pl.ds(pl.multiple_of(x * 16 + offset, 8), 8), :]
+        for k in range(3):
+            v = v + table[k] * got_ref[pl.ds(k * nx + x, 1), :]
+        done[x] = v
+        return excess(acc, v, even_plane, limits)
+
+    def pair(j, _):
+        limits = [jnp.broadcast_to(lim_ref[l : l + 1, :], (8, size)) for l in range(4)]
+        acc = tile(2 * j, True, [acc_ref[l] for l in range(4)], limits)
+        acc = tile(2 * j + 1, False, acc, limits)
+        for l in range(4):
+            acc_ref[l] = acc[l]
+        return 0
+
+    copies = []
+    start = 0
+    for i, stop in enumerate(stops):
+        lax.fori_loop(start // 2, stop // 2, pair, 0, unroll=2)
+        part = pl.ds(start, stop - start)
+        rows = pl.ds(pl.multiple_of(jnp.where(at_tail, ny - 8, 0), 8), 8)
+        copies.append(pltpu.make_async_copy(done.at[part], out_ref.at[part, rows, :], sems.at[i]))
+        copies[-1].start()
+        start = stop
+    return copies
+
+
+def inner_kernel(nx, ny, got_ref, acc_in, lim_ref, base_ref, out_in, out_ref, acc_ref, done, sems):
+    del out_in
+    at_tail = lax.axis_index("core") == 0
+    stops = (nx // 2, nx)
+    for copy in side_tiles(nx, ny, at_tail, got_ref, acc_in, lim_ref, base_ref, out_ref, acc_ref, done, sems, stops):
+        copy.wait()
+
+
+def outer_kernel(nx, ny, scale, got_ref, acc_in, lim_ref, base_ref, hot_ref, out_in, out_ref, mass_ref, acc_ref, done, sems):
     del out_in
     size = base_ref.shape[1]
-    from_l, from_r = edge_weights(size)
-    acc_ref[...] = acc_in[...]
-    even = lax.axis_index("core") == 0
-
-    def tiles(x, even_plane):
-        limits = [jnp.broadcast_to(lim_ref[l : l + 1, :], (8, size)) for l in range(4)]
-        acc = [acc_ref[l] for l in range(4)]
-        inner = [inner_ref[pl.ds(k * nx + x, 1), :] for k in range(3)]
-        outer = [outer_ref[pl.ds(k * nx + x, 1), :] for k in range(3)]
-        left = [jnp.where(even, o, i) for i, o in zip(inner, outer)]
-        right = [jnp.where(even, i, o) for i, o in zip(inner, outer)]
-        for n, got, table in ((0, left, from_l), (1, right, from_r)):
-            v = base_ref[pl.ds(pl.multiple_of(x * 16 + 8 * n, 8), 8), :]
-            for k in range(3):
-                v = v + table[k] * got[k]
-            done[n, x] = v
-            acc = excess(acc, v, even_plane, limits)
-        for l in range(4):
-            acc_ref[l] = acc[l]
-
-    def pair(j, _):
-        tiles(2 * j, True)
-        tiles(2 * j + 1, False)
-        return 0
-
-    copies = []
-    start = 0
-    for i, stop in enumerate((nx // 4, nx // 2, 3 * nx // 4, nx - 4, nx)):
-        lax.fori_loop(start // 2, stop // 2, pair, 0, unroll=2)
-        part = pl.ds(start, stop - start)
-        for n, at in enumerate((0, ny - 8)):
-            copies.append(pltpu.make_async_copy(done.at[n, part], out_ref.at[part, pl.ds(at, 8), :], sems.at[2 * i + n]))
-            copies[-1].start()
-        start = stop
+    at_tail = lax.axis_index("core") != 0
+    stops = (nx // 4, nx // 2, 3 * nx // 4, nx)
+    copies = side_tiles(nx, ny, at_tail, got_ref, acc_in, lim_ref, base_ref, out_ref, acc_ref, done, sems, stops)
     blocks = 2
     width = size // blocks
     lines = []
@@ -335,8 +334,9 @@
 
 def exchange(outer, inner, axes):
     swap_inner, swap_outer = pair_swaps(lax.axis_size(axes))
+    outer = lax.ppermute(outer, axes, swap_outer)
     inner = lax.ppermute(inner, axes, swap_inner)
-    return lax.ppermute(outer, axes, swap_outer), inner
+    return outer, inner
 
 
 def near(*values):
@@ -421,21 +421,33 @@
     )
     n_first, n_second = lax.axis_size(FIRST), lax.axis_size(SECOND)
     scale = 1.0 / (nx * ny * (size // blocks_z))
-    final = pl.pallas_call(
-        functools.partial(final_kernel, nx, ny, scale),
+    inner_side = pl.pallas_call(
+        functools.partial(inner_kernel, nx, ny),
+        out_shape=(jax.ShapeDtypeStruct((nx, ny, size), F32), in_vmem((4, 8, size))),
+        in_specs=[VMEM] * 4 + [ANY],
+        out_specs=(ANY, VMEM),
+        input_output_aliases={4: 0},
+        scratch_shapes=[pltpu.VMEM((nx, 8, size), F32), pltpu.SemaphoreType.DMA((2,))],
+        cost_estimate=cost(10_000_000),
+        compiler_params=PARAMS,
+        name="inner_side",
+    )
+    coeffs, acc = inner_side(*near(inner, acc, limits, base), coeffs)
+    outer_side = pl.pallas_call(
+        functools.partial(outer_kernel, nx, ny, scale),
         out_shape=(jax.ShapeDtypeStruct((nx, ny, size), F32), in_vmem((n_first, 1, 128))),
-        in_specs=[VMEM] * 6 + [ANY],
+        in_specs=[VMEM] * 5 + [ANY],
         out_specs=(ANY, VMEM),
-        input_output_aliases={6: 0},
+        input_output_aliases={5: 0},
         scratch_shapes=[
             pltpu.VMEM((4, 8, size), F32),
-            pltpu.VMEM((2, nx, 8, size), F32),
-            pltpu.SemaphoreType.DMA((10,)),
+            pltpu.VMEM((nx, 8, size), F32),
+            pltpu.SemaphoreType.DMA((4,)),
         ],
         compiler_params=PARAMS,
-        name="final",
-    )
-    coeffs, mass = final(*near(outer, inner, acc, limits, hot, base), coeffs)
+        name="outer_side",
+    )
+    coeffs, mass = outer_side(*near(outer, acc, limits, base, hot), coeffs)
     spread = pl.pallas_call(
         spread_kernel,
         out_shape=in_vmem((n_second, 1, 128)),

time: 65.2 us -> 68 us (1.043)
  blocking collectives: 26 us -> 31.3 us
  starting transfers between devices: 23.9 us -> 20.9 us
    all_to_all x1, blocking collectives: 11.6 us -> 16 us  [shards(): mass = spread(*near(lax.all_to_all(mass, FIRST, 0, 0)))]
    ppermute x2, starting transfers between devices: 17 us -> 15.5 us  [exchange(): outer = lax.ppermute(outer, axes, swap_outer)]
    ppermute x2, starting transfers between devices: 6.87 us -> 5.36 us  [exchange(): inner = lax.ppermute(inner, axes, swap_inner)]
    all_to_all x1, blocking collectives: 14.4 us -> 15.3 us  [shards(): mass = lax.all_to_all(mass, SECOND, 0, 0).sum(0)]
    pallas_call x1 -> x2, Pallas kernels: 1.7 us -> 2.29 us  [the longest x1 1.16 us: shards(): coeffs, acc = inner_side(*near(inner, acc, limits, base), coeffs)]
  transfers between devices with their start and end apart: 4 -> 4, of which waited for: 1 -> 1; matrix products, arithmetic and copies ran while one was open for 0% -> 0% of each run, Pallas kernels for 12% -> 14%
where the time goes in v8:
time: 68 us; the launch traced here: 67.7 us
  blocking collectives  31.3 us (46%)
  starting transfers between devices  20.9 us (31%)
  Pallas kernels  12.1 us (18%)
  waiting for transfers between devices  1.93 us (3%)
  between operations  0.78 us (1%)
  local copies, waits for them, and re-layouts  0.7 us (1%)
    all_to_all x1, blocking collectives, shards(): mass = spread(*near(lax.all_to_all(mass, FIRST, 0, 0)))  16 us
    ppermute x2, starting transfers between devices, exchange(): outer = lax.ppermute(outer, axes, swap_outer)  15.5 us
    all_to_all x1, blocking collectives, shards(): mass = lax.all_to_all(mass, SECOND, 0, 0).sum(0)  15.3 us
    ppermute x2, starting transfers between devices, exchange(): inner = lax.ppermute(inner, axes, swap_inner)  5.36 us
    pallas_call x1, Pallas kernels, shards(): rows(*near(work, got_outer, got_inner, table, cut_exponent.reshape(1, blo...  4.17 us
    pallas_call x1, Pallas kernels, shards(): work, inner, outer, table = bulk(*near(later), far(table))  3.9 us
    ppermute x2, waiting for transfers between devices, exchange(): inner = lax.ppermute(inner, axes, swap_inner)  1.93 us
  transfers between devices with their start and end apart: 4, of which 1 were waited for; matrix products, arithmetic and copies ran while one was open for 0% of the time, Pallas kernels for 14%

profile of v8, /device:TPU:1, one launch (start us, length us, event | category | flops | bytes accessed | tf_op | source)
XLA Modules:
  0.0 67.7 jit_solution(2700350538903890873)
XLA Ops:
  0.6 0.0 copy-start
  0.6 1.3 %edge.1 = (f32[96,512]{1,0:T(8,128)S(1)}, f32[96,512]{1,0:T(8,128)S(1)}) custom-call(f32[1024,512]{1,0:T(8,128)} %bitcast.5), custom_call_target="tpu_custom_call" | custom-call | tf_op jit(solution)/shard_map/edge/pallas_call | solution.py:368
  2.0 0.0 copy-start.1
  2.0 0.0 copy-start.2
  2.0 12.5 %collective-permute-start = (f32[96,512]{1,0:T(8,128)S(1)}, f32[96,512]{1,0:T(8,128)S(1)}, u32[]{:S(2)}, u32[]{:S(2)}) collective-permute-start(f32[96,512]{1,0:T(8,128)S(1)} %get-tuple-element.24), channel_id=1, source_target_pairs={{32,64},{64,32},{96,128},{128,96},{160,192},{192,160},{224,256},{2... | collective-permute-start | bytes 589832 | tf_op jit(solution)/shard_map/ppermute | solution.py:337
  14.5 1.9 %collective-permute-start.1 = (f32[96,512]{1,0:T(8,128)S(1)}, f32[96,512]{1,0:T(8,128)S(1)}, u32[]{:S(2)}, u32[]{:S(2)}) collective-permute-start(f32[96,512]{1,0:T(8,128)S(1)} %get-tuple-element.25), channel_id=1, source_target_pairs={{0,32},{32,0},{64,96},{96,64},{128,160},{160,128},{192,224},{224,1... | collective-permute-start | bytes 589832 | tf_op jit(solution)/shard_map/ppermute | solution.py:338
  16.4 0.0 copy-done
  16.4 3.9 %bulk.1 = (f32[1024,512]{1,0:T(8,128)S(1)}, f32[96,512]{1,0:T(8,128)S(1)}, f32[96,512]{1,0:T(8,128)S(1)}, bf16[512,512]{1,0:T(8,128)(2,1)S(1)}) custom-call(f32[1024,512]{1,0:T(8,128)S(1)} %bitcast.6, bf16[512,512]{1,0:T(8,128)(2,1)} %constant.4.clone.table_hbm), custom_call_target="tpu_custom_call" | custom-call | flops 40000000 | bytes 4194304 | tf_op jit(solution)/shard_map/bulk/pallas_call | solution.py:386
  20.3 0.0 collective-permute-done.got_o_ref
  20.3 1.9 %collective-permute-done.1.got_i_ref = f32[96,512]{1,0:T(8,128)S(1)} collective-permute-done((f32[96,512]{1,0:T(8,128)S(1)}, f32[96,512]{1,0:T(8,128)S(1)}, u32[]{:S(2)}, u32[]{:S(2)}) %collective-permute-start.1) | collective-permute-done | bytes 196640 | tf_op jit(solution)/shard_map/ppermute | solution.py:338
  22.3 0.4 plane.1
  22.7 3.4 %collective-permute-start.3 = (f32[96,512]{1,0:T(8,128)S(1)}, f32[96,512]{1,0:T(8,128)S(1)}, u32[]{:S(2)}, u32[]{:S(2)}) collective-permute-start(f32[96,512]{1,0:T(8,128)S(1)} %get-tuple-element.31), channel_id=1, source_target_pairs={{0,1},{1,0},{2,3},{3,2},{4,5},{5,4},{6,7},{7,6},{8,9},{9,8},{10,11... | collective-permute-start | bytes 589832 | tf_op jit(solution)/shard_map/ppermute | solution.py:338
  26.1 3.0 %collective-permute-start.2 = (f32[96,512]{1,0:T(8,128)S(1)}, f32[96,512]{1,0:T(8,128)S(1)}, u32[]{:S(2)}, u32[]{:S(2)}) collective-permute-start(f32[96,512]{1,0:T(8,128)S(1)} %get-tuple-element.30), channel_id=1, source_target_pairs={{1,2},{2,1},{3,4},{4,3},{5,6},{6,5},{7,8},{8,7},{9,10},{10,9},{11,... | collective-permute-start | bytes 589832 | tf_op jit(solution)/shard_map/ppermute | solution.py:337
  29.1 0.0 copy-done.1
  29.1 0.0 copy-done.2
  29.2 4.2 %rows.1 = (f32[32,32,512]{2,1,0:T(8,128)}, f32[512,512]{1,0:T(8,128)S(1)}, f32[4,8,512]{2,1,0:T(8,128)S(1)}, f32[4,512]{1,0:T(4,128)S(1)}, f32[8,128]{1,0:T(8,128)S(1)}) custom-call(f32[1024,512]{1,0:T(8,128)S(1)} %get-tuple-element.32.w_ref, f32[96,512]{1,0:T(8,128)S(1)} %collective-permute-done.got_o_ref, f32[96,512]{1,0:T(8,128)S(1)} %collective-permute-done.1.got_i_ref, ...), custom_call_target="tpu_custom_call" | custom-call | flops 40000000 | bytes 4194304 | tf_op jit(solution)/shard_map/rows/pallas_call | solution.py:419
  33.3 0.0 collective-permute-done.3.got_ref
  33.3 1.2 %inner_side.1 = (f32[32,32,512]{2,1,0:T(8,128)}, f32[4,8,512]{2,1,0:T(8,128)S(1)}) custom-call(f32[96,512]{1,0:T(8,128)S(1)} %collective-permute-done.3.got_ref, f32[4,8,512]{2,1,0:T(8,128)S(1)} %get-tuple-element.33.acc_in, f32[4,512]{1,0:T(4,128)S(1)} %get-tuple-element.34.lim_ref, ...), custom_call_target="tpu_custom_call", output_to_operand_aliasing={{0}: (4, {})} | custom-call | flops 10000000 | bytes 4194304 | tf_op jit(solution)/shard_map/inner_side/pallas_call | solution.py:435
  34.5 0.0 collective-permute-done.2.got_ref
  34.5 1.1 %outer_side.1 = (f32[32,32,512]{2,1,0:T(8,128)}, f32[16,1,128]{2,1,0:T(1,128)S(1)}) custom-call(f32[96,512]{1,0:T(8,128)S(1)} %collective-permute-done.2.got_ref, f32[4,8,512]{2,1,0:T(8,128)S(1)} %get-tuple-element.37.acc_in, f32[4,512]{1,0:T(4,128)S(1)} %get-tuple-element.34.lim_ref, ...), custom_call_target="tpu_custom_call", output_to_operand_aliasing={{0}: (5, {})} | custom-call | tf_op jit(solution)/shard_map/outer_side/pallas_call | solution.py:450
  35.7 16.0 %all_to_all.10.parts_ref = f32[16,1,128]{2,1,0:T(1,128)S(1)} all-to-all(f32[16,1,128]{2,1,0:T(1,128)S(1)} %get-tuple-element.41), channel_id=1, replica_groups=mesh['z'=8,'y_lo'=2,'y_hi'=4,'x'=4,'core'=2] {'z','core'}, dimensions={0} | all-to-all | bytes 16384 | tf_op jit(solution)/shard_map/all_to_all | solution.py:459
  51.7 15.3 %all_to_all.11 = f32[32,1,128]{2,1,0:T(1,128)S(1)} all-to-all(f32[32,1,128]{2,1,0:T(1,128)S(1)} %spread.1), channel_id=1, replica_groups=mesh['z'=8,'y_lo'=2,'y_hi'=4,'x'=4,'core'=2] {'y_hi','y_lo','x'}, dimensions={0} | all-to-all | bytes 32768 | tf_op jit(solution)/shard_map/all_to_all | solution.py:460
  67.0 0.1 reduce_sum.11
  67.1 0.7 reshape_squeeze.3
  (2 shorter events, 0.0 us)
Async XLA Ops:
  0.6 15.8 %copy-start = (f32[32,32,512]{2,1,0:T(8,128)S(1)}, f32[32,32,512]{2,1,0:T(8,128)}, u32[]{:S(2)}) copy-start(f32[32,32,512]{2,1,0:T(8,128)} %param.4) | copy-start | bytes 6291460
  2.0 27.2 %copy-start.1 = (s32[1,1,2]{2,1,0:T(1,128)S(1)}, s32[1,1,2]{2,1,0:T(1,128)}, u32[]{:S(2)}) copy-start(s32[1,1,2]{2,1,0:T(1,128)} %param.5) | copy-start | bytes 28
  2.0 27.2 %copy-start.2 = (s32[1,1,2]{2,1,0:T(1,128)S(1)}, s32[1,1,2]{2,1,0:T(1,128)}, u32[]{:S(2)}) copy-start(s32[1,1,2]{2,1,0:T(1,128)} %param.6) | copy-start | bytes 28
  2.0 18.4 %collective-permute-start = (f32[96,512]{1,0:T(8,128)S(1)}, f32[96,512]{1,0:T(8,128)S(1)}, u32[]{:S(2)}, u32[]{:S(2)}) collective-permute-start(f32[96,512]{1,0:T(8,128)S(1)} %get-tuple-element.24), channel_id=1, source_target_pairs={{32,64},{64,32},{96,128},{128,96},{160,192},{192,160},{224,256},{2... | collective-permute-start | bytes 589832 | tf_op jit(solution)/shard_map/ppermute | solution.py:337
  14.5 7.8 %collective-permute-start.1 = (f32[96,512]{1,0:T(8,128)S(1)}, f32[96,512]{1,0:T(8,128)S(1)}, u32[]{:S(2)}, u32[]{:S(2)}) collective-permute-start(f32[96,512]{1,0:T(8,128)S(1)} %get-tuple-element.25), channel_id=1, source_target_pairs={{0,32},{32,0},{64,96},{96,64},{128,160},{160,128},{192,224},{224,1... | collective-permute-start | bytes 589832 | tf_op jit(solution)/shard_map/ppermute | solution.py:338
  22.7 10.7 %collective-permute-start.3 = (f32[96,512]{1,0:T(8,128)S(1)}, f32[96,512]{1,0:T(8,128)S(1)}, u32[]{:S(2)}, u32[]{:S(2)}) collective-permute-start(f32[96,512]{1,0:T(8,128)S(1)} %get-tuple-element.31), channel_id=1, source_target_pairs={{0,1},{1,0},{2,3},{3,2},{4,5},{5,4},{6,7},{7,6},{8,9},{9,8},{10,11... | collective-permute-start | bytes 589832 | tf_op jit(solution)/shard_map/ppermute | solution.py:338
  26.1 8.4 %collective-permute-start.2 = (f32[96,512]{1,0:T(8,128)S(1)}, f32[96,512]{1,0:T(8,128)S(1)}, u32[]{:S(2)}, u32[]{:S(2)}) collective-permute-start(f32[96,512]{1,0:T(8,128)S(1)} %get-tuple-element.30), channel_id=1, source_target_pairs={{1,2},{2,1},{3,4},{4,3},{5,6},{6,5},{7,8},{8,7},{9,10},{10,9},{11,... | collective-permute-start | bytes 589832 | tf_op jit(solution)/shard_map/ppermute | solution.py:337

commit v9 on v7

--- a/solution.py
+++ b/solution.py
@@ -299,7 +299,7 @@
 
     copies = []
     start = 0
-    for i, stop in enumerate((nx // 4, nx // 2, 3 * nx // 4, nx - 4, nx)):
+    for i, stop in enumerate((4, 12, 20, nx - 4, nx)):
         lax.fori_loop(start // 2, stop // 2, pair, 0, unroll=2)
         part = pl.ds(start, stop - start)
         for n, at in enumerate((0, ny - 8)):

time: 65.2 us -> 65.1 us (level)
  no operation moved by 1% of the time
where the time goes in v9:
time: 65.1 us; the launch traced here: 64.8 us
  blocking collectives  26 us (40%)
  starting transfers between devices  23.9 us (37%)
  Pallas kernels  11.4 us (18%)
  waiting for transfers between devices  1.93 us (3%)
  between operations  0.78 us (1%)
  local copies, waits for them, and re-layouts  0.7 us (1%)
    ppermute x2, starting transfers between devices, exchange(): return (lax.ppermute(outer, axes, swap_outer), inner)  17 us
    all_to_all x1, blocking collectives, shards(): mass = lax.all_to_all(mass, SECOND, 0, 0).sum(0)  14.4 us
    all_to_all x1, blocking collectives, shards(): mass = spread(*near(lax.all_to_all(mass, FIRST, 0, 0)))  11.6 us
    ppermute x2, starting transfers between devices, exchange(): inner = lax.ppermute(inner, axes, swap_inner)  6.87 us
    pallas_call x1, Pallas kernels, shards(): rows(*near(work, got_outer, got_inner, table, cut_exponent.reshape(1, blo...  4.17 us
    pallas_call x1, Pallas kernels, shards(): work, inner, outer, table = bulk(*near(later), far(table))  3.9 us
    ppermute x2, waiting for transfers between devices, exchange(): inner = lax.ppermute(inner, axes, swap_inner)  1.93 us
    pallas_call x1, Pallas kernels, shards(): coeffs, mass = final(*near(outer, inner, acc, limits, hot, base), coeffs)  1.65 us
  transfers between devices with their start and end apart: 4, of which 1 were waited for; matrix products, arithmetic and copies ran while one was open for 0% of the time, Pallas kernels for 12%

profile of v9, /device:TPU:1, one launch (start us, length us, event | category | flops | bytes accessed | tf_op | source)
XLA Modules:
  0.0 64.8 jit_solution(11515652940882973694)
XLA Ops:
  0.6 0.0 copy-start
  0.6 1.3 %edge.1 = (f32[96,512]{1,0:T(8,128)S(1)}, f32[96,512]{1,0:T(8,128)S(1)}) custom-call(f32[1024,512]{1,0:T(8,128)} %bitcast.5), custom_call_target="tpu_custom_call" | custom-call | tf_op jit(solution)/shard_map/edge/pallas_call | solution.py:368
  2.0 0.0 copy-start.1
  2.0 0.0 copy-start.2
  2.0 12.5 %collective-permute-start = (f32[96,512]{1,0:T(8,128)S(1)}, f32[96,512]{1,0:T(8,128)S(1)}, u32[]{:S(2)}, u32[]{:S(2)}) collective-permute-start(f32[96,512]{1,0:T(8,128)S(1)} %get-tuple-element.22), channel_id=1, source_target_pairs={{32,64},{64,32},{96,128},{128,96},{160,192},{192,160},{224,256},{2... | collective-permute-start | bytes 589832 | tf_op jit(solution)/shard_map/ppermute | solution.py:339
  14.5 1.9 %collective-permute-start.1 = (f32[96,512]{1,0:T(8,128)S(1)}, f32[96,512]{1,0:T(8,128)S(1)}, u32[]{:S(2)}, u32[]{:S(2)}) collective-permute-start(f32[96,512]{1,0:T(8,128)S(1)} %get-tuple-element.23), channel_id=1, source_target_pairs={{0,32},{32,0},{64,96},{96,64},{128,160},{160,128},{192,224},{224,1... | collective-permute-start | bytes 589832 | tf_op jit(solution)/shard_map/ppermute | solution.py:338
  16.4 0.0 copy-done
  16.4 3.9 %bulk.1 = (f32[1024,512]{1,0:T(8,128)S(1)}, f32[96,512]{1,0:T(8,128)S(1)}, f32[96,512]{1,0:T(8,128)S(1)}, bf16[512,512]{1,0:T(8,128)(2,1)S(1)}) custom-call(f32[1024,512]{1,0:T(8,128)S(1)} %bitcast.6, bf16[512,512]{1,0:T(8,128)(2,1)} %constant.4.clone.table_hbm), custom_call_target="tpu_custom_call" | custom-call | flops 40000000 | bytes 4194304 | tf_op jit(solution)/shard_map/bulk/pallas_call | solution.py:386
  20.3 0.0 collective-permute-done.got_o_ref
  20.3 1.9 %collective-permute-done.1.got_i_ref = f32[96,512]{1,0:T(8,128)S(1)} collective-permute-done((f32[96,512]{1,0:T(8,128)S(1)}, f32[96,512]{1,0:T(8,128)S(1)}, u32[]{:S(2)}, u32[]{:S(2)}) %collective-permute-start.1) | collective-permute-done | bytes 196640 | tf_op jit(solution)/shard_map/ppermute | solution.py:338
  22.3 0.4 plane.1
  22.7 4.5 %collective-permute-start.2 = (f32[96,512]{1,0:T(8,128)S(1)}, f32[96,512]{1,0:T(8,128)S(1)}, u32[]{:S(2)}, u32[]{:S(2)}) collective-permute-start(f32[96,512]{1,0:T(8,128)S(1)} %get-tuple-element.28), channel_id=1, source_target_pairs={{1,2},{2,1},{3,4},{4,3},{5,6},{6,5},{7,8},{8,7},{9,10},{10,9},{11,... | collective-permute-start | bytes 589832 | tf_op jit(solution)/shard_map/ppermute | solution.py:339
  27.2 4.9 %collective-permute-start.3 = (f32[96,512]{1,0:T(8,128)S(1)}, f32[96,512]{1,0:T(8,128)S(1)}, u32[]{:S(2)}, u32[]{:S(2)}) collective-permute-start(f32[96,512]{1,0:T(8,128)S(1)} %get-tuple-element.29), channel_id=1, source_target_pairs={{0,1},{1,0},{2,3},{3,2},{4,5},{5,4},{6,7},{7,6},{8,9},{9,8},{10,11... | collective-permute-start | bytes 589832 | tf_op jit(solution)/shard_map/ppermute | solution.py:338
  32.2 0.0 copy-done.1
  32.2 0.0 copy-done.2
  32.2 4.2 %rows.1 = (f32[32,32,512]{2,1,0:T(8,128)}, f32[512,512]{1,0:T(8,128)S(1)}, f32[4,8,512]{2,1,0:T(8,128)S(1)}, f32[4,512]{1,0:T(4,128)S(1)}, f32[8,128]{1,0:T(8,128)S(1)}) custom-call(f32[1024,512]{1,0:T(8,128)S(1)} %get-tuple-element.30.w_ref, f32[96,512]{1,0:T(8,128)S(1)} %collective-permute-done.got_o_ref, f32[96,512]{1,0:T(8,128)S(1)} %collective-permute-done.1.got_i_ref, ...), custom_call_target="tpu_custom_call" | custom-call | flops 40000000 | bytes 4194304 | tf_op jit(solution)/shard_map/rows/pallas_call | solution.py:419
  36.4 0.0 collective-permute-done.2.outer_ref
  36.4 0.0 collective-permute-done.3.inner_ref
  36.4 1.6 %final.1 = (f32[32,32,512]{2,1,0:T(8,128)}, f32[16,1,128]{2,1,0:T(1,128)S(1)}) custom-call(f32[96,512]{1,0:T(8,128)S(1)} %collective-permute-done.2.outer_ref, f32[96,512]{1,0:T(8,128)S(1)} %collective-permute-done.3.inner_ref, f32[4,8,512]{2,1,0:T(8,128)S(1)} %get-tuple-element.31.acc_in, ...), custom_call_target="tpu_custom_call", output_to_operand_aliasing={{0}: (6, {})} | custom-call | tf_op jit(solution)/shard_map/final/pallas_call | solution.py:438
  38.0 11.6 %all_to_all.10.parts_ref = f32[16,1,128]{2,1,0:T(1,128)S(1)} all-to-all(f32[16,1,128]{2,1,0:T(1,128)S(1)} %get-tuple-element.37), channel_id=1, replica_groups=mesh['z'=8,'y_lo'=2,'y_hi'=4,'x'=4,'core'=2] {'z','core'}, dimensions={0} | all-to-all | bytes 16384 | tf_op jit(solution)/shard_map/all_to_all | solution.py:447
  49.7 14.4 %all_to_all.11 = f32[32,1,128]{2,1,0:T(1,128)S(1)} all-to-all(f32[32,1,128]{2,1,0:T(1,128)S(1)} %spread.1), channel_id=1, replica_groups=mesh['z'=8,'y_lo'=2,'y_hi'=4,'x'=4,'core'=2] {'y_hi','y_lo','x'}, dimensions={0} | all-to-all | bytes 32768 | tf_op jit(solution)/shard_map/all_to_all | solution.py:448
  64.1 0.1 reduce_sum.11
  64.2 0.7 %reshape_squeeze.3 = f32[4,16]{1,0:T(4,128)} reshape(f32[64]{0:T(128)S(1)} %slice_reduce_fusion) | data formatting | bytes 512 | tf_op jit(solution)/shard_map/reshape;squeeze | solution.py:449
  (2 shorter events, 0.0 us)
Async XLA Ops:
  0.6 15.8 %copy-start = (f32[32,32,512]{2,1,0:T(8,128)S(1)}, f32[32,32,512]{2,1,0:T(8,128)}, u32[]{:S(2)}) copy-start(f32[32,32,512]{2,1,0:T(8,128)} %param.4) | copy-start | bytes 6291460
  2.0 30.2 %copy-start.1 = (s32[1,1,2]{2,1,0:T(1,128)S(1)}, s32[1,1,2]{2,1,0:T(1,128)}, u32[]{:S(2)}) copy-start(s32[1,1,2]{2,1,0:T(1,128)} %param.5) | copy-start | bytes 28
  2.0 30.2 %copy-start.2 = (s32[1,1,2]{2,1,0:T(1,128)S(1)}, s32[1,1,2]{2,1,0:T(1,128)}, u32[]{:S(2)}) copy-start(s32[1,1,2]{2,1,0:T(1,128)} %param.6) | copy-start | bytes 28
  2.0 18.4 %collective-permute-start = (f32[96,512]{1,0:T(8,128)S(1)}, f32[96,512]{1,0:T(8,128)S(1)}, u32[]{:S(2)}, u32[]{:S(2)}) collective-permute-start(f32[96,512]{1,0:T(8,128)S(1)} %get-tuple-element.22), channel_id=1, source_target_pairs={{32,64},{64,32},{96,128},{128,96},{160,192},{192,160},{224,256},{2... | collective-permute-start | bytes 589832 | tf_op jit(solution)/shard_map/ppermute | solution.py:339
  14.5 7.8 %collective-permute-start.1 = (f32[96,512]{1,0:T(8,128)S(1)}, f32[96,512]{1,0:T(8,128)S(1)}, u32[]{:S(2)}, u32[]{:S(2)}) collective-permute-start(f32[96,512]{1,0:T(8,128)S(1)} %get-tuple-element.23), channel_id=1, source_target_pairs={{0,32},{32,0},{64,96},{96,64},{128,160},{160,128},{192,224},{224,1... | collective-permute-start | bytes 589832 | tf_op jit(solution)/shard_map/ppermute | solution.py:338
  22.7 13.7 %collective-permute-start.2 = (f32[96,512]{1,0:T(8,128)S(1)}, f32[96,512]{1,0:T(8,128)S(1)}, u32[]{:S(2)}, u32[]{:S(2)}) collective-permute-start(f32[96,512]{1,0:T(8,128)S(1)} %get-tuple-element.28), channel_id=1, source_target_pairs={{1,2},{2,1},{3,4},{4,3},{5,6},{6,5},{7,8},{8,7},{9,10},{10,9},{11,... | collective-permute-start | bytes 589832 | tf_op jit(solution)/shard_map/ppermute | solution.py:339
  27.2 9.2 %collective-permute-start.3 = (f32[96,512]{1,0:T(8,128)S(1)}, f32[96,512]{1,0:T(8,128)S(1)}, u32[]{:S(2)}, u32[]{:S(2)}) collective-permute-start(f32[96,512]{1,0:T(8,128)S(1)} %get-tuple-element.29), channel_id=1, source_target_pairs={{0,1},{1,0},{2,3},{3,2},{4,5},{5,4},{6,7},{7,6},{8,9},{9,8},{10,11... | collective-permute-start | bytes 589832 | tf_op jit(solution)/shard_map/ppermute | solution.py:338
